TPU v7x, 128 devices: a whole 4x4x4 slice. The times are simulated.
128 devices in a mesh: gx: 16 (over z, x), gy: 8 (over y, core).
Axes of the slice: x: 4, y: 4, z: 4, core: 2. Of those that a mesh axis runs over, the one named last changes fastest.
Arguments:
- pressure: float32 [10, 1024, 4096], P(None, 'gx', 'gy'), may hold values from -6 to 6
- pressure_old: float32 [10, 1024, 4096], P(None, 'gx', 'gy'), may hold values from -6 to 6
- conductivity: float32 [10, 1024, 4096], P(None, 'gx', 'gy'), may hold values from 0.1 to 1
- porosity: float32 [10, 1024, 4096], P(None, 'gx', 'gy'), may hold values from 2 to 8
- recharge: float32 [1024, 4096], P('gx', 'gy'), may hold values from -6 to 6
- active: int32 [1024, 4096], P('gx', 'gy'), may hold values from 0 to 1, as said below
Outputs:
- final_pressure: float32 [10, 1024, 4096], P(None, 'gx', 'gy')
- linear_residual: float32 [10, 1024, 4096], P(None, 'gx', 'gy')
Inputs may be any that keep to these rules, and one draw needn't show every extreme that they name: `active`: 1 marks a land column, 0 an ocean column.
All inputs are finite; a program needn't handle non-finite values.
Results may differ from a plain program's by a relative error of at most 0.0003.
Values sent between devices are 32-bit elements; how exact they have to be, the bound alone decides.
No kernel may reach another device: no remote copies, remote signals or barrier semaphores. Data moves between devices by JAX's collectives and lax.ppermute only.
A program may use at most 128 MiB of HBM per device.

v0:
```python
import jax
import jax.numpy as jnp
from jax import lax
from jax.sharding import Mesh
from jax.sharding import PartitionSpec as P

NEWTON = 2
GX_GY = ("gx_0", "gx_1", "gy_0", "gy_1")
GX = ("gx_0", "gx_1")
GY = ("gy_0", "gy_1")


residual_sat = 0.1
vertical_factor = 2.0
epsilon = 1e-06


def padded(value, sides, width):
    edges = {}
    for axis, dim in sides:
        size, length = (lax.axis_size(axis), value.shape[dim])
        up = [(i, (i + 1) % size) for i in range(size - 1)]
        last = lax.slice_in_dim(value, length - width, length, axis=dim)
        initial = lax.slice_in_dim(value, 0, width, axis=dim)
        edges[dim] = (
            lax.ppermute(last, axis, up),
            lax.ppermute(initial, axis, [(b, a) for a, b in up]),
        )
    done = []
    for _, dim in sides:
        low, high = edges[dim]
        around = [(width, width) if d in done else (0, 0) for d in range(value.ndim)]
        value = jnp.concatenate([jnp.pad(low, around), value, jnp.pad(high, around)], axis=dim)
        done.append(dim)
    return value


def by_axis(value, axes):
    for axis in axes:
        value = lax.psum(value, axis)
    return value


def interior(array):
    return array[:, 1:-1, 1:-1]


def saturation(values):
    return residual_sat + (1.0 - residual_sat) * jax.nn.sigmoid(values)


def sat_slope(values):
    sigma = jax.nn.sigmoid(values)
    return (1.0 - residual_sat) * sigma * (1.0 - sigma)


def face_pair(press_low, press_high, cond_low, cond_high, act_low, act_high, factor, gravity):
    transmit = 0.5 * factor * (cond_low + cond_high) * act_low * act_high
    sig_low = jax.nn.sigmoid(press_low)
    sig_high = jax.nn.sigmoid(press_high)
    mobility = 0.5 * (sig_low * sig_low + sig_high * sig_high)
    head_drop = press_low - press_high + gravity
    coef_low = transmit * (mobility + sig_low * sig_low * (1.0 - sig_low) * head_drop)
    coef_high = transmit * (sig_high * sig_high * (1.0 - sig_high) * head_drop - mobility)
    return (coef_low, coef_high, transmit * mobility * head_drop)


def coefficients(pressure, conduct, active):
    across_x = face_pair(
        pressure[:, :-1, 1:-1],
        pressure[:, 1:, 1:-1],
        conduct[:, :-1, 1:-1],
        conduct[:, 1:, 1:-1],
        active[:, :-1, 1:-1],
        active[:, 1:, 1:-1],
        1.0,
        0.0,
    )
    across_y = face_pair(
        pressure[:, 1:-1, :-1],
        pressure[:, 1:-1, 1:],
        conduct[:, 1:-1, :-1],
        conduct[:, 1:-1, 1:],
        active[:, 1:-1, :-1],
        active[:, 1:-1, 1:],
        1.0,
        0.0,
    )
    inner_p = interior(pressure)
    inner_k = interior(conduct)
    inner_a = interior(active)
    across_z = face_pair(
        inner_p[:-1],
        inner_p[1:],
        inner_k[:-1],
        inner_k[1:],
        inner_a[:-1],
        inner_a[1:],
        vertical_factor,
        -1.0,
    )
    return (across_x, across_y, across_z)


def outflow(flow_x, flow_y, flow_z):
    total = flow_x[:, 1:] - flow_x[:, :-1] + flow_y[:, :, 1:] - flow_y[:, :, :-1]
    zeros = jnp.zeros_like(flow_z[:1])
    return total + jnp.concatenate([flow_z, zeros], 0) - jnp.concatenate([zeros, flow_z], 0)


def jacobian_apply(vector, faces, diagonal, active):
    x_low, x_high, x_flow = faces[0]
    y_low, y_high, y_flow = faces[1]
    z_low, z_high, z_flow = faces[2]
    flow_x = x_low * vector[:, :-1, 1:-1] + x_high * vector[:, 1:, 1:-1]
    flow_y = y_low * vector[:, 1:-1, :-1] + y_high * vector[:, 1:-1, 1:]
    center = interior(vector)
    flow_z = z_low * center[:-1] + z_high * center[1:]
    return active * (diagonal * center + outflow(flow_x, flow_y, flow_z)) + (1.0 - active) * center


def newton_residual(pressure, faces, pressure_old, porosity, recharge, active):
    center = interior(pressure)
    storage = porosity * (saturation(center) - saturation(pressure_old))
    inflow = jnp.concatenate([jnp.zeros_like(center[:-1]), recharge[None]], 0)
    flows = outflow(faces[0][2], faces[1][2], faces[2][2])
    return active * (storage - inflow + flows) + (1.0 - active) * center


def least_squares(first_norm, entry_one, entry_two, entry_three, entry_four, entry_five):
    radius = jnp.sqrt(entry_one * entry_one + entry_two * entry_two)
    cosine = entry_one / radius
    sine = entry_two / radius
    top_right = cosine * entry_three + sine * entry_four
    lower = cosine * entry_four - sine * entry_three
    weight_two = -lower * sine * first_norm / (lower * lower + entry_five * entry_five)
    weight_one = (cosine * first_norm - top_right * weight_two) / radius
    return (weight_one, weight_two)


def body(pressure, pressure_old, conductivity, porosity, recharge, active):
    layers = pressure.shape[0]
    active_flat = active.astype(jnp.float32)
    active_cells = jnp.broadcast_to(active_flat[None], pressure.shape)
    stacked = jnp.concatenate([conductivity, active_flat[None]], 0)
    widened = padded(stacked, ((GX, 1), (GY, 2)), 1)
    cond_ext = widened[:layers]
    act_ext = jnp.broadcast_to(widened[layers][None], cond_ext.shape)
    current = pressure
    leftover = jnp.zeros_like(pressure)
    for newton_index in range(NEWTON):
        diagonal = porosity * sat_slope(current)
        current_ext = padded(current, ((GX, 1), (GY, 2)), 1)
        faces = coefficients(current_ext, cond_ext, act_ext)
        remainder = -newton_residual(
            current_ext, faces, pressure_old, porosity, recharge, active_cells
        )
        first_norm = jnp.sqrt(by_axis(jnp.sum(remainder * remainder), GX_GY) + epsilon)
        basis_one = remainder / first_norm
        basis_ext = padded(basis_one, ((GX, 1), (GY, 2)), 1)
        image_one = jacobian_apply(basis_ext, faces, diagonal, active_cells)
        entry_one, square_one = (
            by_axis(jnp.sum(image_one * basis_one), GX_GY),
            by_axis(jnp.sum(image_one * image_one), GX_GY),
        )
        ortho_one = image_one - entry_one * basis_one
        entry_two = jnp.sqrt(square_one - entry_one * entry_one + epsilon)
        basis_two = ortho_one / entry_two
        second_ext = padded(basis_two, ((GX, 1), (GY, 2)), 1)
        image_two = jacobian_apply(second_ext, faces, diagonal, active_cells)
        entry_three, entry_four, square_two = (
            by_axis(jnp.sum(image_two * basis_one), GX_GY),
            by_axis(jnp.sum(image_two * basis_two), GX_GY),
            by_axis(jnp.sum(image_two * image_two), GX_GY),
        )
        entry_five = jnp.sqrt(
            square_two - entry_three * entry_three - entry_four * entry_four + epsilon
        )
        weight_one, weight_two = least_squares(
            first_norm, entry_one, entry_two, entry_three, entry_four, entry_five
        )
        current = current + (weight_one * basis_one + weight_two * basis_two)
        leftover = remainder - weight_one * image_one - weight_two * image_two
    return (current, leftover)


def solution(mesh):
    torus = Mesh(mesh.devices.reshape(4, 4, 4, 2), ("gx_0", "gx_1", "gy_0", "gy_1"))
    in_specs = (
        P(None, GX, GY),
        P(None, GX, GY),
        P(None, GX, GY),
        P(None, GX, GY),
        P(GX, GY),
        P(GX, GY),
    )
    out_specs = (P(None, GX, GY), P(None, GX, GY))
    return jax.shard_map(body, mesh=torus, in_specs=in_specs, out_specs=out_specs, check_vma=False)
```

profile of v0, /device:TPU:1, one launch (start us, length us, event | category | flops | bytes accessed | tf_op | source)
XLA Modules:
  0.0 389.7 jit_solution(7502140902498342127)
XLA Ops:
  9.0 4.0 %collective-permute-start.2 = (f32[11,64,1]{2,1,0:T(8,128)S(1)}, f32[11,64,1]{2,1,0:T(8,128)S(1)}, u32[]{:S(2)}, u32[]{:S(2)}) collective-permute-start(f32[11,64,1]{2,1,0:T(8,128)S(1)} %get-tuple-element.74), channel_id=1, source_target_pairs={{0,1},{1,2},{2,3},{3,4},{4,5},{5,6},{6,7},{8,9},{9,10},{10,11},{11... | collective-permute-start | bytes 8456 | tf_op jit(solution)/shard_map/ppermute | solution.py:26
  18.5 4.9 %collective-permute-start.4 = (f32[10,1,512]{2,1,0:T(1,128)S(1)}, f32[10,1,512]{2,1,0:T(1,128)S(1)}, u32[]{:S(2)}, u32[]{:S(2)}) collective-permute-start(f32[10,1,512]{2,1,0:T(1,128)S(1)} %get-tuple-element.98), channel_id=1, source_target_pairs={{0,8},{8,16},{16,24},{24,32},{32,40},{40,48},{48,56},{56,64},{64,7... | collective-permute-start | bytes 61448 | tf_op jit(solution)/shard_map/ppermute | solution.py:26
  23.4 3.9 %collective-permute-start.6 = (f32[10,64,1]{2,1,0:T(8,128)}, f32[10,64,1]{2,1,0:T(8,128)}, u32[]{:S(2)}, u32[]{:S(2)}) collective-permute-start(f32[10,64,1]{2,1,0:T(8,128)} %get-tuple-element.96), channel_id=1, source_target_pairs={{0,1},{1,2},{2,3},{3,4},{4,5},{5,6},{6,7},{8,9},{9,10},{10,11},{11... | collective-permute-start | bytes 7688 | tf_op jit(solution)/shard_map/ppermute | solution.py:26
  36.9 5.1 %multiply_multiply_fusion.1 = (f32[10,64,513]{2,1,0:T(8,128)S(1)}, f32[10,64,513]{2,1,0:T(8,128)}) fusion(f32[10,64,1]{2,1,0:T(8,128)} %collective-permute-done.7, f32[10,1,512]{2,1,0:T(1,128)S(1)} %collective-permute-done.5, f32[10,64,512]{2,1,0:T(8,128)S(1)} %copy-done, f32[10,1,512]{2,1,0:T(1,128)S(1)} %collective-permute-done.4, ...), kind=kLoop, calls=%fused_computation.83 | loop fusion | flops 11162880 | bytes 5738672 | tf_op jit(solution)/shard_map/mul | solution.py:65
  45.0 13.0 %psum.336 = f32[]{:T(128)} all-reduce(f32[]{:T(128)} %get-tuple-element.66), channel_id=1, replica_groups=mesh['gx_0'=4,'gx_1'=4,'gy_0'=4,'gy_1'=2] {'gx_0'}, use_global_device_ids=true, to_apply=%region_1.2 | all-reduce | flops 1 | bytes 8 | tf_op jit(solution)/shard_map/psum | solution.py:40
  57.9 7.2 %psum.337 = f32[]{:T(128)} all-reduce(f32[]{:T(128)} %psum.336), channel_id=1, replica_groups=mesh['gx_0'=4,'gx_1'=4,'gy_0'=4,'gy_1'=2] {'gx_1'}, use_global_device_ids=true, to_apply=%region_2.3 | all-reduce | flops 1 | bytes 8 | tf_op jit(solution)/shard_map/psum | solution.py:40
  65.1 8.0 %psum.338 = f32[]{:T(128)} all-reduce(f32[]{:T(128)} %psum.337), channel_id=1, replica_groups=mesh['gx_0'=4,'gx_1'=4,'gy_0'=4,'gy_1'=2] {'gy_0'}, use_global_device_ids=true, to_apply=%region_3.4 | all-reduce | flops 1 | bytes 8 | tf_op jit(solution)/shard_map/psum | solution.py:40
  73.1 9.5 %psum.339 = f32[]{:T(128)} all-reduce(f32[]{:T(128)} %psum.338), channel_id=1, replica_groups=mesh['gx_0'=4,'gx_1'=4,'gy_0'=4,'gy_1'=2] {'gy_1'}, use_global_device_ids=true, to_apply=%region_4.5 | all-reduce | flops 1 | bytes 8 | tf_op jit(solution)/shard_map/psum | solution.py:40
  99.7 4.4 %fusion.19 = (f32[10,64,513]{2,1,0:T(8,128)S(1)}, f32[10,64,513]{2,1,0:T(8,128)}, f32[10,64,513]{2,1,0:T(8,128)}) fusion(f32[10,64,1]{2,1,0:T(8,128)S(1)} %collective-permute-done.11, f32[10,1,512]{2,1,0:T(1,128)S(1)} %collective-permute-done.9, f32[10,64,512]{2,1,0:T(8,128)S(1)} %negate_divide_fusion, f32[10,1,512]{2,1,0:T(1,128)S(1)} %collective-permute-done.8, ...), kind=kLoop, calls=%fused_computation.46 | loop fusion | flops 13789440 | bytes 7966720 | tf_op jit(solution)/shard_map/add | solution.py:116
  107.1 10.9 %all-reduce.38 = (f32[]{:T(128)}, f32[]{:T(128)}) all-reduce(f32[]{:T(128)} %get-tuple-element.11, f32[]{:T(128)} %get-tuple-element.10), channel_id=1, replica_groups=mesh['gx_0'=4,'gx_1'=4,'gy_0'=4,'gy_1'=2] {'gx_0'}, use_global_device_ids=true, to_apply=%region_11.12 | all-reduce | flops 2 | bytes 16 | tf_op jit(solution)/shard_map/psum | solution.py:40
  118.1 6.7 %all-reduce.34 = (f32[]{:T(128)}, f32[]{:T(128)}) all-reduce(f32[]{:T(128)} %get-tuple-element.40, f32[]{:T(128)} %get-tuple-element.41), channel_id=1, replica_groups=mesh['gx_0'=4,'gx_1'=4,'gy_0'=4,'gy_1'=2] {'gx_1'}, use_global_device_ids=true, to_apply=%region_12.13 | all-reduce | flops 2 | bytes 16 | tf_op jit(solution)/shard_map/psum | solution.py:40
  124.8 7.6 %all-reduce.30 = (f32[]{:T(128)}, f32[]{:T(128)}) all-reduce(f32[]{:T(128)} %get-tuple-element.30, f32[]{:T(128)} %get-tuple-element.31), channel_id=1, replica_groups=mesh['gx_0'=4,'gx_1'=4,'gy_0'=4,'gy_1'=2] {'gy_0'}, use_global_device_ids=true, to_apply=%region_13.14 | all-reduce | flops 2 | bytes 16 | tf_op jit(solution)/shard_map/psum | solution.py:40
  132.4 7.7 %all-reduce.42 = (f32[]{:T(128)}, f32[]{:T(128)}) all-reduce(f32[]{:T(128)} %get-tuple-element.20, f32[]{:T(128)} %get-tuple-element.21), channel_id=1, replica_groups=mesh['gx_0'=4,'gx_1'=4,'gy_0'=4,'gy_1'=2] {'gy_1'}, use_global_device_ids=true, to_apply=%region_14.15 | all-reduce | flops 2 | bytes 16 | tf_op jit(solution)/shard_map/psum | solution.py:40
  168.7 10.3 %all-reduce.37 = (f32[]{:T(128)}, f32[]{:T(128)}, f32[]{:T(128)}) all-reduce(f32[]{:T(128)} %get-tuple-element.8, f32[]{:T(128)} %get-tuple-element.9, f32[]{:T(128)} %get-tuple-element.7), channel_id=1, replica_groups=mesh['gx_0'=4,'gx_1'=4,'gy_0'=4,'gy_1'=2] {'gx_0'}, use_global_device_ids=true, to_apply=%region_21.22 | all-reduce | flops 3 | bytes 24 | tf_op jit(solution)/shard_map/psum | solution.py:40
  179.0 6.7 %all-reduce.33 = (f32[]{:T(128)}, f32[]{:T(128)}, f32[]{:T(128)}) all-reduce(f32[]{:T(128)} %get-tuple-element.37, f32[]{:T(128)} %get-tuple-element.38, f32[]{:T(128)} %get-tuple-element.39), channel_id=1, replica_groups=mesh['gx_0'=4,'gx_1'=4,'gy_0'=4,'gy_1'=2] {'gx_1'}, use_global_device_ids=true, to_apply=%region_22.23 | all-reduce | flops 3 | bytes 24 | tf_op jit(solution)/shard_map/psum | solution.py:40
  185.7 6.7 %all-reduce.29 = (f32[]{:T(128)}, f32[]{:T(128)}, f32[]{:T(128)}) all-reduce(f32[]{:T(128)} %get-tuple-element.27, f32[]{:T(128)} %get-tuple-element.28, f32[]{:T(128)} %get-tuple-element.29), channel_id=1, replica_groups=mesh['gx_0'=4,'gx_1'=4,'gy_0'=4,'gy_1'=2] {'gy_0'}, use_global_device_ids=true, to_apply=%region_23.24 | all-reduce | flops 3 | bytes 24 | tf_op jit(solution)/shard_map/psum | solution.py:40
  192.4 8.5 %all-reduce.41 = (f32[]{:T(128)}, f32[]{:T(128)}, f32[]{:T(128)}) all-reduce(f32[]{:T(128)} %get-tuple-element.17, f32[]{:T(128)} %get-tuple-element.18, f32[]{:T(128)} %get-tuple-element.19), channel_id=1, replica_groups=mesh['gx_0'=4,'gx_1'=4,'gy_0'=4,'gy_1'=2] {'gy_1'}, use_global_device_ids=true, to_apply=%region_24.25 | all-reduce | flops 3 | bytes 24 | tf_op jit(solution)/shard_map/psum | solution.py:40
  221.0 4.5 %collective-permute-done.19 = f32[10,64,1]{2,1,0:T(8,128)S(1)} collective-permute-done((f32[10,64,1]{2,1,0:T(8,128)S(1)}, f32[10,64,1]{2,1,0:T(8,128)S(1)}, u32[]{:S(2)}, u32[]{:S(2)}) %collective-permute-start.19) | collective-permute-done | bytes 2592 | tf_op jit(solution)/shard_map/ppermute | solution.py:27
  229.7 9.8 %psum.360 = f32[]{:T(128)} all-reduce(f32[]{:T(128)} %get-tuple-element.57), channel_id=1, replica_groups=mesh['gx_0'=4,'gx_1'=4,'gy_0'=4,'gy_1'=2] {'gx_0'}, use_global_device_ids=true, to_apply=%region_31.32 | all-reduce | flops 1 | bytes 8 | tf_op jit(solution)/shard_map/psum | solution.py:40
  239.5 6.7 %psum.361 = f32[]{:T(128)} all-reduce(f32[]{:T(128)} %psum.360), channel_id=1, replica_groups=mesh['gx_0'=4,'gx_1'=4,'gy_0'=4,'gy_1'=2] {'gx_1'}, use_global_device_ids=true, to_apply=%region_32.33 | all-reduce | flops 1 | bytes 8 | tf_op jit(solution)/shard_map/psum | solution.py:40
  246.2 7.4 %psum.362 = f32[]{:T(128)} all-reduce(f32[]{:T(128)} %psum.361), channel_id=1, replica_groups=mesh['gx_0'=4,'gx_1'=4,'gy_0'=4,'gy_1'=2] {'gy_0'}, use_global_device_ids=true, to_apply=%region_33.34 | all-reduce | flops 1 | bytes 8 | tf_op jit(solution)/shard_map/psum | solution.py:40
  253.6 7.7 %psum.363 = f32[]{:T(128)} all-reduce(f32[]{:T(128)} %psum.362), channel_id=1, replica_groups=mesh['gx_0'=4,'gx_1'=4,'gy_0'=4,'gy_1'=2] {'gy_1'}, use_global_device_ids=true, to_apply=%region_34.35 | all-reduce | flops 1 | bytes 8 | tf_op jit(solution)/shard_map/psum | solution.py:40
  276.4 4.4 %collective-permute-done.23 = f32[10,64,1]{2,1,0:T(8,128)S(1)} collective-permute-done((f32[10,64,1]{2,1,0:T(8,128)S(1)}, f32[10,64,1]{2,1,0:T(8,128)S(1)}, u32[]{:S(2)}, u32[]{:S(2)}) %collective-permute-start.23) | collective-permute-done | bytes 2592 | tf_op jit(solution)/shard_map/ppermute | solution.py:27
  287.1 10.3 %all-reduce.36 = (f32[]{:T(128)}, f32[]{:T(128)}) all-reduce(f32[]{:T(128)} %get-tuple-element.6, f32[]{:T(128)} %get-tuple-element.5), channel_id=1, replica_groups=mesh['gx_0'=4,'gx_1'=4,'gy_0'=4,'gy_1'=2] {'gx_0'}, use_global_device_ids=true, to_apply=%region_41.42 | all-reduce | flops 2 | bytes 16 | tf_op jit(solution)/shard_map/psum | solution.py:40
  297.4 6.7 %all-reduce.32 = (f32[]{:T(128)}, f32[]{:T(128)}) all-reduce(f32[]{:T(128)} %get-tuple-element.35, f32[]{:T(128)} %get-tuple-element.36), channel_id=1, replica_groups=mesh['gx_0'=4,'gx_1'=4,'gy_0'=4,'gy_1'=2] {'gx_1'}, use_global_device_ids=true, to_apply=%region_42.43 | all-reduce | flops 2 | bytes 16 | tf_op jit(solution)/shard_map/psum | solution.py:40
  304.1 6.7 %all-reduce.28 = (f32[]{:T(128)}, f32[]{:T(128)}) all-reduce(f32[]{:T(128)} %get-tuple-element.25, f32[]{:T(128)} %get-tuple-element.26), channel_id=1, replica_groups=mesh['gx_0'=4,'gx_1'=4,'gy_0'=4,'gy_1'=2] {'gy_0'}, use_global_device_ids=true, to_apply=%region_43.44 | all-reduce | flops 2 | bytes 16 | tf_op jit(solution)/shard_map/psum | solution.py:40
  310.8 8.5 %all-reduce.40 = (f32[]{:T(128)}, f32[]{:T(128)}) all-reduce(f32[]{:T(128)} %get-tuple-element.15, f32[]{:T(128)} %get-tuple-element.16), channel_id=1, replica_groups=mesh['gx_0'=4,'gx_1'=4,'gy_0'=4,'gy_1'=2] {'gy_1'}, use_global_device_ids=true, to_apply=%region_44.45 | all-reduce | flops 2 | bytes 16 | tf_op jit(solution)/shard_map/psum | solution.py:40
  348.4 9.8 %all-reduce.35 = (f32[]{:T(128)}, f32[]{:T(128)}, f32[]{:T(128)}) all-reduce(f32[]{:T(128)} %get-tuple-element.3, f32[]{:T(128)} %get-tuple-element.4, f32[]{:T(128)} %get-tuple-element.2), channel_id=1, replica_groups=mesh['gx_0'=4,'gx_1'=4,'gy_0'=4,'gy_1'=2] {'gx_0'}, use_global_device_ids=true, to_apply=%region_51.52 | all-reduce | flops 3 | bytes 24 | tf_op jit(solution)/shard_map/psum | solution.py:40
  358.3 6.6 %all-reduce.31 = (f32[]{:T(128)}, f32[]{:T(128)}, f32[]{:T(128)}) all-reduce(f32[]{:T(128)} %get-tuple-element.32, f32[]{:T(128)} %get-tuple-element.33, f32[]{:T(128)} %get-tuple-element.34), channel_id=1, replica_groups=mesh['gx_0'=4,'gx_1'=4,'gy_0'=4,'gy_1'=2] {'gx_1'}, use_global_device_ids=true, to_apply=%region_52.53 | all-reduce | flops 3 | bytes 24 | tf_op jit(solution)/shard_map/psum | solution.py:40
  364.9 7.5 %all-reduce.27 = (f32[]{:T(128)}, f32[]{:T(128)}, f32[]{:T(128)}) all-reduce(f32[]{:T(128)} %get-tuple-element.22, f32[]{:T(128)} %get-tuple-element.23, f32[]{:T(128)} %get-tuple-element.24), channel_id=1, replica_groups=mesh['gx_0'=4,'gx_1'=4,'gy_0'=4,'gy_1'=2] {'gy_0'}, use_global_device_ids=true, to_apply=%region_53.54 | all-reduce | flops 3 | bytes 24 | tf_op jit(solution)/shard_map/psum | solution.py:40
  372.4 7.7 %all-reduce.39 = (f32[]{:T(128)}, f32[]{:T(128)}, f32[]{:T(128)}) all-reduce(f32[]{:T(128)} %get-tuple-element.12, f32[]{:T(128)} %get-tuple-element.13, f32[]{:T(128)} %get-tuple-element.14), channel_id=1, replica_groups=mesh['gx_0'=4,'gx_1'=4,'gy_0'=4,'gy_1'=2] {'gy_1'}, use_global_device_ids=true, to_apply=%region_54.55 | all-reduce | flops 3 | bytes 24 | tf_op jit(solution)/shard_map/psum | solution.py:40
  385.3 4.4 %multiply_subtract_fusion = (f32[10,64,512]{2,1,0:T(8,128)}, f32[10,64,512]{2,1,0:T(8,128)}) fusion(f32[10,64,512]{2,1,0:T(8,128)} %get-tuple-element.52, f32[10,64,512]{2,1,0:T(8,128)} %get-tuple-element.53, f32[10,64,512]{2,1,0:T(8,128)} %get-tuple-element.58, f32[]{:T(128)S(6)} %div.125, f32[]{:T(128)S(6)} %div.126, ...), kind=kLoop, calls=%fused_computation.169 | loop fusion | flops 3276800 | bytes 9175052 | tf_op jit(solution)/shard_map/sub | solution.py:183
  (192 shorter events, 136.2 us)
Async XLA Ops:
  1.7 13.3 %copy-start = (f32[10,64,512]{2,1,0:T(8,128)S(1)}, f32[10,64,512]{2,1,0:T(8,128)}, u32[]{:S(2)}) copy-start(f32[10,64,512]{2,1,0:T(8,128)} %param.6) | copy-start | bytes 3932164
  3.4 28.3 %collective-permute-start = (f32[11,1,512]{2,1,0:T(1,128)}, f32[11,1,512]{2,1,0:T(1,128)S(1)}, u32[]{:S(2)}, u32[]{:S(2)}) collective-permute-start(f32[11,1,512]{2,1,0:T(1,128)} %get-tuple-element.72), channel_id=1, source_target_pairs={{0,8},{8,16},{16,24},{24,32},{32,40},{40,48},{48,56},{56,64},{64,7... | collective-permute-start | bytes 67592 | tf_op jit(solution)/shard_map/ppermute | solution.py:26
  7.4 24.4 %collective-permute-start.1 = (f32[11,1,512]{2,1,0:T(1,128)S(1)}, f32[11,1,512]{2,1,0:T(1,128)S(1)}, u32[]{:S(2)}, u32[]{:S(2)}) collective-permute-start(f32[11,1,512]{2,1,0:T(1,128)S(1)} %get-tuple-element.73), channel_id=1, source_target_pairs={{8,0},{16,8},{24,16},{32,24},{40,32},{48,40},{56,48},{64,56},{72,6... | collective-permute-start | bytes 67592 | tf_op jit(solution)/shard_map/ppermute | solution.py:27
  9.0 9.5 %collective-permute-start.2 = (f32[11,64,1]{2,1,0:T(8,128)S(1)}, f32[11,64,1]{2,1,0:T(8,128)S(1)}, u32[]{:S(2)}, u32[]{:S(2)}) collective-permute-start(f32[11,64,1]{2,1,0:T(8,128)S(1)} %get-tuple-element.74), channel_id=1, source_target_pairs={{0,1},{1,2},{2,3},{3,4},{4,5},{5,6},{6,7},{8,9},{9,10},{10,11},{11... | collective-permute-start | bytes 8456 | tf_op jit(solution)/shard_map/ppermute | solution.py:26
  13.1 10.4 %collective-permute-start.3 = (f32[11,64,1]{2,1,0:T(8,128)S(1)}, f32[11,64,1]{2,1,0:T(8,128)S(1)}, u32[]{:S(2)}, u32[]{:S(2)}) collective-permute-start(f32[11,64,1]{2,1,0:T(8,128)S(1)} %get-tuple-element.75), channel_id=1, source_target_pairs={{1,0},{2,1},{3,2},{4,3},{5,4},{6,5},{7,6},{9,8},{10,9},{11,10},{12... | collective-permute-start | bytes 8456 | tf_op jit(solution)/shard_map/ppermute | solution.py:27
  15.0 13.1 %collective-permute-start.5 = (f32[10,1,512]{2,1,0:T(1,128)S(1)}, f32[10,1,512]{2,1,0:T(1,128)S(1)}, u32[]{:S(2)}, u32[]{:S(2)}) collective-permute-start(f32[10,1,512]{2,1,0:T(1,128)S(1)} %get-tuple-element.99), channel_id=1, source_target_pairs={{8,0},{16,8},{24,16},{32,24},{40,32},{48,40},{56,48},{64,56},{72,6... | collective-permute-start | bytes 61448 | tf_op jit(solution)/shard_map/ppermute | solution.py:27
  18.5 16.1 %collective-permute-start.4 = (f32[10,1,512]{2,1,0:T(1,128)S(1)}, f32[10,1,512]{2,1,0:T(1,128)S(1)}, u32[]{:S(2)}, u32[]{:S(2)}) collective-permute-start(f32[10,1,512]{2,1,0:T(1,128)S(1)} %get-tuple-element.98), channel_id=1, source_target_pairs={{0,8},{8,16},{16,24},{24,32},{32,40},{40,48},{48,56},{56,64},{64,7... | collective-permute-start | bytes 61448 | tf_op jit(solution)/shard_map/ppermute | solution.py:26
  23.4 12.4 %collective-permute-start.6 = (f32[10,64,1]{2,1,0:T(8,128)}, f32[10,64,1]{2,1,0:T(8,128)}, u32[]{:S(2)}, u32[]{:S(2)}) collective-permute-start(f32[10,64,1]{2,1,0:T(8,128)} %get-tuple-element.96), channel_id=1, source_target_pairs={{0,1},{1,2},{2,3},{3,4},{4,5},{5,6},{6,7},{8,9},{9,10},{10,11},{11... | collective-permute-start | bytes 7688 | tf_op jit(solution)/shard_map/ppermute | solution.py:26
  28.2 8.7 %collective-permute-start.7 = (f32[10,64,1]{2,1,0:T(8,128)}, f32[10,64,1]{2,1,0:T(8,128)}, u32[]{:S(2)}, u32[]{:S(2)}) collective-permute-start(f32[10,64,1]{2,1,0:T(8,128)} %get-tuple-element.97), channel_id=1, source_target_pairs={{1,0},{2,1},{3,2},{4,3},{5,4},{6,5},{7,6},{9,8},{10,9},{11,10},{12... | collective-permute-start | bytes 7688 | tf_op jit(solution)/shard_map/ppermute | solution.py:27
  83.3 10.5 %copy-start.17 = (f32[9,64,512]{2,1,0:T(8,128)S(1)}, f32[9,64,512]{2,1,0:T(8,128)}, u32[]{:S(2)}) copy-start(f32[9,64,512]{2,1,0:T(8,128)} %get-tuple-element.69) | copy-start | bytes 3538948
  85.1 9.5 %collective-permute-start.8 = (f32[10,1,512]{2,1,0:T(1,128)S(1)}, f32[10,1,512]{2,1,0:T(1,128)S(1)}, u32[]{:S(2)}, u32[]{:S(2)}) collective-permute-start(f32[10,1,512]{2,1,0:T(1,128)S(1)} %get-tuple-element.94), channel_id=1, source_target_pairs={{0,8},{8,16},{16,24},{24,32},{32,40},{40,48},{48,56},{56,64},{64,7... | collective-permute-start | bytes 61448 | tf_op jit(solution)/shard_map/ppermute | solution.py:26
  88.1 6.5 %collective-permute-start.9 = (f32[10,1,512]{2,1,0:T(1,128)S(1)}, f32[10,1,512]{2,1,0:T(1,128)S(1)}, u32[]{:S(2)}, u32[]{:S(2)}) collective-permute-start(f32[10,1,512]{2,1,0:T(1,128)S(1)} %get-tuple-element.95), channel_id=1, source_target_pairs={{8,0},{16,8},{24,16},{32,24},{40,32},{48,40},{56,48},{64,56},{72,6... | collective-permute-start | bytes 61448 | tf_op jit(solution)/shard_map/ppermute | solution.py:27
  89.4 8.8 %collective-permute-start.10 = (f32[10,64,1]{2,1,0:T(8,128)S(1)}, f32[10,64,1]{2,1,0:T(8,128)S(1)}, u32[]{:S(2)}, u32[]{:S(2)}) collective-permute-start(f32[10,64,1]{2,1,0:T(8,128)S(1)} %get-tuple-element.92), channel_id=1, source_target_pairs={{0,1},{1,2},{2,3},{3,4},{4,5},{5,6},{6,7},{8,9},{9,10},{10,11},{11... | collective-permute-start | bytes 7688 | tf_op jit(solution)/shard_map/ppermute | solution.py:26
  91.3 8.4 %collective-permute-start.11 = (f32[10,64,1]{2,1,0:T(8,128)S(1)}, f32[10,64,1]{2,1,0:T(8,128)S(1)}, u32[]{:S(2)}, u32[]{:S(2)}) collective-permute-start(f32[10,64,1]{2,1,0:T(8,128)S(1)} %get-tuple-element.93), channel_id=1, source_target_pairs={{1,0},{2,1},{3,2},{4,3},{5,4},{6,5},{7,6},{9,8},{10,9},{11,10},{12... | collective-permute-start | bytes 7688 | tf_op jit(solution)/shard_map/ppermute | solution.py:27
  144.7 21.6 %copy-start.6 = (f32[10,64,512]{2,1,0:T(8,128)}, f32[10,64,512]{2,1,0:T(8,128)S(1)}, u32[]{:S(2)}) copy-start(f32[10,64,512]{2,1,0:T(8,128)S(1)} %subtract_divide_fusion.1) | copy-start | bytes 3932164
  146.6 11.6 %collective-permute-start.12 = (f32[10,1,512]{2,1,0:T(1,128)S(1)}, f32[10,1,512]{2,1,0:T(1,128)S(1)}, u32[]{:S(2)}, u32[]{:S(2)}) collective-permute-start(f32[10,1,512]{2,1,0:T(1,128)S(1)} %get-tuple-element.90), channel_id=1, source_target_pairs={{0,8},{8,16},{16,24},{24,32},{32,40},{40,48},{48,56},{56,64},{64,7... | collective-permute-start | bytes 61448 | tf_op jit(solution)/shard_map/ppermute | solution.py:26
  150.2 8.0 %collective-permute-start.13 = (f32[10,1,512]{2,1,0:T(1,128)S(1)}, f32[10,1,512]{2,1,0:T(1,128)S(1)}, u32[]{:S(2)}, u32[]{:S(2)}) collective-permute-start(f32[10,1,512]{2,1,0:T(1,128)S(1)} %get-tuple-element.91), channel_id=1, source_target_pairs={{8,0},{16,8},{24,16},{32,24},{40,32},{48,40},{56,48},{64,56},{72,6... | collective-permute-start | bytes 61448 | tf_op jit(solution)/shard_map/ppermute | solution.py:27
  153.1 7.6 %collective-permute-start.14 = (f32[10,64,1]{2,1,0:T(8,128)}, f32[10,64,1]{2,1,0:T(8,128)}, u32[]{:S(2)}, u32[]{:S(2)}) collective-permute-start(f32[10,64,1]{2,1,0:T(8,128)} %get-tuple-element.88), channel_id=1, source_target_pairs={{0,1},{1,2},{2,3},{3,4},{4,5},{5,6},{6,7},{8,9},{9,10},{10,11},{11... | collective-permute-start | bytes 7688 | tf_op jit(solution)/shard_map/ppermute | solution.py:26
  155.7 8.7 %collective-permute-start.15 = (f32[10,64,1]{2,1,0:T(8,128)}, f32[10,64,1]{2,1,0:T(8,128)}, u32[]{:S(2)}, u32[]{:S(2)}) collective-permute-start(f32[10,64,1]{2,1,0:T(8,128)} %get-tuple-element.89), channel_id=1, source_target_pairs={{1,0},{2,1},{3,2},{4,3},{5,4},{6,5},{7,6},{9,8},{10,9},{11,10},{12... | collective-permute-start | bytes 7688 | tf_op jit(solution)/shard_map/ppermute | solution.py:27
  209.8 9.8 %collective-permute-start.16 = (f32[10,1,512]{2,1,0:T(1,128)S(1)}, f32[10,1,512]{2,1,0:T(1,128)S(1)}, u32[]{:S(2)}, u32[]{:S(2)}) collective-permute-start(f32[10,1,512]{2,1,0:T(1,128)S(1)} %get-tuple-element.86), channel_id=1, source_target_pairs={{0,8},{8,16},{16,24},{24,32},{32,40},{40,48},{48,56},{56,64},{64,7... | collective-permute-start | bytes 61448 | tf_op jit(solution)/shard_map/ppermute | solution.py:26
  213.6 6.0 %collective-permute-start.17 = (f32[10,1,512]{2,1,0:T(1,128)S(1)}, f32[10,1,512]{2,1,0:T(1,128)S(1)}, u32[]{:S(2)}, u32[]{:S(2)}) collective-permute-start(f32[10,1,512]{2,1,0:T(1,128)S(1)} %get-tuple-element.87), channel_id=1, source_target_pairs={{8,0},{16,8},{24,16},{32,24},{40,32},{48,40},{56,48},{64,56},{72,6... | collective-permute-start | bytes 61448 | tf_op jit(solution)/shard_map/ppermute | solution.py:27
  215.1 5.9 %collective-permute-start.18 = (f32[10,64,1]{2,1,0:T(8,128)S(1)}, f32[10,64,1]{2,1,0:T(8,128)S(1)}, u32[]{:S(2)}, u32[]{:S(2)}) collective-permute-start(f32[10,64,1]{2,1,0:T(8,128)S(1)} %get-tuple-element.84), channel_id=1, source_target_pairs={{0,1},{1,2},{2,3},{3,4},{4,5},{5,6},{6,7},{8,9},{9,10},{10,11},{11... | collective-permute-start | bytes 7688 | tf_op jit(solution)/shard_map/ppermute | solution.py:26
  217.0 8.5 %collective-permute-start.19 = (f32[10,64,1]{2,1,0:T(8,128)S(1)}, f32[10,64,1]{2,1,0:T(8,128)S(1)}, u32[]{:S(2)}, u32[]{:S(2)}) collective-permute-start(f32[10,64,1]{2,1,0:T(8,128)S(1)} %get-tuple-element.85), channel_id=1, source_target_pairs={{1,0},{2,1},{3,2},{4,3},{5,4},{6,5},{7,6},{9,8},{10,9},{11,10},{12... | collective-permute-start | bytes 7688 | tf_op jit(solution)/shard_map/ppermute | solution.py:27
  264.5 10.0 %collective-permute-start.20 = (f32[10,1,512]{2,1,0:T(1,128)S(1)}, f32[10,1,512]{2,1,0:T(1,128)S(1)}, u32[]{:S(2)}, u32[]{:S(2)}) collective-permute-start(f32[10,1,512]{2,1,0:T(1,128)S(1)} %get-tuple-element.82), channel_id=1, source_target_pairs={{0,8},{8,16},{16,24},{24,32},{32,40},{40,48},{48,56},{56,64},{64,7... | collective-permute-start | bytes 61448 | tf_op jit(solution)/shard_map/ppermute | solution.py:26
  268.1 6.4 %collective-permute-start.21 = (f32[10,1,512]{2,1,0:T(1,128)S(1)}, f32[10,1,512]{2,1,0:T(1,128)S(1)}, u32[]{:S(2)}, u32[]{:S(2)}) collective-permute-start(f32[10,1,512]{2,1,0:T(1,128)S(1)} %get-tuple-element.83), channel_id=1, source_target_pairs={{8,0},{16,8},{24,16},{32,24},{40,32},{48,40},{56,48},{64,56},{72,6... | collective-permute-start | bytes 61448 | tf_op jit(solution)/shard_map/ppermute | solution.py:27
  269.6 6.8 %collective-permute-start.22 = (f32[10,64,1]{2,1,0:T(8,128)S(1)}, f32[10,64,1]{2,1,0:T(8,128)S(1)}, u32[]{:S(2)}, u32[]{:S(2)}) collective-permute-start(f32[10,64,1]{2,1,0:T(8,128)S(1)} %get-tuple-element.80), channel_id=1, source_target_pairs={{0,1},{1,2},{2,3},{3,4},{4,5},{5,6},{6,7},{8,9},{9,10},{10,11},{11... | collective-permute-start | bytes 7688 | tf_op jit(solution)/shard_map/ppermute | solution.py:26
  272.3 8.5 %collective-permute-start.23 = (f32[10,64,1]{2,1,0:T(8,128)S(1)}, f32[10,64,1]{2,1,0:T(8,128)S(1)}, u32[]{:S(2)}, u32[]{:S(2)}) collective-permute-start(f32[10,64,1]{2,1,0:T(8,128)S(1)} %get-tuple-element.81), channel_id=1, source_target_pairs={{1,0},{2,1},{3,2},{4,3},{5,4},{6,5},{7,6},{9,8},{10,9},{11,10},{12... | collective-permute-start | bytes 7688 | tf_op jit(solution)/shard_map/ppermute | solution.py:27
  325.9 11.7 %collective-permute-start.24 = (f32[10,1,512]{2,1,0:T(1,128)S(1)}, f32[10,1,512]{2,1,0:T(1,128)S(1)}, u32[]{:S(2)}, u32[]{:S(2)}) collective-permute-start(f32[10,1,512]{2,1,0:T(1,128)S(1)} %get-tuple-element.78), channel_id=1, source_target_pairs={{0,8},{8,16},{16,24},{24,32},{32,40},{40,48},{48,56},{56,64},{64,7... | collective-permute-start | bytes 61448 | tf_op jit(solution)/shard_map/ppermute | solution.py:26
  329.6 8.1 %collective-permute-start.25 = (f32[10,1,512]{2,1,0:T(1,128)S(1)}, f32[10,1,512]{2,1,0:T(1,128)S(1)}, u32[]{:S(2)}, u32[]{:S(2)}) collective-permute-start(f32[10,1,512]{2,1,0:T(1,128)S(1)} %get-tuple-element.79), channel_id=1, source_target_pairs={{8,0},{16,8},{24,16},{32,24},{40,32},{48,40},{56,48},{64,56},{72,6... | collective-permute-start | bytes 61448 | tf_op jit(solution)/shard_map/ppermute | solution.py:27
  332.6 8.4 %collective-permute-start.26 = (f32[10,64,1]{2,1,0:T(8,128)}, f32[10,64,1]{2,1,0:T(8,128)}, u32[]{:S(2)}, u32[]{:S(2)}) collective-permute-start(f32[10,64,1]{2,1,0:T(8,128)} %get-tuple-element.76), channel_id=1, source_target_pairs={{0,1},{1,2},{2,3},{3,4},{4,5},{5,6},{6,7},{8,9},{9,10},{10,11},{11... | collective-permute-start | bytes 7688 | tf_op jit(solution)/shard_map/ppermute | solution.py:26
  334.5 8.7 %collective-permute-start.27 = (f32[10,64,1]{2,1,0:T(8,128)}, f32[10,64,1]{2,1,0:T(8,128)}, u32[]{:S(2)}, u32[]{:S(2)}) collective-permute-start(f32[10,64,1]{2,1,0:T(8,128)} %get-tuple-element.77), channel_id=1, source_target_pairs={{1,0},{2,1},{3,2},{4,3},{5,4},{6,5},{7,6},{9,8},{10,9},{11,10},{12... | collective-permute-start | bytes 7688 | tf_op jit(solution)/shard_map/ppermute | solution.py:27
  345.5 39.8 %copy-start.5 = (f32[10,64,512]{2,1,0:T(8,128)S(1)}, f32[10,64,512]{2,1,0:T(8,128)}, u32[]{:S(2)}) copy-start(f32[10,64,512]{2,1,0:T(8,128)} %copy-done.3) | copy-start | bytes 3932164
  (41 other events, 206.7 us)
where the time goes:
time: 392 us; the launch traced here: 390 us
  blocking collectives  198 us (51%)
  other arithmetic  74.3 us (19%)
  starting transfers between devices  71.2 us (18%)
  between operations  19.5 us (5%)
  waiting for transfers between devices  17.5 us (4%)
  local copies, waits for them, and re-layouts  8.9 us (2%)
    psum x24, blocking collectives, by_axis(): value = lax.psum(value, axis)  198 us
    ppermute x14, starting transfers between devices, padded(): lax.ppermute(last, axis, up)  45.4 us
    ppermute x14, starting transfers between devices, padded(): lax.ppermute(initial, axis, [(b, a) for a, b in up])  25.8 us
    ppermute x14, waiting for transfers between devices, padded(): lax.ppermute(initial, axis, [(b, a) for a, b in up])  17.3 us
    add x4, other arithmetic, jacobian_apply(): flow_y = y_low * vector[:, 1:-1, :-1] + y_high * vector[:, 1:-1, 1:]  11.4 us
    mul x6, other arithmetic, face_pair(): return (coef_low, coef_high, transmit * mobility * head_drop)  10.8 us
    add x4, other arithmetic, jacobian_apply(): flow_x = x_low * vector[:, :-1, 1:-1] + x_high * vector[:, 1:, 1:-1]  10.7 us
  transfers between devices with their start and end apart: 28, of which 7 were waited for; matrix products, arithmetic and copies ran while one was open for 6% of the time, Pallas kernels for 0%

commit v1 on v0

v1 whole, which is shorter than its diff:
```python
import jax
import jax.numpy as jnp
from jax import lax
from jax.experimental import pallas as pl
from jax.experimental.pallas import tpu as pltpu
from jax.sharding import Mesh
from jax.sharding import PartitionSpec as P

GX = ("gx_0", "gx_1")
GY = ("gy_0", "gy_1")
ALL = GX + GY

EPS = 1e-06
NT = 5
ROWS = 80
TOP = 8
F32 = jnp.float32


def lanes():
    return lax.broadcasted_iota(jnp.int32, (8, 128), 1)


def from_north(tiles):
    lane = lanes()
    turned = [pltpu.roll(tile, 127, 1) for tile in tiles]
    count = len(tiles)
    return [jnp.where(lane == 127, turned[(t + 1) % count], turned[t]) for t in range(count)]


def from_south(tiles):
    lane = lanes()
    turned = [pltpu.roll(tile, 1, 1) for tile in tiles]
    count = len(tiles)
    return [jnp.where(lane == 0, turned[(t - 1) % count], turned[t]) for t in range(count)]


def tile_of(ref, layer, t, start):
    return ref[layer, t, pl.ds(start, 8), :]


def tiles_of(ref, layer, start):
    return [tile_of(ref, layer, t, start) for t in range(NT)]


def flat_tiles(ref, start):
    return [ref[t, pl.ds(start, 8), :] for t in range(NT)]


UNITS = 25


def load_kernel(layers, par, p_in, k_in, o_in, r_in, rech_in, act_in,
                p_ref, k_ref, o_ref, r_ref, rech_ref, act_ref, send_a, send_b, act_int, sems):
    copies = []
    for order, t in enumerate((0, 3, 1, 2)):
        cols = pl.ds(128 * t, 128)
        for f, (src, dst) in enumerate(((p_in, p_ref), (k_in, k_ref), (o_in, o_ref), (r_in, r_ref))):
            copies.append(pltpu.make_async_copy(
                src.at[:, :, cols], dst.at[:, t, pl.ds(TOP, 64), :], sems.at[order * 6 + f]))
        copies.append(pltpu.make_async_copy(
            rech_in.at[:, cols], rech_ref.at[t, pl.ds(TOP, 64), :], sems.at[order * 6 + 4]))
        copies.append(pltpu.make_async_copy(act_in.at[:, cols], act_int.at[t], sems.at[order * 6 + 5]))
    for copy in copies:
        copy.start()
    zero = jnp.zeros((8, 128), F32)

    def clear(layer, carry):
        for ref in (p_ref, k_ref, o_ref, r_ref):
            for t in range(NT):
                ref[layer, t, 0:8, :] = zero
                ref[layer, t, ROWS - 8:ROWS, :] = zero
        return carry

    lax.fori_loop(0, layers, clear, 0)
    for ref in (rech_ref, act_ref):
        for t in range(NT):
            ref[t, 0:8, :] = zero
            ref[t, ROWS - 8:ROWS, :] = zero
    for copy in copies[:12]:
        copy.wait()
    for t in (0, 3):
        act_ref[t, TOP:TOP + 64, :] = act_int[t].astype(F32)
    first = lanes() < 5
    last = lanes() >= 123
    odd = par[0] == 1

    def pack(row, carry):
        start = pl.multiple_of(TOP + 8 * row, 8)
        low = [zero, zero]
        high = [zero, zero]
        units = [(ref, layer) for ref in (p_ref, k_ref, o_ref, r_ref) for layer in range(layers)]
        units = units + [(act_ref, None), (rech_ref, None)]
        for u, (ref, layer) in enumerate(units):
            at = 5 * (u % UNITS)
            here = u // UNITS
            if layer is None:
                a, b = ref[0, pl.ds(start, 8), :], ref[3, pl.ds(start, 8), :]
            else:
                a, b = tile_of(ref, layer, 0, start), tile_of(ref, layer, 3, start)
            a = jnp.where(first, a, 0.0)
            b = jnp.where(last, b, 0.0)
            low[here] = low[here] + (pltpu.roll(a, at, 1) if at else a)
            high[here] = high[here] + pltpu.roll(b, (at + 5) % 128, 1)
        out = pl.multiple_of(8 * row, 8)
        for here in range(2):
            send_a[here, pl.ds(out, 8), :] = jnp.where(odd, low[here], high[here])
            send_b[here, pl.ds(out, 8), :] = jnp.where(odd, high[here], low[here])
        return carry

    lax.fori_loop(0, 8, pack, 0)
    for copy in copies[12:]:
        copy.wait()
    for t in (1, 2):
        act_ref[t, TOP:TOP + 64, :] = act_int[t].astype(F32)


def strip_rows(layers):
    return ((0, 5), (5, 5), (10, 4), (14, 4))


def turn_kernel(layers, par_y, par_x, p_old, k_old, o_old, r_old, rech_old, act_old, got_a, got_b,
                p_ref, k_ref, o_ref, r_ref, rech_ref, act_ref, send_a, send_b):
    odd = par_y[0] == 1
    left_edge = lanes() >= 123
    right_edge = lanes() < 5

    def unpack(row, carry):
        start = pl.multiple_of(TOP + 8 * row, 8)
        src = pl.multiple_of(8 * row, 8)
        a = [got_a[here, pl.ds(src, 8), :] for here in range(2)]
        b = [got_b[here, pl.ds(src, 8), :] for here in range(2)]
        below = [jnp.where(odd, a[h], b[h]) for h in range(2)]
        above = [jnp.where(odd, b[h], a[h]) for h in range(2)]
        units = [(ref, layer) for ref in (p_ref, k_ref, o_ref, r_ref) for layer in range(layers)]
        units = units + [(act_ref, None), (rech_ref, None)]
        for u, (ref, layer) in enumerate(units):
            at = 5 * (u % UNITS)
            here = u // UNITS
            left = pltpu.roll(below[here], (123 - at) % 128, 1)
            right = pltpu.roll(above[here], (128 - at) % 128, 1) if at else above[here]
            value = jnp.where(left_edge, left, jnp.where(right_edge, right, 0.0))
            if layer is None:
                ref[4, pl.ds(start, 8), :] = value
            else:
                ref[layer, 4, pl.ds(start, 8), :] = value
        return carry

    lax.fori_loop(0, 8, unpack, 0)
    up = par_x[0] == 1
    low, high = TOP, TOP + 64
    fields = (p_ref, k_ref, o_ref, r_ref)
    for send, lower in ((send_a, up), (send_b, jnp.logical_not(up))):
        start5 = jnp.where(lower, low, high - 5)
        start4 = jnp.where(lower, low, high - 4)

        def fill(layer, carry):
            for (at, depth), ref in zip(strip_rows(layers), fields):
                start = start5 if depth == 5 else start4
                for t in range(NT):
                    send[t, pl.ds(layer * 18 + at, depth), :] = ref[layer, t, pl.ds(start, depth), :]
            return carry

        lax.fori_loop(0, layers, fill, 0)
        for t in range(NT):
            send[t, 18 * layers:18 * layers + 5, :] = act_ref[t, pl.ds(start5, 5), :]
            send[t, 18 * layers + 5:18 * layers + 9, :] = rech_ref[t, pl.ds(start4, 4), :]


def place_strips(layers, up, refs, got_a, got_b):
    p_ref, k_ref, o_ref, r_ref, rech_ref, act_ref = refs
    fields = (p_ref, k_ref, o_ref, r_ref)
    low, high = TOP, TOP + 64
    for got, above in ((got_a, jnp.logical_not(up)), (got_b, up)):
        dst5 = jnp.where(above, high, low - 5)
        dst4 = jnp.where(above, high, low - 4)

        def fill(layer, carry):
            for (at, depth), ref in zip(strip_rows(layers), fields):
                start = dst5 if depth == 5 else dst4
                for t in range(NT):
                    ref[layer, t, pl.ds(start, depth), :] = got[t, pl.ds(layer * 18 + at, depth), :]
            return carry

        lax.fori_loop(0, layers, fill, 0)
        for t in range(NT):
            act_ref[t, pl.ds(dst5, 5), :] = got[t, 18 * layers:18 * layers + 5, :]
            rech_ref[t, pl.ds(dst4, 4), :] = got[t, 18 * layers + 5:18 * layers + 9, :]


def sigmoid_tile(value, layer, t, start, sig_ref, mob_ref, der_ref):
    sig = jax.nn.sigmoid(value)
    square = sig * sig
    sig_ref[layer, t, pl.ds(start, 8), :] = sig
    mob_ref[layer, t, pl.ds(start, 8), :] = 0.5 * square
    der_ref[layer, t, pl.ds(start, 8), :] = square - square * sig


def face(trans, p_a, p_b, m_a, m_b, s_a, s_b, gravity):
    drop = p_a - p_b
    if gravity:
        drop = drop + gravity
    by_mob = trans * (m_a + m_b)
    by_drop = trans * drop
    return by_mob + s_a * by_drop, s_b * by_drop - by_mob, by_mob * drop


def far_faces(layers, starts, s, make_trans):
    def one_layer(layer, carry):
        upper = jnp.minimum(layer + 1, layers - 1)
        inner = jnp.where(layer + 1 < layers, 1.0, 0.0).astype(F32)
        for start in starts:
            rows = pl.ds(start, 8)
            for t in range(NT):
                if make_trans:
                    trans = s.ax[t, rows, :] * (tile_of(s.k, layer, t, start) + tile_of(s.k, layer, t, start + 1))
                    s.tx[layer, t, rows, :] = trans
                else:
                    trans = tile_of(s.tx, layer, t, start)
                p = tile_of(s.p, layer, t, start)
                m = tile_of(s.m, layer, t, start)
                der = tile_of(s.s, layer, t, start)
                ca, cb, flow = face(
                    trans, p, tile_of(s.p, layer, t, start + 1), m, tile_of(s.m, layer, t, start + 1),
                    der, tile_of(s.s, layer, t, start + 1), 0.0)
                s.xa[layer, t, rows, :] = ca
                s.xb[layer, t, rows, :] = cb
                s.xf[layer, t, rows, :] = flow
                if make_trans:
                    trans = (s.act[t, rows, :] * inner) * (
                        tile_of(s.k, layer, t, start) + tile_of(s.k, upper, t, start))
                    s.tz[layer, t, rows, :] = trans
                else:
                    trans = tile_of(s.tz, layer, t, start)
                za, zb, zf = face(
                    trans, p, tile_of(s.p, upper, t, start), m, tile_of(s.m, upper, t, start),
                    der, tile_of(s.s, upper, t, start), -1.0)
                s.za[layer + 1, t, rows, :] = za
                s.zb[layer + 1, t, rows, :] = zb
                s.zf[layer + 1, t, rows, :] = zf
        return carry

    lax.fori_loop(0, layers, one_layer, 0)


def assemble(layers, starts, s, make_trans):
    def one_layer(layer, carry):
        for start in starts:
            rows = pl.ds(start, 8)
            p = tiles_of(s.p, layer, start)
            m = tiles_of(s.m, layer, start)
            der = tiles_of(s.s, layer, start)
            if make_trans:
                k = tiles_of(s.k, layer, start)
                k_north = from_north(k)
                ty = [s.ay[t, rows, :] * (k[t] + k_north[t]) for t in range(NT)]
                for t in range(NT):
                    s.ty[layer, t, rows, :] = ty[t]
            else:
                ty = tiles_of(s.ty, layer, start)
            p_north, m_north, s_north = from_north(p), from_north(m), from_north(der)
            across_y = [face(ty[t], p[t], p_north[t], m[t], m_north[t], der[t], s_north[t], 0.0) for t in range(NT)]
            ya = from_south([f[0] for f in across_y])
            yb = from_south([f[1] for f in across_y])
            yf = from_south([f[2] for f in across_y])
            for t in range(NT):
                s.ya[layer, t, rows, :] = ya[t]
                s.yb[layer, t, rows, :] = across_y[t][1]
                sig = tile_of(s.sig, layer, t, start)
                ap = tile_of(s.ap, layer, t, start)
                ocean = 1.0 - s.act[t, rows, :]
                stored = ap * sig
                center = (stored - stored * sig) + ocean
                center = center + (tile_of(s.xa, layer, t, start) - tile_of(s.xb, layer, t, start - 1))
                center = center + (across_y[t][0] - yb[t]) + (tile_of(s.za, layer + 1, t, start) - tile_of(s.zb, layer, t, start))
                s.c[layer, t, rows, :] = center
                flows = (tile_of(s.xf, layer, t, start) - tile_of(s.xf, layer, t, start - 1))
                flows = flows + (across_y[t][2] - yf[t]) + (tile_of(s.zf, layer + 1, t, start) - tile_of(s.zf, layer, t, start))
                s.q[layer, t, rows, :] = (tile_of(s.s0, layer, t, start) - stored) - ocean * p[t] - flows
        return carry

    lax.fori_loop(0, layers, one_layer, 0)


def product_tile(layers, s, v_ref, layer, start, count):
    v = tiles_of(v_ref, layer, start)
    north, south = from_north(v), from_south(v)
    upper = jnp.minimum(layer + 1, layers - 1)
    lower = jnp.maximum(layer - 1, 0)
    out = []
    for t in range(count):
        value = tile_of(s.c, layer, t, start) * v[t]
        value = value + (tile_of(s.xb, layer, t, start) * tile_of(v_ref, layer, t, start + 1)
                         - tile_of(s.xa, layer, t, start - 1) * tile_of(v_ref, layer, t, start - 1))
        value = value + (tile_of(s.yb, layer, t, start) * north[t] - tile_of(s.ya, layer, t, start) * south[t])
        value = value + (tile_of(s.zb, layer + 1, t, start) * tile_of(v_ref, upper, t, start)
                         - tile_of(s.za, layer, t, start) * tile_of(v_ref, lower, t, start))
        out.append(value)
    return v, out


def first_product(layers, starts, s):
    def one_layer(layer, carry):
        for start in starts:
            _, out = product_tile(layers, s, s.q, layer, start, NT)
            for t in range(NT):
                s.w[layer, t, pl.ds(start, 8), :] = out[t]
        return carry

    lax.fori_loop(0, layers, one_layer, 0)


def second_product(layers, starts, s, sums, z_ref):
    def one_layer(layer, sums):
        sums = list(sums)
        for start in starts:
            w, z = product_tile(layers, s, s.w, layer, start, NT - 1)
            for t in range(NT - 1):
                q = tile_of(s.q, layer, t, start)
                if z_ref is not None:
                    z_ref[layer, t, pl.ds(start - TOP, 8), :] = z[t]
                for i, (a, b) in enumerate(((q, q), (q, w[t]), (q, z[t]), (w[t], w[t]), (w[t], z[t]), (z[t], z[t]))):
                    sums[i] = sums[i] + a * b
        return tuple(sums)

    return lax.fori_loop(0, layers, one_layer, sums)


def put_sums(sums, out_ref):
    lane = lax.broadcasted_iota(jnp.int32, (1, 128), 1)
    row = jnp.zeros((1, 128), F32)
    for i, part in enumerate(sums):
        total = jnp.sum(jnp.sum(part, axis=0, keepdims=True), axis=1, keepdims=True)
        row = row + jnp.where(lane == i, total, 0.0)
    out_ref[...] = jnp.broadcast_to(row, out_ref.shape)


def step_weights(sums_ref):
    total = jnp.sum(sums_ref[...], axis=0, keepdims=True)
    lane = lax.broadcasted_iota(jnp.int32, (1, 128), 1)
    qq, qw, qz, ww, wz, zz = (
        jnp.sum(jnp.where(lane == i, total, 0.0), axis=1, keepdims=True) for i in range(6))
    first = qq + EPS
    qq, qw, qz, ww, wz, zz = (entry / first for entry in (qq, qw, qz, ww, wz, zz))
    norm = jnp.sqrt(first)
    h11 = qw
    left = jnp.maximum(ww - 2.0 * h11 * qw + h11 * h11 * qq, 0.0)
    square = left + EPS
    h21 = jnp.sqrt(square)
    h12 = (qz - h11 * qw) / h21
    h22 = (wz - h11 * qz - h11 * (ww - h11 * qw)) / square
    length = (zz - 2.0 * h11 * wz + h11 * h11 * ww) / square
    cross = (qw - h11 * qq) / h21
    rest = (length - 2.0 * (h12 * h12 + h22 * h22) + h12 * h12 * qq + h22 * h22 * (left / square)
            + 2.0 * h12 * h22 * cross)
    third = jnp.maximum(rest, 0.0) + EPS
    radius = jnp.sqrt(h11 * h11 + square)
    cosine = h11 / radius
    sine = h21 / radius
    top = cosine * h12 + sine * h22
    lower = cosine * h22 - sine * h12
    y2 = -lower * sine * norm / (lower * lower + third)
    y1 = (cosine * norm - top * y2) / radius
    b = y2 / (norm * h21)
    a = y1 / norm - b * h11
    return jnp.broadcast_to(a, (8, 128)), jnp.broadcast_to(b, (8, 128))


class Refs:
    def __init__(self, **refs):
        self.__dict__.update(refs)


COEFS = ("sig", "m", "s", "c", "xa", "xb", "ya", "yb", "za", "zb", "zf", "xf")


def coef_scratch(layers):
    return [pltpu.VMEM((layers + (name in ("za", "zb", "zf")), NT, ROWS, 128), F32) for name in COEFS]


def clear_bottom(s):
    zero = jnp.zeros((8, 128), F32)
    for ref in (s.za, s.zb, s.zf):
        for t in range(NT):
            for row in range(0, ROWS, 8):
                ref[0, t, row:row + 8, :] = zero


def first_kernel(layers, par_x, p_old, k_old, o_old, r_old, rech_old, act_old, got_a, got_b,
                 p_ref, k_ref, s0_ref, ap_ref, rech_ref, act_ref, tx, ty, tz, q_ref, w_ref, sums_ref,
                 ax, ay, *coefs):
    place_strips(layers, par_x[0] == 1, (p_ref, k_ref, s0_ref, ap_ref, rech_ref, act_ref), got_a, got_b)
    s = Refs(p=p_ref, k=k_ref, s0=s0_ref, ap=ap_ref, act=act_ref, tx=tx, ty=ty, tz=tz, q=q_ref, w=w_ref,
             ax=ax, ay=ay, **dict(zip(COEFS, coefs)))
    clear_bottom(s)
    def pairs(i, carry):
        start = 4 * i
        act = flat_tiles(act_ref, start)
        north = from_north(act)
        for t in range(NT):
            ax[t, pl.ds(start, 8), :] = 0.5 * act[t] * act_ref[t, pl.ds(start + 1, 8), :]
            ay[t, pl.ds(start, 8), :] = 0.5 * act[t] * north[t]
        return carry

    lax.fori_loop(0, 18, pairs, 0)

    def point(layer, carry):
        top = jnp.where(layer == layers - 1, 1.0, 0.0).astype(F32)
        for start in range(0, ROWS, 8):
            rows = pl.ds(start, 8)
            for t in range(NT):
                sigmoid_tile(tile_of(p_ref, layer, t, start), layer, t, start, s.sig, s.m, s.s)
                act = act_ref[t, rows, :]
                ap = (0.9 * act) * tile_of(ap_ref, layer, t, start)
                ap_ref[layer, t, rows, :] = ap
                s0_ref[layer, t, rows, :] = (
                    ap * jax.nn.sigmoid(tile_of(s0_ref, layer, t, start)) + (top * act) * rech_ref[t, rows, :])
        return carry

    lax.fori_loop(0, layers, point, 0)
    starts = range(4, 76, 8)
    far_faces(layers, (0, *starts), s, True)
    assemble(layers, starts, s, True)
    first_product(layers, starts, s)
    sums = tuple(jnp.zeros((8, 128), F32) for _ in range(6))
    sums = second_product(layers, range(TOP, TOP + 64, 8), s, sums, None)
    put_sums(sums, sums_ref)


def next_kernel(layers, p_old, s0_ref, ap_ref, act_ref, tx, ty, tz, q_old, w_old, got_ref,
                p_ref, q_ref, w_ref, z_ref, sums_ref, *coefs):
    a, b = step_weights(got_ref)
    s = Refs(p=p_ref, s0=s0_ref, ap=ap_ref, act=act_ref, tx=tx, ty=ty, tz=tz, q=q_ref, w=w_ref,
             **dict(zip(COEFS, coefs)))
    clear_bottom(s)

    def point(layer, carry):
        for start in range(4, 76, 8):
            rows = pl.ds(start, 8)
            for t in range(NT):
                p = tile_of(p_ref, layer, t, start) + (
                    a * tile_of(q_ref, layer, t, start) + b * tile_of(w_ref, layer, t, start))
                p_ref[layer, t, rows, :] = p
                sigmoid_tile(p, layer, t, start, s.sig, s.m, s.s)
        return carry

    lax.fori_loop(0, layers, point, 0)
    starts = range(4, 76, 8)
    far_faces(layers, (0, *starts), s, False)
    assemble(layers, starts, s, False)
    first_product(layers, starts, s)
    sums = tuple(jnp.zeros((8, 128), F32) for _ in range(6))
    sums = second_product(layers, range(TOP, TOP + 64, 8), s, sums, z_ref)
    put_sums(sums, sums_ref)


def last_kernel(layers, p_ref, q_ref, w_ref, z_ref, got_ref, final_out, left_out, final_buf, left_buf, sems):
    a, b = step_weights(got_ref)
    for layer in range(layers):
        for start in range(0, 64, 8):
            for t in range(NT - 1):
                q = q_ref[layer, t, TOP + start:TOP + start + 8, :]
                w = w_ref[layer, t, TOP + start:TOP + start + 8, :]
                place = (layer, slice(start, start + 8), slice(128 * t, 128 * t + 128))
                final_buf[place] = p_ref[layer, t, TOP + start:TOP + start + 8, :] + (a * q + b * w)
                left_buf[place] = (q - a * w) - b * z_ref[layer, t, start:start + 8, :]
        pltpu.make_async_copy(final_buf.at[layer], final_out.at[layer], sems.at[layer, 0]).start()
        pltpu.make_async_copy(left_buf.at[layer], left_out.at[layer], sems.at[layer, 1]).start()
    for layer in range(layers):
        pltpu.make_async_copy(final_buf.at[layer], final_out.at[layer], sems.at[layer, 0]).wait()
        pltpu.make_async_copy(left_buf.at[layer], left_out.at[layer], sems.at[layer, 1]).wait()


VM = pl.BlockSpec(memory_space=pltpu.VMEM)
HB = pl.BlockSpec(memory_space=pl.ANY)
SM = pl.BlockSpec(memory_space=pltpu.SMEM)


def grant(mib):
    return pltpu.CompilerParams(vmem_limit_bytes=mib * 1024 * 1024)


def keep(*arrays):
    return [pltpu.with_memory_space_constraint(array, pltpu.VMEM) for array in arrays]


def outside(*arrays):
    return [pltpu.with_memory_space_constraint(array, pltpu.HBM) for array in arrays]


def swap(value, axes, first):
    size = lax.axis_size(axes)
    pairs = [(i, i + 1) for i in range(first, size - 1, 2)]
    return lax.ppermute(value, axes, pairs + [(b, a) for a, b in pairs])


def bound(kernel, *args):
    def call(*refs):
        kernel(*args, *refs)

    return call


def body(pressure, pressure_old, conductivity, porosity, recharge, active):
    layers = pressure.shape[0]
    par_x = (lax.axis_index(GX) % 2).astype(jnp.int32).reshape(1)
    par_y = (lax.axis_index(GY) % 2).astype(jnp.int32).reshape(1)
    field = pltpu.VMEM((layers, NT, ROWS, 128), F32)
    plane = pltpu.VMEM((NT, ROWS, 128), F32)
    strip_y = pltpu.VMEM((2, 64, 128), F32)
    strip_x = pltpu.VMEM((NT, 192, 128), F32)
    state = (field,) * 4 + (plane,) * 2
    *fields, send_a, send_b = pl.pallas_call(
        bound(load_kernel, layers), name="load", out_shape=state + (strip_y,) * 2,
        in_specs=[SM] + [HB] * 6, out_specs=(VM,) * 8,
        scratch_shapes=[pltpu.VMEM((4, 64, 128), jnp.int32), pltpu.SemaphoreType.DMA((24,))],
        compiler_params=grant(6),
    )(par_y, *outside(pressure, conductivity, pressure_old, porosity, recharge, active))
    got_a = swap(send_a, GY, 0)
    got_b = swap(send_b, GY, 1)
    *fields, send_a, send_b = pl.pallas_call(
        bound(turn_kernel, layers), name="turn", out_shape=state + (strip_x,) * 2,
        in_specs=[SM] * 2 + [VM] * 8, out_specs=(VM,) * 8,
        input_output_aliases={i + 2: i for i in range(6)}, compiler_params=grant(6),
    )(par_y, par_x, *keep(*fields), got_a, got_b)
    got_a = swap(send_a, GX, 0)
    got_b = swap(send_b, GX, 1)
    p, _, s0, ap, _, act, tx, ty, tz, q, w, sums = pl.pallas_call(
        bound(first_kernel, layers), name="first",
        out_shape=state + (field,) * 5 + (jax.ShapeDtypeStruct((128, 128), F32),),
        in_specs=[SM] + [VM] * 8, out_specs=(VM,) * 12,
        input_output_aliases={i + 1: i for i in range(6)},
        scratch_shapes=[plane, plane] + coef_scratch(layers), compiler_params=grant(30),
    )(par_x, *keep(*fields), got_a, got_b)
    sums = lax.all_to_all(sums, ALL, 0, 0, tiled=True)
    p, q, w, z, sums = pl.pallas_call(
        bound(next_kernel, layers), name="next",
        out_shape=(field,) * 3 + (pltpu.VMEM((layers, 4, 64, 128), F32), jax.ShapeDtypeStruct((128, 128), F32)),
        in_specs=[VM] * 10, out_specs=(VM,) * 5, input_output_aliases={0: 0, 7: 1, 8: 2},
        scratch_shapes=coef_scratch(layers), compiler_params=grant(30),
    )(*keep(p, s0, ap, act, tx, ty, tz, q, w), sums)
    sums = lax.all_to_all(sums, ALL, 0, 0, tiled=True)
    out = jax.ShapeDtypeStruct(pressure.shape, F32)
    block = pltpu.VMEM(pressure.shape, F32)
    return pl.pallas_call(
        bound(last_kernel, layers), name="last", out_shape=(out, out),
        in_specs=[VM] * 5, out_specs=(HB, HB),
        scratch_shapes=[block, block, pltpu.SemaphoreType.DMA((layers, 2))], compiler_params=grant(8),
    )(*keep(p, q, w, z), sums)


def solution(mesh):
    torus = Mesh(mesh.devices.reshape(4, 4, 4, 2), ALL)
    field = P(None, GX, GY)
    plane = P(GX, GY)
    return jax.shard_map(
        body, mesh=torus, in_specs=(field,) * 4 + (plane,) * 2, out_specs=(field, field), check_vma=False)
```

time: 392 us -> 116 us (0.30)
  blocking collectives: 198 us -> 42 us
  other arithmetic: 74.3 us -> 0 us
  starting transfers between devices: 71.2 us -> 6.58 us
  Pallas kernels: 0 us -> 40 us
  between operations: 19.5 us -> 0.74 us
  local copies, waits for them, and re-layouts: 8.9 us -> 17.3 us
  waiting for transfers between devices: 17.5 us -> 9.44 us
    psum x24 -> x0, blocking collectives: 198 us -> none  [by_axis(): value = lax.psum(value, axis)]
    ppermute x28 -> x4, starting transfers between devices: 71.2 us -> 6.58 us  [swap(): return lax.ppermute(value, axes, pairs + [(b, a) for a, b in pairs])]
    all_to_all x0 -> x2, blocking collectives: none -> 42 us  [body(): sums = lax.all_to_all(sums, ALL, 0, 0, tiled=True)]
    pallas_call x0 -> x5, Pallas kernels: none -> 40 us  [the longest x1 18.3 us: body(): pl.pallas_call(bound(first_kernel, layers), name='first', out_shape=state...]
    add x13 -> x0, other arithmetic: 29.7 us -> none  [the longest x4 11.4 us: jacobian_apply(): flow_y = y_low * vector[:, 1:-1, :-1] + y_high * vector[:, 1:-1, 1:]]
    reduce_sum x6 -> x0, other arithmetic: 16.6 us -> none  [the longest x2 5.9 us: body(): jnp.sum(image_one * basis_one)]
    unnamed x91 -> x24, local copies, waits for them, and re-layouts: 2.73 us -> 17.3 us
    mul x8 -> x0, other arithmetic: 11 us -> none  [the longest x6 10.8 us: face_pair(): return (coef_low, coef_high, transmit * mobility * head_drop)]
  transfers between devices with their start and end apart: 28 -> 4, of which waited for: 7 -> 2; matrix products, arithmetic and copies ran while one was open for 6% -> 0% of each run, Pallas kernels for 0% -> 0%
where the time goes in v1:
time: 116 us
  blocking collectives  42 us (36%)
  Pallas kernels  40 us (34%)
  local copies, waits for them, and re-layouts  17.3 us (15%)
  waiting for transfers between devices  9.44 us (8%)
  starting transfers between devices  6.58 us (6%)
    all_to_all x2, blocking collectives, body(): sums = lax.all_to_all(sums, ALL, 0, 0, tiled=True)  42 us
    pallas_call x1, Pallas kernels, body(): pl.pallas_call(bound(first_kernel, layers), name='first', out_shape=state...  18.3 us
    unnamed x24, local copies, waits for them, and re-layouts  17.3 us
    pallas_call x1, Pallas kernels, body(): pl.pallas_call(bound(next_kernel, layers), name='next', out_shape=(field,...  15.2 us
    ppermute x4, waiting for transfers between devices, swap(): return lax.ppermute(value, axes, pairs + [(b, a) for a, b in pairs])  9.44 us
    ppermute x4, starting transfers between devices, swap(): return lax.ppermute(value, axes, pairs + [(b, a) for a, b in pairs])  6.58 us
    pallas_call x1, Pallas kernels, body(): pl.pallas_call(bound(load_kernel, layers), name='load', out_shape=state +...  3.24 us
  transfers between devices with their start and end apart: 4, of which 2 were waited for; matrix products, arithmetic and copies ran while one was open for 0% of the time, Pallas kernels for 0%

profile of v1, /device:TPU:1, one launch (start us, length us, event | category | flops | bytes accessed | tf_op | source)
XLA Modules:
  0.0 116.1 jit_solution(15504042086900788781)
XLA Ops:
  0.6 3.2 %load.1 = (f32[10,5,80,128]{3,2,1,0:T(8,128)S(1)}, f32[10,5,80,128]{3,2,1,0:T(8,128)S(1)}, f32[10,5,80,128]{3,2,1,0:T(8,128)S(1)}, f32[10,5,80,128]{3,2,1,0:T(8,...) custom-call(s32[1]{0:T(128)} %bitcast.1.refs_0_, ...), custom_call_target="tpu_custom_call" | custom-call | tf_op jit(solution)/shard_map/load/pallas_call | solution.py:513
  3.9 0.0 copy-start
  3.9 1.3 %copy-done = f32[10,5,80,128]{3,2,1,0:T(8,128)} copy-done((f32[10,5,80,128]{3,2,1,0:T(8,128)}, f32[10,5,80,128]{3,2,1,0:T(8,128)S(1)}, u32[]{:S(2)}) %copy-start) | copy-done | bytes 2048024
  5.2 0.0 copy-start.4
  5.2 1.3 %copy-done.4 = f32[10,5,80,128]{3,2,1,0:T(8,128)} copy-done((f32[10,5,80,128]{3,2,1,0:T(8,128)}, f32[10,5,80,128]{3,2,1,0:T(8,128)S(1)}, u32[]{:S(2)}) %copy-start.4) | copy-done | bytes 2048024
  6.5 0.0 copy-start.8
  6.5 1.3 %copy-done.8 = f32[10,5,80,128]{3,2,1,0:T(8,128)} copy-done((f32[10,5,80,128]{3,2,1,0:T(8,128)}, f32[10,5,80,128]{3,2,1,0:T(8,128)S(1)}, u32[]{:S(2)}) %copy-start.8) | copy-done | bytes 2048024
  7.8 1.4 %collective-permute-start = (f32[2,64,128]{2,1,0:T(8,128)S(1)}, f32[2,64,128]{2,1,0:T(8,128)S(1)}, u32[]{:S(2)}, u32[]{:S(2)}) collective-permute-start(f32[2,64,128]{2,1,0:T(8,128)S(1)} %get-tuple-element.39), channel_id=1, source_target_pairs={{0,1},{2,3},{4,5},{6,7},{1,0},{3,2},{5,4},{7,6},{8,9},{10,11},{12,... | collective-permute-start | bytes 196616 | tf_op jit(solution)/shard_map/ppermute | solution.py:494
  9.2 3.2 %collective-permute-start.1 = (f32[2,64,128]{2,1,0:T(8,128)S(1)}, f32[2,64,128]{2,1,0:T(8,128)S(1)}, u32[]{:S(2)}, u32[]{:S(2)}) collective-permute-start(f32[2,64,128]{2,1,0:T(8,128)S(1)} %get-tuple-element.40), channel_id=1, source_target_pairs={{1,2},{3,4},{5,6},{2,1},{4,3},{6,5},{9,10},{11,12},{13,14},{10,9},... | collective-permute-start | bytes 196616 | tf_op jit(solution)/shard_map/ppermute | solution.py:494
  12.4 0.0 collective-permute-done.refs_8_
  12.4 2.3 %collective-permute-done.1.refs_9_ = f32[2,64,128]{2,1,0:T(8,128)S(1)} collective-permute-done((f32[2,64,128]{2,1,0:T(8,128)S(1)}, f32[2,64,128]{2,1,0:T(8,128)S(1)}, u32[]{:S(2)}, u32[]{:S(2)}) %collective-permute-start.1) | collective-permute-done | bytes 65568 | tf_op jit(solution)/shard_map/ppermute | solution.py:494
  14.8 0.0 copy-start.1
  14.8 1.6 %copy-done.1 = f32[10,5,80,128]{3,2,1,0:T(8,128)S(1)} copy-done((f32[10,5,80,128]{3,2,1,0:T(8,128)S(1)}, f32[10,5,80,128]{3,2,1,0:T(8,128)}, u32[]{:S(2)}) %copy-start.1) | copy-done | bytes 2048024
  16.4 1.6 %copy-done.5 = f32[10,5,80,128]{3,2,1,0:T(8,128)S(1)} copy-done((f32[10,5,80,128]{3,2,1,0:T(8,128)S(1)}, f32[10,5,80,128]{3,2,1,0:T(8,128)}, u32[]{:S(2)}) %copy-start.5) | copy-done | bytes 2048024
  17.9 1.6 %copy-done.9 = f32[10,5,80,128]{3,2,1,0:T(8,128)S(1)} copy-done((f32[10,5,80,128]{3,2,1,0:T(8,128)S(1)}, f32[10,5,80,128]{3,2,1,0:T(8,128)}, u32[]{:S(2)}) %copy-start.9) | copy-done | bytes 2048024
  19.5 1.5 %turn.1 = (f32[10,5,80,128]{3,2,1,0:T(8,128)S(1)}, f32[10,5,80,128]{3,2,1,0:T(8,128)S(1)}, f32[10,5,80,128]{3,2,1,0:T(8,128)S(1)}, f32[10,5,80,128]{3,2,1,0:T(8,...) custom-call(s32[1]{0:T(128)} %bitcast.1.refs_0_, ...), custom_call_target="tpu_custom_call", output_to_operand_aliasing={{0}: (2, {}), {1}: (3, {}), {2}: (4, {}), {3}: (5, {}), {4}... | custom-call | tf_op jit(solution)/shard_map/turn/pallas_call | solution.py:521
  21.0 0.0 copy-start.2
  21.0 1.3 %copy-done.2 = f32[10,5,80,128]{3,2,1,0:T(8,128)} copy-done((f32[10,5,80,128]{3,2,1,0:T(8,128)}, f32[10,5,80,128]{3,2,1,0:T(8,128)S(1)}, u32[]{:S(2)}) %copy-start.2) | copy-done | bytes 2048024
  22.3 1.3 %copy-done.6 = f32[10,5,80,128]{3,2,1,0:T(8,128)} copy-done((f32[10,5,80,128]{3,2,1,0:T(8,128)}, f32[10,5,80,128]{3,2,1,0:T(8,128)S(1)}, u32[]{:S(2)}) %copy-start.6) | copy-done | bytes 2048024
  23.6 1.3 %copy-done.10 = f32[10,5,80,128]{3,2,1,0:T(8,128)} copy-done((f32[10,5,80,128]{3,2,1,0:T(8,128)}, f32[10,5,80,128]{3,2,1,0:T(8,128)S(1)}, u32[]{:S(2)}) %copy-start.10) | copy-done | bytes 2048024
  24.9 1.3 %collective-permute-start.2 = (f32[5,192,128]{2,1,0:T(8,128)S(1)}, f32[5,192,128]{2,1,0:T(8,128)S(1)}, u32[]{:S(2)}, u32[]{:S(2)}) collective-permute-start(f32[5,192,128]{2,1,0:T(8,128)S(1)} %get-tuple-element.47), channel_id=1, source_target_pairs={{0,8},{16,24},{32,40},{48,56},{64,72},{80,88},{96,104},{112,120},{... | collective-permute-start | bytes 1474568 | tf_op jit(solution)/shard_map/ppermute | solution.py:494
  26.3 0.7 collective-permute-start.3
  26.9 7.1 %collective-permute-done.2.refs_7_ = f32[5,192,128]{2,1,0:T(8,128)S(1)} collective-permute-done((f32[5,192,128]{2,1,0:T(8,128)S(1)}, f32[5,192,128]{2,1,0:T(8,128)S(1)}, u32[]{:S(2)}, u32[]{:S(2)}) %collective-permute-start.2) | collective-permute-done | bytes 491552 | tf_op jit(solution)/shard_map/ppermute | solution.py:494
  34.0 0.0 collective-permute-done.3.refs_8_
  34.0 1.6 %copy-done.3 = f32[10,5,80,128]{3,2,1,0:T(8,128)S(1)} copy-done((f32[10,5,80,128]{3,2,1,0:T(8,128)S(1)}, f32[10,5,80,128]{3,2,1,0:T(8,128)}, u32[]{:S(2)}) %copy-start.3) | copy-done | bytes 2048024
  35.6 1.6 %copy-done.7 = f32[10,5,80,128]{3,2,1,0:T(8,128)S(1)} copy-done((f32[10,5,80,128]{3,2,1,0:T(8,128)S(1)}, f32[10,5,80,128]{3,2,1,0:T(8,128)}, u32[]{:S(2)}) %copy-start.7) | copy-done | bytes 2048024
  37.2 1.6 %copy-done.11 = f32[10,5,80,128]{3,2,1,0:T(8,128)S(1)} copy-done((f32[10,5,80,128]{3,2,1,0:T(8,128)S(1)}, f32[10,5,80,128]{3,2,1,0:T(8,128)}, u32[]{:S(2)}) %copy-start.11) | copy-done | bytes 2048024
  38.8 18.3 %first.1 = (f32[10,5,80,128]{3,2,1,0:T(8,128)S(1)}, f32[10,5,80,128]{3,2,1,0:T(8,128)S(1)}, f32[10,5,80,128]{3,2,1,0:T(8,128)S(1)}, f32[10,5,80,128]{3,2,1,0:T(8...) custom-call(s32[1]{0:T(128)} %bitcast.refs_1_.refs_0_, ...), custom_call_target="tpu_custom_call", output_to_operand_aliasing={{0}: (1, {}), {1}: (2, {}), {2}: (3, {}), {3}: (4, {}), {4}... | custom-call | tf_op jit(solution)/shard_map/first/pallas_call | solution.py:528
  57.0 28.2 %all_to_all.22 = f32[128,1,128]{2,1,0:T(1,128)S(1)} all-to-all(f32[128,1,128]{2,1,0:T(1,128)S(1)} %bitcast.12), channel_id=1, replica_groups=mesh['gx_0'=4,'gx_1'=4,'gy_0'=4,'gy_1'=2] {'gx_0','gx_1','gy_0','gy_1'}, dimensions={0} | all-to-all | bytes 131072 | tf_op jit(solution)/shard_map/all_to_all | solution.py:535
  85.2 15.2 %next.1 = (f32[10,5,80,128]{3,2,1,0:T(8,128)S(1)}, f32[10,5,80,128]{3,2,1,0:T(8,128)S(1)}, f32[10,5,80,128]{3,2,1,0:T(8,128)S(1)}, f32[10,4,64,128]{3,2,1,0:T(8,128)S(1)}, f32[128,128]{1,0:T(8,128)S(1)}) custom-call(f32[10,5,80,128]{3,2,1,0:T(8,128)S(1)} %get-tuple-element.49.refs_0_, ...), custom_call_target="tpu_custom_call", output_to_operand_aliasing={{0}: (0, {}), {1}: (7, {}), {2}: (8, {})} | custom-call | tf_op jit(solution)/shard_map/next/pallas_call | solution.py:536
  100.4 13.8 %all_to_all.23 = f32[128,1,128]{2,1,0:T(1,128)S(1)} all-to-all(f32[128,1,128]{2,1,0:T(1,128)S(1)} %bitcast.13), channel_id=1, replica_groups=mesh['gx_0'=4,'gx_1'=4,'gy_0'=4,'gy_1'=2] {'gx_0','gx_1','gy_0','gy_1'}, dimensions={0} | all-to-all | bytes 131072 | tf_op jit(solution)/shard_map/all_to_all | solution.py:542
  114.3 1.8 %last.1 = (f32[10,64,512]{2,1,0:T(8,128)}, f32[10,64,512]{2,1,0:T(8,128)}) custom-call(f32[10,5,80,128]{3,2,1,0:T(8,128)S(1)} %get-tuple-element.59.refs_0_, f32[10,5,80,128]{3,2,1,0:T(8,128)S(1)} %get-tuple-element.60.refs_1_, f32[10,5,80,128]{3,2,1,0:T(8,128)S(1)} %get-tuple-element.61.refs_2_, f32[10,4,64,128]{3,2,1,0:T(8,128)S(1)} %get-tuple-element.62.refs_3_, ...), custom_call_target="tpu_custom_call" | custom-call | tf_op jit(solution)/shard_map/last/pallas_call | solution.py:545
  (7 shorter events, 0.0 us)
Async XLA Ops:
  3.9 1.3 %copy-start = (f32[10,5,80,128]{3,2,1,0:T(8,128)}, f32[10,5,80,128]{3,2,1,0:T(8,128)S(1)}, u32[]{:S(2)}) copy-start(f32[10,5,80,128]{3,2,1,0:T(8,128)S(1)} %get-tuple-element.35.refs_4_) | copy-start | bytes 6144004
  5.2 1.3 %copy-start.4 = (f32[10,5,80,128]{3,2,1,0:T(8,128)}, f32[10,5,80,128]{3,2,1,0:T(8,128)S(1)}, u32[]{:S(2)}) copy-start(f32[10,5,80,128]{3,2,1,0:T(8,128)S(1)} %get-tuple-element.36.refs_5_) | copy-start | bytes 6144004
  6.5 1.3 %copy-start.8 = (f32[10,5,80,128]{3,2,1,0:T(8,128)}, f32[10,5,80,128]{3,2,1,0:T(8,128)S(1)}, u32[]{:S(2)}) copy-start(f32[10,5,80,128]{3,2,1,0:T(8,128)S(1)} %get-tuple-element.34.refs_3_) | copy-start | bytes 6144004
  7.8 4.6 %collective-permute-start = (f32[2,64,128]{2,1,0:T(8,128)S(1)}, f32[2,64,128]{2,1,0:T(8,128)S(1)}, u32[]{:S(2)}, u32[]{:S(2)}) collective-permute-start(f32[2,64,128]{2,1,0:T(8,128)S(1)} %get-tuple-element.39), channel_id=1, source_target_pairs={{0,1},{2,3},{4,5},{6,7},{1,0},{3,2},{5,4},{7,6},{8,9},{10,11},{12,... | collective-permute-start | bytes 196616 | tf_op jit(solution)/shard_map/ppermute | solution.py:494
  9.2 5.6 %collective-permute-start.1 = (f32[2,64,128]{2,1,0:T(8,128)S(1)}, f32[2,64,128]{2,1,0:T(8,128)S(1)}, u32[]{:S(2)}, u32[]{:S(2)}) collective-permute-start(f32[2,64,128]{2,1,0:T(8,128)S(1)} %get-tuple-element.40), channel_id=1, source_target_pairs={{1,2},{3,4},{5,6},{2,1},{4,3},{6,5},{9,10},{11,12},{13,14},{10,9},... | collective-permute-start | bytes 196616 | tf_op jit(solution)/shard_map/ppermute | solution.py:494
  14.8 1.6 %copy-start.1 = (f32[10,5,80,128]{3,2,1,0:T(8,128)S(1)}, f32[10,5,80,128]{3,2,1,0:T(8,128)}, u32[]{:S(2)}) copy-start(f32[10,5,80,128]{3,2,1,0:T(8,128)} %copy-done) | copy-start | bytes 6144004
  16.4 1.6 %copy-start.5 = (f32[10,5,80,128]{3,2,1,0:T(8,128)S(1)}, f32[10,5,80,128]{3,2,1,0:T(8,128)}, u32[]{:S(2)}) copy-start(f32[10,5,80,128]{3,2,1,0:T(8,128)} %copy-done.4) | copy-start | bytes 6144004
  17.9 1.6 %copy-start.9 = (f32[10,5,80,128]{3,2,1,0:T(8,128)S(1)}, f32[10,5,80,128]{3,2,1,0:T(8,128)}, u32[]{:S(2)}) copy-start(f32[10,5,80,128]{3,2,1,0:T(8,128)} %copy-done.8) | copy-start | bytes 6144004
  21.0 1.3 %copy-start.2 = (f32[10,5,80,128]{3,2,1,0:T(8,128)}, f32[10,5,80,128]{3,2,1,0:T(8,128)S(1)}, u32[]{:S(2)}) copy-start(f32[10,5,80,128]{3,2,1,0:T(8,128)S(1)} %get-tuple-element.43.refs_3_) | copy-start | bytes 6144004
  22.3 1.3 %copy-start.6 = (f32[10,5,80,128]{3,2,1,0:T(8,128)}, f32[10,5,80,128]{3,2,1,0:T(8,128)S(1)}, u32[]{:S(2)}) copy-start(f32[10,5,80,128]{3,2,1,0:T(8,128)S(1)} %get-tuple-element.44.refs_4_) | copy-start | bytes 6144004
  23.6 1.3 %copy-start.10 = (f32[10,5,80,128]{3,2,1,0:T(8,128)}, f32[10,5,80,128]{3,2,1,0:T(8,128)S(1)}, u32[]{:S(2)}) copy-start(f32[10,5,80,128]{3,2,1,0:T(8,128)S(1)} %get-tuple-element.42.refs_2_) | copy-start | bytes 6144004
  24.9 9.1 %collective-permute-start.2 = (f32[5,192,128]{2,1,0:T(8,128)S(1)}, f32[5,192,128]{2,1,0:T(8,128)S(1)}, u32[]{:S(2)}, u32[]{:S(2)}) collective-permute-start(f32[5,192,128]{2,1,0:T(8,128)S(1)} %get-tuple-element.47), channel_id=1, source_target_pairs={{0,8},{16,24},{32,40},{48,56},{64,72},{80,88},{96,104},{112,120},{... | collective-permute-start | bytes 1474568 | tf_op jit(solution)/shard_map/ppermute | solution.py:494
  26.3 7.8 %collective-permute-start.3 = (f32[5,192,128]{2,1,0:T(8,128)S(1)}, f32[5,192,128]{2,1,0:T(8,128)S(1)}, u32[]{:S(2)}, u32[]{:S(2)}) collective-permute-start(f32[5,192,128]{2,1,0:T(8,128)S(1)} %get-tuple-element.48), channel_id=1, source_target_pairs={{8,16},{24,32},{40,48},{56,64},{72,80},{88,96},{104,112},{16,8},{3... | collective-permute-start | bytes 1474568 | tf_op jit(solution)/shard_map/ppermute | solution.py:494
  34.0 1.6 %copy-start.3 = (f32[10,5,80,128]{3,2,1,0:T(8,128)S(1)}, f32[10,5,80,128]{3,2,1,0:T(8,128)}, u32[]{:S(2)}) copy-start(f32[10,5,80,128]{3,2,1,0:T(8,128)} %copy-done.2) | copy-start | bytes 6144004
  35.6 1.6 %copy-start.7 = (f32[10,5,80,128]{3,2,1,0:T(8,128)S(1)}, f32[10,5,80,128]{3,2,1,0:T(8,128)}, u32[]{:S(2)}) copy-start(f32[10,5,80,128]{3,2,1,0:T(8,128)} %copy-done.6) | copy-start | bytes 6144004
  37.2 1.6 %copy-start.11 = (f32[10,5,80,128]{3,2,1,0:T(8,128)S(1)}, f32[10,5,80,128]{3,2,1,0:T(8,128)}, u32[]{:S(2)}) copy-start(f32[10,5,80,128]{3,2,1,0:T(8,128)} %copy-done.10) | copy-start | bytes 6144004

commit v2 on v1

v2 whole, which is shorter than its diff:
```python
import jax
import jax.numpy as jnp
from jax import lax
from jax.experimental import pallas as pl
from jax.experimental.pallas import tpu as pltpu
from jax.sharding import Mesh
from jax.sharding import PartitionSpec as P

GX = ("gx_0", "gx_1")
GY = ("gy_0", "gy_1")
ALL = GX + GY

EPS = 1e-06
NT = 5
ROWS = 80
TOP = 8
SPAN = 416
F32 = jnp.float32


def lanes():
    return lax.broadcasted_iota(jnp.int32, (8, 128), 1)


def from_north(tiles):
    lane = lanes()
    turned = [pltpu.roll(tile, 127, 1) for tile in tiles]
    count = len(tiles)
    return [jnp.where(lane == 127, turned[(t + 1) % count], turned[t]) for t in range(count)]


def from_south(tiles):
    lane = lanes()
    turned = [pltpu.roll(tile, 1, 1) for tile in tiles]
    count = len(tiles)
    return [jnp.where(lane == 0, turned[(t - 1) % count], turned[t]) for t in range(count)]


def at(t, start, size=8):
    return pl.ds(ROWS * t + start, size)


def tile_of(ref, layer, t, start):
    return ref[layer, at(t, start), :]


def tiles_of(ref, layer, start):
    return [tile_of(ref, layer, t, start) for t in range(NT)]


def flat_tiles(ref, start):
    return [ref[at(t, start), :] for t in range(NT)]


UNITS = 25


def strip_units(layers):
    return [(f, layer) for f in range(4) for layer in range(layers)] + [(4, None), (5, None)]


def edge_kernel(layers, par, p_in, k_in, o_in, r_in, act_in, rech_in, send_a, send_b, edges, act_edges, rech_edges, sems):
    copies = []
    for side, first in ((0, 0), (1, 384)):
        cols = pl.ds(first, 128)
        for f, src in enumerate((p_in, k_in, o_in, r_in)):
            copies.append(pltpu.make_async_copy(src.at[:, :, cols], edges.at[f, side], sems.at[side * 6 + f]))
        copies.append(pltpu.make_async_copy(act_in.at[:, cols], act_edges.at[side], sems.at[side * 6 + 4]))
        copies.append(pltpu.make_async_copy(rech_in.at[:, cols], rech_edges.at[side], sems.at[side * 6 + 5]))
    for copy in copies:
        copy.start()
    for copy in copies:
        copy.wait()
    first = lanes() < 5
    last = lanes() >= 123
    odd = par[0] == 1
    zero = jnp.zeros((8, 128), F32)

    def pack(row, carry):
        rows = pl.ds(pl.multiple_of(8 * row, 8), 8)
        low = [zero, zero]
        high = [zero, zero]
        for u, (f, layer) in enumerate(strip_units(layers)):
            place = 5 * (u % UNITS)
            here = u // UNITS
            if f == 4:
                a, b = act_edges[0, rows, :].astype(F32), act_edges[1, rows, :].astype(F32)
            elif f == 5:
                a, b = rech_edges[0, rows, :], rech_edges[1, rows, :]
            else:
                a, b = edges[f, 0, layer, rows, :], edges[f, 1, layer, rows, :]
            a = jnp.where(first, a, 0.0)
            b = jnp.where(last, b, 0.0)
            low[here] = low[here] + (pltpu.roll(a, place, 1) if place else a)
            high[here] = high[here] + pltpu.roll(b, (place + 5) % 128, 1)
        for here in range(2):
            send_a[here, rows, :] = jnp.where(odd, low[here], high[here])
            send_b[here, rows, :] = jnp.where(odd, high[here], low[here])
        return carry

    lax.fori_loop(0, 8, pack, 0)


def unpack_strips(layers, odd, got_a, got_b, rows, put):
    left_edge = lanes() >= 123
    right_edge = lanes() < 5
    a = [got_a[here, rows, :] for here in range(2)]
    b = [got_b[here, rows, :] for here in range(2)]
    below = [jnp.where(odd, a[h], b[h]) for h in range(2)]
    above = [jnp.where(odd, b[h], a[h]) for h in range(2)]
    for u, (f, layer) in enumerate(strip_units(layers)):
        place = 5 * (u % UNITS)
        here = u // UNITS
        left = pltpu.roll(below[here], (123 - place) % 128, 1)
        right = pltpu.roll(above[here], 128 - place, 1) if place else above[here]
        put(f, layer, jnp.where(left_edge, left, jnp.where(right_edge, right, 0.0)))


STRIP_ROWS = ((0, 5), (5, 5), (10, 4), (14, 4))


def turn_kernel(layers, par_y, par_x, p_in, k_in, o_in, r_in, act_in, rech_in, got_a, got_b,
                send_a, send_b, edges, act_edges, rech_edges, act_int, sems):
    copies = []
    for side, first in ((0, 0), (1, 56)):
        rows = pl.ds(first, 8)
        for t in range(4):
            cols = pl.ds(128 * t, 128)
            for f, src in enumerate((p_in, k_in, o_in, r_in)):
                copies.append(pltpu.make_async_copy(
                    src.at[:, rows, cols], edges.at[f, side, :, t], sems.at[side, t, f]))
            copies.append(pltpu.make_async_copy(act_in.at[rows, cols], act_int.at[side, t], sems.at[side, t, 4]))
            copies.append(pltpu.make_async_copy(rech_in.at[rows, cols], rech_edges.at[side, t], sems.at[side, t, 5]))
    for copy in copies:
        copy.start()
    odd = par_y[0] == 1
    for side in range(2):
        def put(f, layer, value):
            if f == 4:
                act_edges[side, 4] = value
            elif f == 5:
                rech_edges[side, 4] = value
            else:
                edges[f, side, layer, 4] = value

        unpack_strips(layers, odd, got_a, got_b, pl.ds(56 * side, 8), put)
    for copy in copies:
        copy.wait()
    for side in range(2):
        for t in range(4):
            act_edges[side, t] = act_int[side, t].astype(F32)
    for send, side in ((send_a, 1 - par_x[0]), (send_b, par_x[0])):
        start5 = 3 * side
        start4 = 4 * side

        def fill(layer, carry):
            for f, (place, depth) in enumerate(STRIP_ROWS):
                start = start5 if depth == 5 else start4
                for t in range(NT):
                    send[t, pl.ds(layer * 18 + place, depth), :] = edges[f, side, layer, t, pl.ds(start, depth), :]
            return carry

        lax.fori_loop(0, layers, fill, 0)
        for t in range(NT):
            send[t, 18 * layers:18 * layers + 5, :] = act_edges[side, t, pl.ds(start5, 5), :]
            send[t, 18 * layers + 5:18 * layers + 9, :] = rech_edges[side, t, pl.ds(start4, 4), :]


def place_strips(layers, up, refs, got_a, got_b):
    p_ref, k_ref, o_ref, r_ref, rech_ref, act_ref = refs
    fields = (p_ref, k_ref, o_ref, r_ref)
    low, high = TOP, TOP + 64
    for got, above in ((got_a, jnp.logical_not(up)), (got_b, up)):
        dst5 = jnp.where(above, high, low - 5)
        dst4 = jnp.where(above, high, low - 4)

        def fill(layer, carry):
            for (place, depth), ref in zip(STRIP_ROWS, fields):
                start = dst5 if depth == 5 else dst4
                for t in range(NT):
                    ref[layer, at(t, start, depth), :] = got[t, pl.ds(layer * 18 + place, depth), :]
            return carry

        lax.fori_loop(0, layers, fill, 0)
        for t in range(NT):
            act_ref[at(t, dst5, 5), :] = got[t, 18 * layers:18 * layers + 5, :]
            rech_ref[at(t, dst4, 4), :] = got[t, 18 * layers + 5:18 * layers + 9, :]


def sigmoid_tile(value, layer, t, start, sig_ref, mob_ref, der_ref):
    sig = jax.nn.sigmoid(value)
    square = sig * sig
    sig_ref[layer, at(t, start), :] = sig
    mob_ref[layer, at(t, start), :] = 0.5 * square
    der_ref[layer, at(t, start), :] = square - square * sig


def face(trans, p_a, p_b, m_a, m_b, s_a, s_b, gravity):
    drop = p_a - p_b
    if gravity:
        drop = drop + gravity
    by_mob = trans * (m_a + m_b)
    by_drop = trans * drop
    return by_mob + s_a * by_drop, s_b * by_drop - by_mob, by_mob * drop


def far_faces(layers, starts, s, make_trans):
    def one_layer(layer, carry):
        upper = jnp.minimum(layer + 1, layers - 1)
        inner = jnp.where(layer + 1 < layers, 1.0, 0.0).astype(F32)
        for start in starts:
            for t in range(NT):
                here = at(t, start)
                if make_trans:
                    trans = s.ax[here, :] * (tile_of(s.k, layer, t, start) + tile_of(s.k, layer, t, start + 1))
                    s.tx[layer, here, :] = trans
                else:
                    trans = tile_of(s.tx, layer, t, start)
                p = tile_of(s.p, layer, t, start)
                m = tile_of(s.m, layer, t, start)
                der = tile_of(s.s, layer, t, start)
                ca, cb, flow = face(
                    trans, p, tile_of(s.p, layer, t, start + 1), m, tile_of(s.m, layer, t, start + 1),
                    der, tile_of(s.s, layer, t, start + 1), 0.0)
                s.xa[layer, here, :] = ca
                s.xb[layer, here, :] = cb
                s.xf[layer, here, :] = flow
                if make_trans:
                    trans = (s.act[here, :] * inner) * (
                        tile_of(s.k, layer, t, start) + tile_of(s.k, upper, t, start))
                    s.tz[layer, here, :] = trans
                else:
                    trans = tile_of(s.tz, layer, t, start)
                za, zb, zf = face(
                    trans, p, tile_of(s.p, upper, t, start), m, tile_of(s.m, upper, t, start),
                    der, tile_of(s.s, upper, t, start), -1.0)
                s.za[layer + 1, here, :] = za
                s.zb[layer + 1, here, :] = zb
                s.zf[layer + 1, here, :] = zf
        return carry

    lax.fori_loop(0, layers, one_layer, 0)


def assemble(layers, starts, s, make_trans):
    def one_layer(layer, carry):
        for start in starts:
            p = tiles_of(s.p, layer, start)
            m = tiles_of(s.m, layer, start)
            der = tiles_of(s.s, layer, start)
            if make_trans:
                k = tiles_of(s.k, layer, start)
                k_north = from_north(k)
                ty = [s.ay[at(t, start), :] * (k[t] + k_north[t]) for t in range(NT)]
                for t in range(NT):
                    s.ty[layer, at(t, start), :] = ty[t]
            else:
                ty = tiles_of(s.ty, layer, start)
            p_north, m_north, s_north = from_north(p), from_north(m), from_north(der)
            across_y = [face(ty[t], p[t], p_north[t], m[t], m_north[t], der[t], s_north[t], 0.0) for t in range(NT)]
            ya = from_south([f[0] for f in across_y])
            yb = from_south([f[1] for f in across_y])
            yf = from_south([f[2] for f in across_y])
            for t in range(NT):
                here = at(t, start)
                s.ya[layer, here, :] = ya[t]
                s.yb[layer, here, :] = across_y[t][1]
                sig = tile_of(s.sig, layer, t, start)
                ap = tile_of(s.ap, layer, t, start)
                ocean = 1.0 - s.act[here, :]
                stored = ap * sig
                center = (stored - stored * sig) + ocean
                center = center + (tile_of(s.xa, layer, t, start) - tile_of(s.xb, layer, t, start - 1))
                center = center + (across_y[t][0] - yb[t]) + (tile_of(s.za, layer + 1, t, start) - tile_of(s.zb, layer, t, start))
                s.c[layer, here, :] = center
                flows = (tile_of(s.xf, layer, t, start) - tile_of(s.xf, layer, t, start - 1))
                flows = flows + (across_y[t][2] - yf[t]) + (tile_of(s.zf, layer + 1, t, start) - tile_of(s.zf, layer, t, start))
                s.q[layer, here, :] = (tile_of(s.s0, layer, t, start) - stored) - ocean * p[t] - flows
        return carry

    lax.fori_loop(0, layers, one_layer, 0)


def product_tile(layers, s, v_ref, layer, start, count):
    v = tiles_of(v_ref, layer, start)
    north, south = from_north(v), from_south(v)
    upper = jnp.minimum(layer + 1, layers - 1)
    lower = jnp.maximum(layer - 1, 0)
    out = []
    for t in range(count):
        value = tile_of(s.c, layer, t, start) * v[t]
        value = value + (tile_of(s.xb, layer, t, start) * tile_of(v_ref, layer, t, start + 1)
                         - tile_of(s.xa, layer, t, start - 1) * tile_of(v_ref, layer, t, start - 1))
        value = value + (tile_of(s.yb, layer, t, start) * north[t] - tile_of(s.ya, layer, t, start) * south[t])
        value = value + (tile_of(s.zb, layer + 1, t, start) * tile_of(v_ref, upper, t, start)
                         - tile_of(s.za, layer, t, start) * tile_of(v_ref, lower, t, start))
        out.append(value)
    return v, out


def first_product(layers, starts, s):
    def one_layer(layer, carry):
        for start in starts:
            _, out = product_tile(layers, s, s.q, layer, start, NT)
            for t in range(NT):
                s.w[layer, at(t, start), :] = out[t]
        return carry

    lax.fori_loop(0, layers, one_layer, 0)


def second_product(layers, starts, s, sums, z_ref):
    def one_layer(layer, sums):
        sums = list(sums)
        for start in starts:
            w, z = product_tile(layers, s, s.w, layer, start, NT - 1)
            for t in range(NT - 1):
                q = tile_of(s.q, layer, t, start)
                if z_ref is not None:
                    z_ref[layer, pl.ds(64 * t + start - TOP, 8), :] = z[t]
                for i, (a, b) in enumerate(((q, q), (q, w[t]), (q, z[t]), (w[t], w[t]), (w[t], z[t]), (z[t], z[t]))):
                    sums[i] = sums[i] + a * b
        return tuple(sums)

    return lax.fori_loop(0, layers, one_layer, sums)


def put_sums(sums, out_ref):
    lane = lax.broadcasted_iota(jnp.int32, (1, 128), 1)
    row = jnp.zeros((1, 128), F32)
    for i, part in enumerate(sums):
        total = jnp.sum(jnp.sum(part, axis=0, keepdims=True), axis=1, keepdims=True)
        row = row + jnp.where(lane == i, total, 0.0)
    out_ref[...] = jnp.broadcast_to(row, out_ref.shape)


def step_weights(sums_ref):
    total = jnp.sum(sums_ref[...], axis=0, keepdims=True)
    lane = lax.broadcasted_iota(jnp.int32, (1, 128), 1)
    qq, qw, qz, ww, wz, zz = (
        jnp.sum(jnp.where(lane == i, total, 0.0), axis=1, keepdims=True) for i in range(6))
    first = qq + EPS
    qq, qw, qz, ww, wz, zz = (entry / first for entry in (qq, qw, qz, ww, wz, zz))
    norm = jnp.sqrt(first)
    h11 = qw
    left = jnp.maximum(ww - 2.0 * h11 * qw + h11 * h11 * qq, 0.0)
    square = left + EPS
    h21 = jnp.sqrt(square)
    h12 = (qz - h11 * qw) / h21
    h22 = (wz - h11 * qz - h11 * (ww - h11 * qw)) / square
    length = (zz - 2.0 * h11 * wz + h11 * h11 * ww) / square
    cross = (qw - h11 * qq) / h21
    rest = (length - 2.0 * (h12 * h12 + h22 * h22) + h12 * h12 * qq + h22 * h22 * (left / square)
            + 2.0 * h12 * h22 * cross)
    third = jnp.maximum(rest, 0.0) + EPS
    radius = jnp.sqrt(h11 * h11 + square)
    cosine = h11 / radius
    sine = h21 / radius
    top = cosine * h12 + sine * h22
    lower = cosine * h22 - sine * h12
    y2 = -lower * sine * norm / (lower * lower + third)
    y1 = (cosine * norm - top * y2) / radius
    b = y2 / (norm * h21)
    a = y1 / norm - b * h11
    return jnp.broadcast_to(a, (8, 128)), jnp.broadcast_to(b, (8, 128))


class Refs:
    def __init__(self, **refs):
        self.__dict__.update(refs)


STATE = ("p", "k", "s0", "ap", "tx", "ty", "tz", "q", "w")
COEFS = ("c", "xa", "xb", "ya", "yb", "za", "zb", "xf", "zf")
POINT = ("sig", "m", "s")
TALL = ("za", "zb", "zf")


def space(layers, name):
    return pltpu.VMEM((layers + (name in TALL), SPAN, 128), F32)


def clear_bottom(s):
    zero = jnp.zeros((8, 128), F32)

    def clear(i, carry):
        for ref in (s.za, s.zb, s.zf):
            ref[0, pl.ds(pl.multiple_of(8 * i, 8), 8), :] = zero
        return carry

    lax.fori_loop(0, SPAN // 8, clear, 0)


def mask_pairs(s, starts):
    for start in starts:
        act = flat_tiles(s.act, start)
        north = from_north(act)
        for t in range(NT):
            s.ax[at(t, start), :] = 0.5 * act[t] * s.act[at(t, start + 1), :]
            s.ay[at(t, start), :] = 0.5 * act[t] * north[t]


def points(layers, s, new, old):
    def point(layer, carry):
        top = jnp.where(layer == layers - 1, 1.0, 0.0).astype(F32)
        for start in (*new, *old):
            for t in range(NT):
                sigmoid_tile(tile_of(s.p, layer, t, start), layer, t, start, s.sig, s.m, s.s)
                if start in new:
                    act = s.act[at(t, start), :]
                    ap = (0.9 * act) * tile_of(s.ap, layer, t, start)
                    s.ap[layer, at(t, start), :] = ap
                    s.s0[layer, at(t, start), :] = (
                        ap * jax.nn.sigmoid(tile_of(s.s0, layer, t, start)) + (top * act) * s.rech[at(t, start), :])
        return carry

    lax.fori_loop(0, layers, point, 0)


def inner_kernel(layers, par_y, p_in, k_in, o_in, r_in, act_in, rech_in, got_a, got_b, after, *refs):
    names = STATE + COEFS + ("act", "rech", "ax", "ay")
    s = Refs(**dict(zip(names, refs)))
    part_ref = refs[len(names)]
    s.sig, s.m, s.s, act_int, sems = refs[len(names) + 1:]
    copies = []
    for t in range(4):
        cols = pl.ds(128 * t, 128)
        for f, (src, dst) in enumerate(((p_in, s.p), (k_in, s.k), (o_in, s.s0), (r_in, s.ap))):
            copies.append(pltpu.make_async_copy(src.at[:, :, cols], dst.at[:, at(t, TOP, 64), :], sems.at[t, f]))
        copies.append(pltpu.make_async_copy(act_in.at[:, cols], act_int.at[t], sems.at[t, 4]))
        copies.append(pltpu.make_async_copy(rech_in.at[:, cols], s.rech.at[at(t, TOP, 64), :], sems.at[t, 5]))
    for copy in copies:
        copy.start()
    zero = jnp.zeros((8, 128), F32)
    fields = (s.p, s.k, s.s0, s.ap)

    def clear(layer, carry):
        for ref in fields:
            for t in range(NT):
                ref[layer, at(t, 0), :] = zero
                ref[layer, at(t, ROWS - 8), :] = zero
        return carry

    lax.fori_loop(0, layers, clear, 0)
    for ref in (s.act, s.rech):
        for t in range(NT):
            ref[at(t, 0), :] = zero
            ref[at(t, ROWS - 8), :] = zero
    clear_bottom(s)
    odd = par_y[0] == 1

    def unpack(row, carry):
        start = pl.multiple_of(TOP + 8 * row, 8)

        def put(f, layer, value):
            if f == 4:
                s.act[at(4, start), :] = value
            elif f == 5:
                s.rech[at(4, start), :] = value
            else:
                fields[f][layer, at(4, start), :] = value

        unpack_strips(layers, odd, got_a, got_b, pl.ds(pl.multiple_of(8 * row, 8), 8), put)
        return carry

    lax.fori_loop(0, 8, unpack, 0)
    for copy in copies:
        copy.wait()
    for t in range(4):
        s.act[at(t, TOP, 64), :] = act_int[t].astype(F32)
    points(layers, s, range(8, 72, 8), ())
    mask_pairs(s, (*range(8, 64, 8), 63))
    far_faces(layers, (*range(8, 64, 8), 63), s, True)
    assemble(layers, range(12, 68, 8), s, True)
    first_product(layers, range(20, 60, 8), s)
    sums = second_product(layers, range(24, 56, 8), s, (zero,) * 6, None)
    for i in range(6):
        part_ref[i] = sums[i]


def first_kernel(layers, par_x, *refs):
    names = STATE + COEFS + ("act", "rech", "ax", "ay")
    count = len(names)
    part_ref, got_a, got_b = refs[count:count + 3]
    refs = refs[count + 3:]
    s = Refs(**dict(zip(names, refs)))
    sums_ref = refs[count]
    s.sig, s.m, s.s = refs[count + 1:]
    place_strips(layers, par_x[0] == 1, (s.p, s.k, s.s0, s.ap, s.rech, s.act), got_a, got_b)
    points(layers, s, (0, 72), (8, 64))
    mask_pairs(s, (0, 4, 64, 68))
    far_faces(layers, (0, 64, 68), s, True)
    assemble(layers, (4, 68), s, True)
    first_product(layers, (4, 12, 60, 68), s)
    sums = second_product(layers, (8, 16, 56, 64), s, tuple(part_ref[i] for i in range(6)), None)
    put_sums(sums, sums_ref)


KEPT = ("s0", "ap", "tx", "ty", "tz", "act")
SHARED = 4
MOVED = ("p", "q", "w") + COEFS[:SHARED]


def next_kernel(layers, *refs):
    kept, refs = refs[:len(KEPT)], refs[len(KEPT) + len(MOVED):]
    got_ref, *refs = refs
    s = Refs(**dict(zip(KEPT, kept)), **dict(zip(MOVED, refs)))
    z_ref, sums_ref, *own = refs[len(MOVED):]
    for name, ref in zip(COEFS[SHARED:] + POINT, own):
        setattr(s, name, ref)
    p_ref, q_ref, w_ref = s.p, s.q, s.w
    a, b = step_weights(got_ref)
    if SHARED < len(COEFS):
        clear_bottom(s)

    def point(layer, carry):
        for start in range(4, 76, 8):
            for t in range(NT):
                p = tile_of(p_ref, layer, t, start) + (
                    a * tile_of(q_ref, layer, t, start) + b * tile_of(w_ref, layer, t, start))
                p_ref[layer, at(t, start), :] = p
                sigmoid_tile(p, layer, t, start, s.sig, s.m, s.s)
        return carry

    lax.fori_loop(0, layers, point, 0)
    starts = range(4, 76, 8)
    far_faces(layers, (0, *starts), s, False)
    assemble(layers, starts, s, False)
    first_product(layers, starts, s)
    sums = tuple(jnp.zeros((8, 128), F32) for _ in range(6))
    sums = second_product(layers, range(TOP, TOP + 64, 8), s, sums, z_ref)
    put_sums(sums, sums_ref)


def last_kernel(layers, p_ref, q_ref, w_ref, z_ref, got_ref, final_out, left_out, final_buf, left_buf, sems):
    a, b = step_weights(got_ref)
    for layer in range(layers):
        for start in range(0, 64, 8):
            for t in range(NT - 1):
                q = tile_of(q_ref, layer, t, TOP + start)
                w = tile_of(w_ref, layer, t, TOP + start)
                place = (layer, slice(start, start + 8), slice(128 * t, 128 * t + 128))
                final_buf[place] = tile_of(p_ref, layer, t, TOP + start) + (a * q + b * w)
                left_buf[place] = (q - a * w) - b * z_ref[layer, pl.ds(64 * t + start, 8), :]
        pltpu.make_async_copy(final_buf.at[layer], final_out.at[layer], sems.at[layer, 0]).start()
        pltpu.make_async_copy(left_buf.at[layer], left_out.at[layer], sems.at[layer, 1]).start()
    for layer in range(layers):
        pltpu.make_async_copy(final_buf.at[layer], final_out.at[layer], sems.at[layer, 0]).wait()
        pltpu.make_async_copy(left_buf.at[layer], left_out.at[layer], sems.at[layer, 1]).wait()


VM = pl.BlockSpec(memory_space=pltpu.VMEM)
HB = pl.BlockSpec(memory_space=pl.ANY)
SM = pl.BlockSpec(memory_space=pltpu.SMEM)


def grant(mib):
    return pltpu.CompilerParams(vmem_limit_bytes=mib * 1024 * 1024)


def keep(*arrays):
    return [pltpu.with_memory_space_constraint(array, pltpu.VMEM) for array in arrays]


def outside(*arrays):
    return [pltpu.with_memory_space_constraint(array, pltpu.HBM) for array in arrays]


def swap(value, axes, first):
    size = lax.axis_size(axes)
    pairs = [(i, i + 1) for i in range(first, size - 1, 2)]
    return lax.ppermute(value, axes, pairs + [(b, a) for a, b in pairs])


def bound(kernel, *args):
    def call(*refs):
        kernel(*args, *refs)

    return call


def body(pressure, pressure_old, conductivity, porosity, recharge, active):
    layers = pressure.shape[0]
    par_x = (lax.axis_index(GX) % 2).astype(jnp.int32).reshape(1)
    par_y = (lax.axis_index(GY) % 2).astype(jnp.int32).reshape(1)
    inputs = outside(pressure, conductivity, pressure_old, porosity, active, recharge)
    dma = pltpu.SemaphoreType.DMA
    strip_y = pltpu.VMEM((2, 64, 128), F32)
    strip_x = pltpu.VMEM((NT, 192, 128), F32)
    plane = pltpu.VMEM((SPAN, 128), F32)
    part = pltpu.VMEM((6, 8, 128), F32)
    block = jax.ShapeDtypeStruct((128, 128), F32)
    send_a, send_b = pl.pallas_call(
        bound(edge_kernel, layers), name="edge", out_shape=(strip_y,) * 2, in_specs=[SM] + [HB] * 6, out_specs=(VM,) * 2,
        scratch_shapes=[pltpu.VMEM((4, 2, layers, 64, 128), F32), pltpu.VMEM((2, 64, 128), jnp.int32),
                        pltpu.VMEM((2, 64, 128), F32), dma((12,))],
        compiler_params=grant(GRANT),
    )(par_y, *inputs)
    y_a = swap(send_a, GY, 0)
    y_b = swap(send_b, GY, 1)
    send_a, send_b = pl.pallas_call(
        bound(turn_kernel, layers), name="turn", out_shape=(strip_x,) * 2, in_specs=[SM] * 2 + [HB] * 6 + [VM] * 2,
        out_specs=(VM,) * 2,
        scratch_shapes=[pltpu.VMEM((4, 2, layers, NT, 8, 128), F32), pltpu.VMEM((2, NT, 8, 128), F32),
                        pltpu.VMEM((2, NT, 8, 128), F32), pltpu.VMEM((2, 4, 8, 128), jnp.int32), dma((2, 4, 6))],
        compiler_params=grant(GRANT),
    )(par_y, par_x, *inputs, y_a, y_b)
    x_a = swap(send_a, GX, 0)
    x_b = swap(send_b, GX, 1)
    state = tuple(space(layers, name) for name in STATE + COEFS) + (plane,) * 4
    points_scratch = [space(layers, name) for name in POINT]
    *fields, part_sums = pl.pallas_call(
        bound(inner_kernel, layers), name="inner", out_shape=state + (part,),
        in_specs=[SM] + [HB] * 6 + [VM] * 3, out_specs=(VM,) * (len(state) + 1),
        scratch_shapes=points_scratch + [pltpu.VMEM((4, 64, 128), jnp.int32), dma((4, 6))],
        compiler_params=grant(GRANT),
        cost_estimate=pl.CostEstimate(flops=100_000_000, transcendentals=0, bytes_accessed=6_000_000),
    )(par_y, *inputs, y_a, y_b, send_a)
    *fields, sums = pl.pallas_call(
        bound(first_kernel, layers), name="first", out_shape=state + (block,),
        in_specs=[SM] + [VM] * (len(state) + 3), out_specs=(VM,) * (len(state) + 1),
        input_output_aliases={i + 1: i for i in range(len(state))},
        scratch_shapes=points_scratch, compiler_params=grant(GRANT),
    )(par_x, *keep(*fields, part_sums), x_a, x_b)
    sums = lax.all_to_all(sums, ALL, 0, 0, tiled=True)
    named = dict(zip(STATE + COEFS + ("act", "rech", "ax", "ay"), fields))
    moved = tuple(space(layers, name) for name in MOVED)
    p, q, w, *rest = pl.pallas_call(
        bound(next_kernel, layers), name="next",
        out_shape=moved + (pltpu.VMEM((layers, 256, 128), F32), block),
        in_specs=[VM] * (len(KEPT) + len(MOVED) + 1), out_specs=(VM,) * (len(MOVED) + 2),
        input_output_aliases={len(KEPT) + i: i for i in range(len(MOVED))},
        scratch_shapes=[space(layers, name) for name in COEFS[SHARED:] + POINT], compiler_params=grant(GRANT2),
    )(*keep(*(named[n] for n in KEPT + MOVED)), sums)
    z, sums = rest[-2:]
    sums = lax.all_to_all(sums, ALL, 0, 0, tiled=True)
    out = jax.ShapeDtypeStruct(pressure.shape, F32)
    buffer = pltpu.VMEM(pressure.shape, F32)
    return pl.pallas_call(
        bound(last_kernel, layers), name="last", out_shape=(out, out), in_specs=[VM] * 5, out_specs=(HB, HB),
        scratch_shapes=[buffer, buffer, dma((layers, 2))], compiler_params=grant(GRANT),
    )(*keep(p, q, w, z), sums)


GRANT = 10
GRANT2 = 20


def solution(mesh):
    torus = Mesh(mesh.devices.reshape(4, 4, 4, 2), ALL)
    field = P(None, GX, GY)
    plane = P(GX, GY)
    return jax.shard_map(
        body, mesh=torus, in_specs=(field,) * 4 + (plane,) * 2, out_specs=(field, field), check_vma=False)
```

time: 116 us -> 88.6 us (0.76)
  local copies, waits for them, and re-layouts: 17.3 us -> 0 us
  blocking collectives: 42 us -> 33.5 us
  waiting for transfers between devices: 9.44 us -> 2.33 us
  starting transfers between devices: 6.58 us -> 9.2 us
  Pallas kernels: 40 us -> 42.6 us
    unnamed x24 -> x0, local copies, waits for them, and re-layouts: 17.3 us -> none
    pallas_call x3 -> x4, Pallas kernels: 19.9 us -> 34.6 us  [the longest x1 14.7 us: body(): pl.pallas_call(bound(next_kernel, layers), name='next', out_shape=moved +...]
    pallas_call x1, Pallas kernels: 18.3 us -> 6.16 us  [body(): pl.pallas_call(bound(first_kernel, layers), name='first', out_shape=state...]
    all_to_all x2, blocking collectives: 42 us -> 33.5 us  [body(): sums = lax.all_to_all(sums, ALL, 0, 0, tiled=True)]
    ppermute x4, waiting for transfers between devices: 9.44 us -> 2.33 us  [swap(): return lax.ppermute(value, axes, pairs + [(b, a) for a, b in pairs])]
    ppermute x4, starting transfers between devices: 6.58 us -> 9.2 us  [swap(): return lax.ppermute(value, axes, pairs + [(b, a) for a, b in pairs])]
  transfers between devices with their start and end apart: 4 -> 4, of which waited for: 2 -> 1; matrix products, arithmetic and copies ran while one was open for 0% -> 0% of each run, Pallas kernels for 0% -> 17%
where the time goes in v2:
time: 88.6 us; the launch traced here: 88.3 us
  Pallas kernels  42.6 us (48%)
  blocking collectives  33.5 us (38%)
  starting transfers between devices  9.2 us (10%)
  waiting for transfers between devices  2.33 us (3%)
    all_to_all x2, blocking collectives, body(): sums = lax.all_to_all(sums, ALL, 0, 0, tiled=True)  33.5 us
    pallas_call x1, Pallas kernels, body(): pl.pallas_call(bound(next_kernel, layers), name='next', out_shape=moved +...  14.7 us
    pallas_call x1, Pallas kernels, body(): pl.pallas_call(bound(inner_kernel, layers), name='inner', out_shape=state...  14.7 us
    ppermute x4, starting transfers between devices, swap(): return lax.ppermute(value, axes, pairs + [(b, a) for a, b in pairs])  9.2 us
    pallas_call x1, Pallas kernels, body(): pl.pallas_call(bound(first_kernel, layers), name='first', out_shape=state...  6.16 us
    pallas_call x1, Pallas kernels, body(): pl.pallas_call(bound(edge_kernel, layers), name='edge', out_shape=(strip_...  3.09 us
    ppermute x4, waiting for transfers between devices, swap(): return lax.ppermute(value, axes, pairs + [(b, a) for a, b in pairs])  2.33 us
    pallas_call x1, Pallas kernels, body(): pl.pallas_call(bound(turn_kernel, layers), name='turn', out_shape=(strip_...  2.1 us
  transfers between devices with their start and end apart: 4, of which 1 were waited for; matrix products, arithmetic and copies ran while one was open for 0% of the time, Pallas kernels for 17%

profile of v2, /device:TPU:1, one launch (start us, length us, event | category | flops | bytes accessed | tf_op | source)
XLA Modules:
  0.0 88.3 jit_solution(14547364367079627803)
XLA Ops:
  0.6 3.1 %edge.1 = (f32[2,64,128]{2,1,0:T(8,128)S(1)}, f32[2,64,128]{2,1,0:T(8,128)S(1)}) custom-call(s32[1]{0:T(128)} %bitcast.1.refs_0_, f32[10,64,512]{2,1,0:T(8,128)} %refs_1_.3, f32[10,64,512]{2,1,0:T(8,128)} %refs_2_.5, f32[10,64,512]{2,1,0:T(8,128)} %refs_3_.5, f32[10,64,512]{2,1,0:T(8,128)} %refs_4_.5, s32[64,512]{1,0:T(8,128)} %refs_5_.5, f32[64,512]{1,0:T(8,128)} %refs_6_.5), custom_call_target="tpu_custom_call" | custom-call | tf_op jit(solution)/shard_map/edge/pallas_call | solution.py:593
  3.7 1.5 %collective-permute-start = (f32[2,64,128]{2,1,0:T(8,128)S(1)}, f32[2,64,128]{2,1,0:T(8,128)S(1)}, u32[]{:S(2)}, u32[]{:S(2)}) collective-permute-start(f32[2,64,128]{2,1,0:T(8,128)S(1)} %get-tuple-element.48), channel_id=1, source_target_pairs={{0,1},{2,3},{4,5},{6,7},{1,0},{3,2},{5,4},{7,6},{8,9},{10,11},{12,... | collective-permute-start | bytes 196616 | tf_op jit(solution)/shard_map/ppermute | solution.py:572
  5.2 3.2 %collective-permute-start.1 = (f32[2,64,128]{2,1,0:T(8,128)S(1)}, f32[2,64,128]{2,1,0:T(8,128)S(1)}, u32[]{:S(2)}, u32[]{:S(2)}) collective-permute-start(f32[2,64,128]{2,1,0:T(8,128)S(1)} %get-tuple-element.49), channel_id=1, source_target_pairs={{1,2},{3,4},{5,6},{2,1},{4,3},{6,5},{9,10},{11,12},{13,14},{10,9},... | collective-permute-start | bytes 196616 | tf_op jit(solution)/shard_map/ppermute | solution.py:572
  8.4 0.0 collective-permute-done.refs_8_.refs_7_
  8.4 2.3 %collective-permute-done.1.refs_9_.refs_8_ = f32[2,64,128]{2,1,0:T(8,128)S(1)} collective-permute-done((f32[2,64,128]{2,1,0:T(8,128)S(1)}, f32[2,64,128]{2,1,0:T(8,128)S(1)}, u32[]{:S(2)}, u32[]{:S(2)}) %collective-permute-start.1) | collective-permute-done | bytes 65568 | tf_op jit(solution)/shard_map/ppermute | solution.py:572
  10.8 2.1 %turn.1 = (f32[5,192,128]{2,1,0:T(8,128)S(1)}, f32[5,192,128]{2,1,0:T(8,128)S(1)}) custom-call(s32[1]{0:T(128)} %bitcast.1.refs_0_, s32[1]{0:T(128)} %bitcast.refs_1_.refs_0_, f32[10,64,512]{2,1,0:T(8,128)} %refs_1_.3, f32[10,64,512]{2,1,0:T(8,128)} %refs_2_.5, f32[10,64,512]{2,1,0:T(8,128)} %refs_3_.5, f32[10,64,512]{2,1,0:T(8,128)} %refs_4_.5, ...), custom_call_target="tpu_custom_call" | custom-call | tf_op jit(solution)/shard_map/turn/pallas_call | solution.py:601
  12.9 0.7 collective-permute-start.3
  13.6 3.8 %collective-permute-start.2 = (f32[5,192,128]{2,1,0:T(8,128)S(1)}, f32[5,192,128]{2,1,0:T(8,128)S(1)}, u32[]{:S(2)}, u32[]{:S(2)}) collective-permute-start(f32[5,192,128]{2,1,0:T(8,128)S(1)} %get-tuple-element.50.refs_9_), channel_id=1, source_target_pairs={{0,8},{16,24},{32,40},{48,56},{64,72},{80,88},{96,104},{112,120},{... | collective-permute-start | bytes 1474568 | tf_op jit(solution)/shard_map/ppermute | solution.py:572
  17.4 14.7 %inner.1 = (f32[10,416,128]{2,1,0:T(8,128)S(1)}, f32[10,416,128]{2,1,0:T(8,128)S(1)}, f32[10,416,128]{2,1,0:T(8,128)S(1)}, f32[10,416,128]{2,1,0:T(8,128)S(1)}, ...) custom-call(s32[1]{0:T(128)} %bitcast.1.refs_0_, ...), custom_call_target="tpu_custom_call" | custom-call | flops 100000000 | bytes 6000000 | tf_op jit(solution)/shard_map/inner/pallas_call | solution.py:612
  32.1 0.0 collective-permute-done.3.refs_25_
  32.1 0.0 collective-permute-done.2.refs_24_
  32.1 6.2 %first.1 = (f32[10,416,128]{2,1,0:T(8,128)S(1)}, f32[10,416,128]{2,1,0:T(8,128)S(1)}, f32[10,416,128]{2,1,0:T(8,128)S(1)}, f32[10,416,128]{2,1,0:T(8,128)S(1)}, ...) custom-call(s32[1]{0:T(128)} %bitcast.refs_1_.refs_0_, ...), custom_call_target="tpu_custom_call", output_to_operand_aliasing={{0}: (1, {}), {1}: (2, {}), {2}: (3, {}), {3}: (4, {}), {4}... | custom-call | tf_op jit(solution)/shard_map/first/pallas_call | solution.py:619
  38.3 19.6 %all_to_all.22 = f32[128,1,128]{2,1,0:T(1,128)S(1)} all-to-all(f32[128,1,128]{2,1,0:T(1,128)S(1)} %bitcast.12), channel_id=1, replica_groups=mesh['gx_0'=4,'gx_1'=4,'gy_0'=4,'gy_1'=2] {'gx_0','gx_1','gy_0','gy_1'}, dimensions={0} | all-to-all | bytes 131072 | tf_op jit(solution)/shard_map/all_to_all | solution.py:625
  57.9 14.7 %next.1 = (f32[10,416,128]{2,1,0:T(8,128)S(1)}, f32[10,416,128]{2,1,0:T(8,128)S(1)}, f32[10,416,128]{2,1,0:T(8,128)S(1)}, f32[10,416,128]{2,1,0:T(8,128)S(1)}, f...) custom-call(f32[10,416,128]{2,1,0:T(8,128)S(1)} %get-tuple-element.7, ...), custom_call_target="tpu_custom_call", output_to_operand_aliasing={{0}: (6, {}), {1}: (7, {}), {2}: (8, {}), {3}: (9, {}), {4}... | custom-call | tf_op jit(solution)/shard_map/next/pallas_call | solution.py:628
  72.6 13.8 %all_to_all.23 = f32[128,1,128]{2,1,0:T(1,128)S(1)} all-to-all(f32[128,1,128]{2,1,0:T(1,128)S(1)} %bitcast.13), channel_id=1, replica_groups=mesh['gx_0'=4,'gx_1'=4,'gy_0'=4,'gy_1'=2] {'gx_0','gx_1','gy_0','gy_1'}, dimensions={0} | all-to-all | bytes 131072 | tf_op jit(solution)/shard_map/all_to_all | solution.py:636
  86.5 1.8 %last.1 = (f32[10,64,512]{2,1,0:T(8,128)}, f32[10,64,512]{2,1,0:T(8,128)}) custom-call(f32[10,416,128]{2,1,0:T(8,128)S(1)} %get-tuple-element.89.refs_0_, f32[10,416,128]{2,1,0:T(8,128)S(1)} %get-tuple-element.90.refs_1_, f32[10,416,128]{2,1,0:T(8,128)S(1)} %get-tuple-element.91.refs_2_, f32[10,256,128]{2,1,0:T(8,128)S(1)} %get-tuple-element.92.refs_3_, ...), custom_call_target="tpu_custom_call" | custom-call | tf_op jit(solution)/shard_map/last/pallas_call | solution.py:639
Async XLA Ops:
  3.7 4.7 %collective-permute-start = (f32[2,64,128]{2,1,0:T(8,128)S(1)}, f32[2,64,128]{2,1,0:T(8,128)S(1)}, u32[]{:S(2)}, u32[]{:S(2)}) collective-permute-start(f32[2,64,128]{2,1,0:T(8,128)S(1)} %get-tuple-element.48), channel_id=1, source_target_pairs={{0,1},{2,3},{4,5},{6,7},{1,0},{3,2},{5,4},{7,6},{8,9},{10,11},{12,... | collective-permute-start | bytes 196616 | tf_op jit(solution)/shard_map/ppermute | solution.py:572
  5.2 5.6 %collective-permute-start.1 = (f32[2,64,128]{2,1,0:T(8,128)S(1)}, f32[2,64,128]{2,1,0:T(8,128)S(1)}, u32[]{:S(2)}, u32[]{:S(2)}) collective-permute-start(f32[2,64,128]{2,1,0:T(8,128)S(1)} %get-tuple-element.49), channel_id=1, source_target_pairs={{1,2},{3,4},{5,6},{2,1},{4,3},{6,5},{9,10},{11,12},{13,14},{10,9},... | collective-permute-start | bytes 196616 | tf_op jit(solution)/shard_map/ppermute | solution.py:572
  12.9 19.2 %collective-permute-start.3 = (f32[5,192,128]{2,1,0:T(8,128)S(1)}, f32[5,192,128]{2,1,0:T(8,128)S(1)}, u32[]{:S(2)}, u32[]{:S(2)}) collective-permute-start(f32[5,192,128]{2,1,0:T(8,128)S(1)} %get-tuple-element.74), channel_id=1, source_target_pairs={{8,16},{24,32},{40,48},{56,64},{72,80},{88,96},{104,112},{16,8},{3... | collective-permute-start | bytes 1474568 | tf_op jit(solution)/shard_map/ppermute | solution.py:572
  13.6 18.5 %collective-permute-start.2 = (f32[5,192,128]{2,1,0:T(8,128)S(1)}, f32[5,192,128]{2,1,0:T(8,128)S(1)}, u32[]{:S(2)}, u32[]{:S(2)}) collective-permute-start(f32[5,192,128]{2,1,0:T(8,128)S(1)} %get-tuple-element.50.refs_9_), channel_id=1, source_target_pairs={{0,8},{16,24},{32,40},{48,56},{64,72},{80,88},{96,104},{112,120},{... | collective-permute-start | bytes 1474568 | tf_op jit(solution)/shard_map/ppermute | solution.py:572

commit v3 on v2

--- a/solution.py
+++ b/solution.py
@@ -59,36 +59,53 @@
     return [(f, layer) for f in range(4) for layer in range(layers)] + [(4, None), (5, None)]
 
 
-def edge_kernel(layers, par, p_in, k_in, o_in, r_in, act_in, rech_in, send_a, send_b, edges, act_edges, rech_edges, sems):
+def edge_kernel(layers, par, par_x, p_in, k_in, o_in, r_in, act_in, rech_in,
+                p_ref, k_ref, o_ref, r_ref, act_ref, rech_ref, send_a, send_b, act_int, sems):
+    fields = (p_ref, k_ref, o_ref, r_ref)
     copies = []
-    for side, first in ((0, 0), (1, 384)):
-        cols = pl.ds(first, 128)
-        for f, src in enumerate((p_in, k_in, o_in, r_in)):
-            copies.append(pltpu.make_async_copy(src.at[:, :, cols], edges.at[f, side], sems.at[side * 6 + f]))
-        copies.append(pltpu.make_async_copy(act_in.at[:, cols], act_edges.at[side], sems.at[side * 6 + 4]))
-        copies.append(pltpu.make_async_copy(rech_in.at[:, cols], rech_edges.at[side], sems.at[side * 6 + 5]))
+    for t in (0, 3, 1, 2):
+        cols = pl.ds(128 * t, 128)
+        own = at(t, TOP, 64)
+        for f, (src, dst) in enumerate(zip((p_in, k_in, o_in, r_in), fields)):
+            copies.append(pltpu.make_async_copy(src.at[:, :, cols], dst.at[:, own, :], sems.at[t, f]))
+        copies.append(pltpu.make_async_copy(act_in.at[:, cols], act_int.at[t], sems.at[t, 4]))
+        copies.append(pltpu.make_async_copy(rech_in.at[:, cols], rech_ref.at[own, :], sems.at[t, 5]))
     for copy in copies:
         copy.start()
-    for copy in copies:
+    zero = jnp.zeros((8, 128), F32)
+
+    def clear(layer, carry):
+        for ref in fields:
+            for t in range(NT):
+                ref[layer, at(t, 0), :] = zero
+                ref[layer, at(t, ROWS - 8), :] = zero
+        return carry
+
+    lax.fori_loop(0, layers, clear, 0)
+    for ref in (act_ref, rech_ref):
+        for t in range(NT):
+            ref[at(t, 0), :] = zero
+            ref[at(t, ROWS - 8), :] = zero
+    for copy in copies[:12]:
         copy.wait()
     first = lanes() < 5
     last = lanes() >= 123
     odd = par[0] == 1
-    zero = jnp.zeros((8, 128), F32)
 
     def pack(row, carry):
         rows = pl.ds(pl.multiple_of(8 * row, 8), 8)
+        start = pl.multiple_of(TOP + 8 * row, 8)
         low = [zero, zero]
         high = [zero, zero]
         for u, (f, layer) in enumerate(strip_units(layers)):
             place = 5 * (u % UNITS)
             here = u // UNITS
             if f == 4:
-                a, b = act_edges[0, rows, :].astype(F32), act_edges[1, rows, :].astype(F32)
+                a, b = act_int[0, rows, :].astype(F32), act_int[3, rows, :].astype(F32)
             elif f == 5:
-                a, b = rech_edges[0, rows, :], rech_edges[1, rows, :]
+                a, b = rech_ref[at(0, start), :], rech_ref[at(3, start), :]
             else:
-                a, b = edges[f, 0, layer, rows, :], edges[f, 1, layer, rows, :]
+                a, b = tile_of(fields[f], layer, 0, start), tile_of(fields[f], layer, 3, start)
             a = jnp.where(first, a, 0.0)
             b = jnp.where(last, b, 0.0)
             low[here] = low[here] + (pltpu.roll(a, place, 1) if place else a)
@@ -99,6 +116,10 @@
         return carry
 
     lax.fori_loop(0, 8, pack, 0)
+    for copy in copies[12:]:
+        copy.wait()
+    for t in range(4):
+        act_ref[at(t, TOP, 64), :] = act_int[t].astype(F32)
 
 
 def unpack_strips(layers, odd, got_a, got_b, rows, put):
@@ -119,51 +140,39 @@
 STRIP_ROWS = ((0, 5), (5, 5), (10, 4), (14, 4))
 
 
-def turn_kernel(layers, par_y, par_x, p_in, k_in, o_in, r_in, act_in, rech_in, got_a, got_b,
-                send_a, send_b, edges, act_edges, rech_edges, act_int, sems):
-    copies = []
-    for side, first in ((0, 0), (1, 56)):
-        rows = pl.ds(first, 8)
-        for t in range(4):
-            cols = pl.ds(128 * t, 128)
-            for f, src in enumerate((p_in, k_in, o_in, r_in)):
-                copies.append(pltpu.make_async_copy(
-                    src.at[:, rows, cols], edges.at[f, side, :, t], sems.at[side, t, f]))
-            copies.append(pltpu.make_async_copy(act_in.at[rows, cols], act_int.at[side, t], sems.at[side, t, 4]))
-            copies.append(pltpu.make_async_copy(rech_in.at[rows, cols], rech_edges.at[side, t], sems.at[side, t, 5]))
-    for copy in copies:
-        copy.start()
+def turn_kernel(layers, par_y, par_x, p_ref, k_ref, o_ref, r_ref, act_ref, rech_ref, got_a, got_b,
+                send_a, send_b, corners, act_corner, rech_corner):
+    fields = (p_ref, k_ref, o_ref, r_ref)
     odd = par_y[0] == 1
     for side in range(2):
         def put(f, layer, value):
             if f == 4:
-                act_edges[side, 4] = value
+                act_corner[side] = value
             elif f == 5:
-                rech_edges[side, 4] = value
+                rech_corner[side] = value
             else:
-                edges[f, side, layer, 4] = value
+                corners[f, side, layer] = value
 
         unpack_strips(layers, odd, got_a, got_b, pl.ds(56 * side, 8), put)
-    for copy in copies:
-        copy.wait()
-    for side in range(2):
-        for t in range(4):
-            act_edges[side, t] = act_int[side, t].astype(F32)
     for send, side in ((send_a, 1 - par_x[0]), (send_b, par_x[0])):
-        start5 = 3 * side
-        start4 = 4 * side
+        first5, first4 = 3 * side, 4 * side
+        start5, start4 = TOP + 59 * side, TOP + 60 * side
 
         def fill(layer, carry):
             for f, (place, depth) in enumerate(STRIP_ROWS):
-                start = start5 if depth == 5 else start4
-                for t in range(NT):
-                    send[t, pl.ds(layer * 18 + place, depth), :] = edges[f, side, layer, t, pl.ds(start, depth), :]
+                start, first = (start5, first5) if depth == 5 else (start4, first4)
+                rows = pl.ds(layer * 18 + place, depth)
+                for t in range(4):
+                    send[t, rows, :] = fields[f][layer, at(t, start, depth), :]
+                send[4, rows, :] = corners[f, side, layer, pl.ds(first, depth), :]
             return carry
 
         lax.fori_loop(0, layers, fill, 0)
-        for t in range(NT):
-            send[t, 18 * layers:18 * layers + 5, :] = act_edges[side, t, pl.ds(start5, 5), :]
-            send[t, 18 * layers + 5:18 * layers + 9, :] = rech_edges[side, t, pl.ds(start4, 4), :]
+        for t in range(4):
+            send[t, 18 * layers:18 * layers + 5, :] = act_ref[at(t, start5, 5), :]
+            send[t, 18 * layers + 5:18 * layers + 9, :] = rech_ref[at(t, start4, 4), :]
+        send[4, 18 * layers:18 * layers + 5, :] = act_corner[side, pl.ds(first5, 5), :]
+        send[4, 18 * layers + 5:18 * layers + 9, :] = rech_corner[side, pl.ds(first4, 4), :]
 
 
 def place_strips(layers, up, refs, got_a, got_b):
@@ -202,6 +211,12 @@
     by_mob = trans * (m_a + m_b)
     by_drop = trans * drop
     return by_mob + s_a * by_drop, s_b * by_drop - by_mob, by_mob * drop
+
+
+def over_layers(layers, one_layer, carry):
+    if layers % 2:
+        return lax.fori_loop(0, layers, one_layer, carry)
+    return lax.fori_loop(0, layers // 2, lambda i, c: one_layer(2 * i + 1, one_layer(2 * i, c)), carry)
 
 
 def far_faces(layers, starts, s, make_trans):
@@ -239,46 +254,61 @@
                 s.zf[layer + 1, here, :] = zf
         return carry
 
-    lax.fori_loop(0, layers, one_layer, 0)
-
-
-def assemble(layers, starts, s, make_trans):
+    over_layers(layers, one_layer, 0)
+
+
+def y_faces(layers, starts, s, make_trans):
     def one_layer(layer, carry):
         for start in starts:
             p = tiles_of(s.p, layer, start)
             m = tiles_of(s.m, layer, start)
             der = tiles_of(s.s, layer, start)
+            p_north, m_north, s_north = from_north(p), from_north(m), from_north(der)
             if make_trans:
                 k = tiles_of(s.k, layer, start)
                 k_north = from_north(k)
-                ty = [s.ay[at(t, start), :] * (k[t] + k_north[t]) for t in range(NT)]
-                for t in range(NT):
-                    s.ty[layer, at(t, start), :] = ty[t]
-            else:
-                ty = tiles_of(s.ty, layer, start)
-            p_north, m_north, s_north = from_north(p), from_north(m), from_north(der)
-            across_y = [face(ty[t], p[t], p_north[t], m[t], m_north[t], der[t], s_north[t], 0.0) for t in range(NT)]
-            ya = from_south([f[0] for f in across_y])
-            yb = from_south([f[1] for f in across_y])
-            yf = from_south([f[2] for f in across_y])
             for t in range(NT):
                 here = at(t, start)
-                s.ya[layer, here, :] = ya[t]
-                s.yb[layer, here, :] = across_y[t][1]
-                sig = tile_of(s.sig, layer, t, start)
+                if make_trans:
+                    trans = s.ay[here, :] * (k[t] + k_north[t])
+                    s.ty[layer, here, :] = trans
+                else:
+                    trans = tile_of(s.ty, layer, t, start)
+                ca, cb, flow = face(trans, p[t], p_north[t], m[t], m_north[t], der[t], s_north[t], 0.0)
+                s.ya[layer, here, :] = ca
+                s.yb[layer, here, :] = cb
+                s.yf[layer, here, :] = flow
+        return carry
+
+    over_layers(layers, one_layer, 0)
+
+
+def assemble(layers, starts, s):
+    def one_layer(layer, carry):
+        for start in starts:
+            ya = tiles_of(s.ya, layer, start)
+            yb = tiles_of(s.yb, layer, start)
+            yf = tiles_of(s.yf, layer, start)
+            ya_south, yb_south, yf_south = from_south(ya), from_south(yb), from_south(yf)
+            for t in range(NT):
+                here = at(t, start)
+                s.ya[layer, here, :] = ya_south[t]
                 ap = tile_of(s.ap, layer, t, start)
                 ocean = 1.0 - s.act[here, :]
+                sig = tile_of(s.sig, layer, t, start)
                 stored = ap * sig
                 center = (stored - stored * sig) + ocean
                 center = center + (tile_of(s.xa, layer, t, start) - tile_of(s.xb, layer, t, start - 1))
-                center = center + (across_y[t][0] - yb[t]) + (tile_of(s.za, layer + 1, t, start) - tile_of(s.zb, layer, t, start))
-                s.c[layer, here, :] = center
-                flows = (tile_of(s.xf, layer, t, start) - tile_of(s.xf, layer, t, start - 1))
-                flows = flows + (across_y[t][2] - yf[t]) + (tile_of(s.zf, layer + 1, t, start) - tile_of(s.zf, layer, t, start))
-                s.q[layer, here, :] = (tile_of(s.s0, layer, t, start) - stored) - ocean * p[t] - flows
-        return carry
-
-    lax.fori_loop(0, layers, one_layer, 0)
+                center = center + (tile_of(s.za, layer + 1, t, start) - tile_of(s.zb, layer, t, start))
+                s.c[layer, here, :] = center + (ya[t] - yb_south[t])
+                flows = tile_of(s.xf, layer, t, start) - tile_of(s.xf, layer, t, start - 1)
+                flows = flows + (tile_of(s.zf, layer + 1, t, start) - tile_of(s.zf, layer, t, start))
+                flows = flows + (yf[t] - yf_south[t])
+                s.q[layer, here, :] = (
+                    (tile_of(s.s0, layer, t, start) - stored) - ocean * tile_of(s.p, layer, t, start) - flows)
+        return carry
+
+    over_layers(layers, one_layer, 0)
 
 
 def product_tile(layers, s, v_ref, layer, start, count):
@@ -306,7 +336,7 @@
                 s.w[layer, at(t, start), :] = out[t]
         return carry
 
-    lax.fori_loop(0, layers, one_layer, 0)
+    over_layers(layers, one_layer, 0)
 
 
 def second_product(layers, starts, s, sums, z_ref):
@@ -322,7 +352,7 @@
                     sums[i] = sums[i] + a * b
         return tuple(sums)
 
-    return lax.fori_loop(0, layers, one_layer, sums)
+    return over_layers(layers, one_layer, sums)
 
 
 def put_sums(sums, out_ref):
@@ -372,8 +402,9 @@
 
 STATE = ("p", "k", "s0", "ap", "tx", "ty", "tz", "q", "w")
 COEFS = ("c", "xa", "xb", "ya", "yb", "za", "zb", "xf", "zf")
-POINT = ("sig", "m", "s")
+POINT = ("sig", "m", "s", "yf")
 TALL = ("za", "zb", "zf")
+PLANES = ("act", "rech", "ax", "ay")
 
 
 def space(layers, name):
@@ -417,35 +448,12 @@
     lax.fori_loop(0, layers, point, 0)
 
 
-def inner_kernel(layers, par_y, p_in, k_in, o_in, r_in, act_in, rech_in, got_a, got_b, after, *refs):
-    names = STATE + COEFS + ("act", "rech", "ax", "ay")
+def inner_kernel(layers, par_y, p_old, k_old, o_old, r_old, act_old, rech_old, got_a, got_b, after, *refs):
+    names = STATE + COEFS + PLANES
     s = Refs(**dict(zip(names, refs)))
-    part_ref = refs[len(names)]
-    s.sig, s.m, s.s, act_int, sems = refs[len(names) + 1:]
-    copies = []
-    for t in range(4):
-        cols = pl.ds(128 * t, 128)
-        for f, (src, dst) in enumerate(((p_in, s.p), (k_in, s.k), (o_in, s.s0), (r_in, s.ap))):
-            copies.append(pltpu.make_async_copy(src.at[:, :, cols], dst.at[:, at(t, TOP, 64), :], sems.at[t, f]))
-        copies.append(pltpu.make_async_copy(act_in.at[:, cols], act_int.at[t], sems.at[t, 4]))
-        copies.append(pltpu.make_async_copy(rech_in.at[:, cols], s.rech.at[at(t, TOP, 64), :], sems.at[t, 5]))
-    for copy in copies:
-        copy.start()
+    part_ref, s.sig, s.m, s.s, s.yf = refs[len(names):]
     zero = jnp.zeros((8, 128), F32)
     fields = (s.p, s.k, s.s0, s.ap)
-
-    def clear(layer, carry):
-        for ref in fields:
-            for t in range(NT):
-                ref[layer, at(t, 0), :] = zero
-                ref[layer, at(t, ROWS - 8), :] = zero
-        return carry
-
-    lax.fori_loop(0, layers, clear, 0)
-    for ref in (s.act, s.rech):
-        for t in range(NT):
-            ref[at(t, 0), :] = zero
-            ref[at(t, ROWS - 8), :] = zero
     clear_bottom(s)
     odd = par_y[0] == 1
 
@@ -464,14 +472,11 @@
         return carry
 
     lax.fori_loop(0, 8, unpack, 0)
-    for copy in copies:
-        copy.wait()
-    for t in range(4):
-        s.act[at(t, TOP, 64), :] = act_int[t].astype(F32)
     points(layers, s, range(8, 72, 8), ())
     mask_pairs(s, (*range(8, 64, 8), 63))
     far_faces(layers, (*range(8, 64, 8), 63), s, True)
-    assemble(layers, range(12, 68, 8), s, True)
+    y_faces(layers, range(12, 68, 8), s, True)
+    assemble(layers, range(12, 68, 8), s)
     first_product(layers, range(20, 60, 8), s)
     sums = second_product(layers, range(24, 56, 8), s, (zero,) * 6, None)
     for i in range(6):
@@ -479,18 +484,19 @@
 
 
 def first_kernel(layers, par_x, *refs):
-    names = STATE + COEFS + ("act", "rech", "ax", "ay")
+    names = STATE + COEFS + PLANES
     count = len(names)
     part_ref, got_a, got_b = refs[count:count + 3]
     refs = refs[count + 3:]
     s = Refs(**dict(zip(names, refs)))
     sums_ref = refs[count]
-    s.sig, s.m, s.s = refs[count + 1:]
+    s.sig, s.m, s.s, s.yf = refs[count + 1:]
     place_strips(layers, par_x[0] == 1, (s.p, s.k, s.s0, s.ap, s.rech, s.act), got_a, got_b)
     points(layers, s, (0, 72), (8, 64))
     mask_pairs(s, (0, 4, 64, 68))
     far_faces(layers, (0, 64, 68), s, True)
-    assemble(layers, (4, 68), s, True)
+    y_faces(layers, (4, 68), s, True)
+    assemble(layers, (4, 68), s)
     first_product(layers, (4, 12, 60, 68), s)
     sums = second_product(layers, (8, 16, 56, 64), s, tuple(part_ref[i] for i in range(6)), None)
     put_sums(sums, sums_ref)
@@ -525,7 +531,8 @@
     lax.fori_loop(0, layers, point, 0)
     starts = range(4, 76, 8)
     far_faces(layers, (0, *starts), s, False)
-    assemble(layers, starts, s, False)
+    y_faces(layers, starts, s, False)
+    assemble(layers, starts, s)
     first_product(layers, starts, s)
     sums = tuple(jnp.zeros((8, 128), F32) for _ in range(6))
     sums = second_product(layers, range(TOP, TOP + 64, 8), s, sums, z_ref)
@@ -581,41 +588,41 @@
 
 def body(pressure, pressure_old, conductivity, porosity, recharge, active):
     layers = pressure.shape[0]
-    par_x = (lax.axis_index(GX) % 2).astype(jnp.int32).reshape(1)
-    par_y = (lax.axis_index(GY) % 2).astype(jnp.int32).reshape(1)
+    par_x = (lax.axis_index(GX[1]) & 1).astype(jnp.int32).reshape(1)
+    par_y = (lax.axis_index(GY[1]) & 1).astype(jnp.int32).reshape(1)
     inputs = outside(pressure, conductivity, pressure_old, porosity, active, recharge)
     dma = pltpu.SemaphoreType.DMA
     strip_y = pltpu.VMEM((2, 64, 128), F32)
     strip_x = pltpu.VMEM((NT, 192, 128), F32)
     plane = pltpu.VMEM((SPAN, 128), F32)
-    part = pltpu.VMEM((6, 8, 128), F32)
+    part = pltpu.VMEM((8, 8, 128), F32)
     block = jax.ShapeDtypeStruct((128, 128), F32)
-    send_a, send_b = pl.pallas_call(
-        bound(edge_kernel, layers), name="edge", out_shape=(strip_y,) * 2, in_specs=[SM] + [HB] * 6, out_specs=(VM,) * 2,
-        scratch_shapes=[pltpu.VMEM((4, 2, layers, 64, 128), F32), pltpu.VMEM((2, 64, 128), jnp.int32),
-                        pltpu.VMEM((2, 64, 128), F32), dma((12,))],
+    loaded = (space(layers, "p"),) * 4 + (plane,) * 2
+    *fields, send_a, send_b = pl.pallas_call(
+        bound(edge_kernel, layers), name="edge", out_shape=loaded + (strip_y,) * 2, in_specs=[SM] * 2 + [HB] * 6,
+        out_specs=(VM,) * 8, scratch_shapes=[pltpu.VMEM((4, 64, 128), jnp.int32), dma((4, 6))],
         compiler_params=grant(GRANT),
-    )(par_y, *inputs)
+    )(par_y, par_x, *inputs)
     y_a = swap(send_a, GY, 0)
     y_b = swap(send_b, GY, 1)
     send_a, send_b = pl.pallas_call(
-        bound(turn_kernel, layers), name="turn", out_shape=(strip_x,) * 2, in_specs=[SM] * 2 + [HB] * 6 + [VM] * 2,
+        bound(turn_kernel, layers), name="turn", out_shape=(strip_x,) * 2, in_specs=[SM] * 2 + [VM] * 8,
         out_specs=(VM,) * 2,
-        scratch_shapes=[pltpu.VMEM((4, 2, layers, NT, 8, 128), F32), pltpu.VMEM((2, NT, 8, 128), F32),
-                        pltpu.VMEM((2, NT, 8, 128), F32), pltpu.VMEM((2, 4, 8, 128), jnp.int32), dma((2, 4, 6))],
+        scratch_shapes=[pltpu.VMEM((4, 2, layers, 8, 128), F32), pltpu.VMEM((2, 8, 128), F32),
+                        pltpu.VMEM((2, 8, 128), F32)],
         compiler_params=grant(GRANT),
-    )(par_y, par_x, *inputs, y_a, y_b)
+    )(par_y, par_x, *keep(*fields), y_a, y_b)
     x_a = swap(send_a, GX, 0)
     x_b = swap(send_b, GX, 1)
     state = tuple(space(layers, name) for name in STATE + COEFS) + (plane,) * 4
     points_scratch = [space(layers, name) for name in POINT]
     *fields, part_sums = pl.pallas_call(
         bound(inner_kernel, layers), name="inner", out_shape=state + (part,),
-        in_specs=[SM] + [HB] * 6 + [VM] * 3, out_specs=(VM,) * (len(state) + 1),
-        scratch_shapes=points_scratch + [pltpu.VMEM((4, 64, 128), jnp.int32), dma((4, 6))],
-        compiler_params=grant(GRANT),
+        in_specs=[SM] + [VM] * 9, out_specs=(VM,) * (len(state) + 1),
+        input_output_aliases={1: 0, 2: 1, 3: 2, 4: 3, 5: len(state) - 4, 6: len(state) - 3},
+        scratch_shapes=points_scratch, compiler_params=grant(GRANT),
         cost_estimate=pl.CostEstimate(flops=100_000_000, transcendentals=0, bytes_accessed=6_000_000),
-    )(par_y, *inputs, y_a, y_b, send_a)
+    )(par_y, *keep(*fields), y_a, y_b, send_a)
     *fields, sums = pl.pallas_call(
         bound(first_kernel, layers), name="first", out_shape=state + (block,),
         in_specs=[SM] + [VM] * (len(state) + 3), out_specs=(VM,) * (len(state) + 1),
@@ -623,7 +630,7 @@
         scratch_shapes=points_scratch, compiler_params=grant(GRANT),
     )(par_x, *keep(*fields, part_sums), x_a, x_b)
     sums = lax.all_to_all(sums, ALL, 0, 0, tiled=True)
-    named = dict(zip(STATE + COEFS + ("act", "rech", "ax", "ay"), fields))
+    named = dict(zip(STATE + COEFS + PLANES, fields))
     moved = tuple(space(layers, name) for name in MOVED)
     p, q, w, *rest = pl.pallas_call(
         bound(next_kernel, layers), name="next",
@@ -642,8 +649,8 @@
     )(*keep(p, q, w, z), sums)
 
 
-GRANT = 10
-GRANT2 = 20
+GRANT = 12
+GRANT2 = 22
 
 
 def solution(mesh):

time: 88.6 us -> 80 us (0.903)
  Pallas kernels: 42.6 us -> 32 us
  blocking collectives: 33.5 us -> 35.5 us
    pallas_call x1, Pallas kernels: 14.7 us -> 10.5 us  [body(): pl.pallas_call(bound(inner_kernel, layers), name='inner', out_shape=state...]
    pallas_call x1, Pallas kernels: 14.7 us -> 10.9 us  [body(): pl.pallas_call(bound(next_kernel, layers), name='next', out_shape=moved +...]
    all_to_all x2, blocking collectives: 33.5 us -> 35.5 us  [body(): sums = lax.all_to_all(sums, ALL, 0, 0, tiled=True)]
    pallas_call x1, Pallas kernels: 2.1 us -> 0.54 us  [body(): pl.pallas_call(bound(turn_kernel, layers), name='turn', out_shape=(strip_...]
    pallas_call x1, Pallas kernels: 6.16 us -> 5.04 us  [body(): pl.pallas_call(bound(first_kernel, layers), name='first', out_shape=state...]
  transfers between devices with their start and end apart: 4 -> 4, of which waited for: 1 -> 1; matrix products, arithmetic and copies ran while one was open for 0% -> 0% of each run, Pallas kernels for 17% -> 13%
where the time goes in v3:
time: 80 us; the launch traced here: 79.8 us
  blocking collectives  35.5 us (44%)
  Pallas kernels  32 us (40%)
  starting transfers between devices  9.2 us (11%)
  waiting for transfers between devices  2.35 us (3%)
    all_to_all x2, blocking collectives, body(): sums = lax.all_to_all(sums, ALL, 0, 0, tiled=True)  35.5 us
    pallas_call x1, Pallas kernels, body(): pl.pallas_call(bound(next_kernel, layers), name='next', out_shape=moved +...  10.9 us
    pallas_call x1, Pallas kernels, body(): pl.pallas_call(bound(inner_kernel, layers), name='inner', out_shape=state...  10.5 us
    ppermute x4, starting transfers between devices, swap(): return lax.ppermute(value, axes, pairs + [(b, a) for a, b in pairs])  9.2 us
    pallas_call x1, Pallas kernels, body(): pl.pallas_call(bound(first_kernel, layers), name='first', out_shape=state...  5.04 us
    pallas_call x1, Pallas kernels, body(): pl.pallas_call(bound(edge_kernel, layers), name='edge', out_shape=loaded...  3.25 us
    ppermute x4, waiting for transfers between devices, swap(): return lax.ppermute(value, axes, pairs + [(b, a) for a, b in pairs])  2.35 us
    pallas_call x1, Pallas kernels, body(): pl.pallas_call(bound(last_kernel, layers), name='last', out_shape=(out, o...  1.84 us
  transfers between devices with their start and end apart: 4, of which 1 were waited for; matrix products, arithmetic and copies ran while one was open for 0% of the time, Pallas kernels for 13%

profile of v3, /device:TPU:1, one launch (start us, length us, event | category | flops | bytes accessed | tf_op | source)
XLA Modules:
  0.0 79.8 jit_solution(6744083494759259626)
XLA Ops:
  0.6 3.2 %edge.1 = (f32[10,416,128]{2,1,0:T(8,128)S(1)}, f32[10,416,128]{2,1,0:T(8,128)S(1)}, f32[10,416,128]{2,1,0:T(8,128)S(1)}, f32[10,416,128]{2,1,0:T(8,128)S(1)}, f...) custom-call(s32[1]{0:T(128)} %bitcast.1.refs_0_, ...), custom_call_target="tpu_custom_call" | custom-call | tf_op jit(solution)/shard_map/edge/pallas_call | solution.py:601
  3.9 1.5 %collective-permute-start = (f32[2,64,128]{2,1,0:T(8,128)S(1)}, f32[2,64,128]{2,1,0:T(8,128)S(1)}, u32[]{:S(2)}, u32[]{:S(2)}) collective-permute-start(f32[2,64,128]{2,1,0:T(8,128)S(1)} %get-tuple-element.60), channel_id=1, source_target_pairs={{0,1},{2,3},{4,5},{6,7},{1,0},{3,2},{5,4},{7,6},{8,9},{10,11},{12,... | collective-permute-start | bytes 196616 | tf_op jit(solution)/shard_map/ppermute | solution.py:579
  5.4 3.2 %collective-permute-start.1 = (f32[2,64,128]{2,1,0:T(8,128)S(1)}, f32[2,64,128]{2,1,0:T(8,128)S(1)}, u32[]{:S(2)}, u32[]{:S(2)}) collective-permute-start(f32[2,64,128]{2,1,0:T(8,128)S(1)} %get-tuple-element.61), channel_id=1, source_target_pairs={{1,2},{3,4},{5,6},{2,1},{4,3},{6,5},{9,10},{11,12},{13,14},{10,9},... | collective-permute-start | bytes 196616 | tf_op jit(solution)/shard_map/ppermute | solution.py:579
  8.6 0.0 collective-permute-done.refs_8_.refs_7_
  8.6 2.3 %collective-permute-done.1.refs_9_.refs_8_ = f32[2,64,128]{2,1,0:T(8,128)S(1)} collective-permute-done((f32[2,64,128]{2,1,0:T(8,128)S(1)}, f32[2,64,128]{2,1,0:T(8,128)S(1)}, u32[]{:S(2)}, u32[]{:S(2)}) %collective-permute-start.1) | collective-permute-done | bytes 65568 | tf_op jit(solution)/shard_map/ppermute | solution.py:579
  10.9 0.5 turn.1
  11.5 0.7 collective-permute-start.3
  12.2 3.8 %collective-permute-start.2 = (f32[5,192,128]{2,1,0:T(8,128)S(1)}, f32[5,192,128]{2,1,0:T(8,128)S(1)}, u32[]{:S(2)}, u32[]{:S(2)}) collective-permute-start(f32[5,192,128]{2,1,0:T(8,128)S(1)} %get-tuple-element.62.refs_9_), channel_id=1, source_target_pairs={{0,8},{16,24},{32,40},{48,56},{64,72},{80,88},{96,104},{112,120},{... | collective-permute-start | bytes 1474568 | tf_op jit(solution)/shard_map/ppermute | solution.py:579
  16.0 10.5 %inner.1 = (f32[10,416,128]{2,1,0:T(8,128)S(1)}, f32[10,416,128]{2,1,0:T(8,128)S(1)}, f32[10,416,128]{2,1,0:T(8,128)S(1)}, f32[10,416,128]{2,1,0:T(8,128)S(1)}, ...) custom-call(s32[1]{0:T(128)} %bitcast.1.refs_0_, ...), custom_call_target="tpu_custom_call", output_to_operand_aliasing={{0}: (1, {}), {1}: (2, {}), {2}: (3, {}), {3}: (4, {}), {18... | custom-call | flops 100000000 | bytes 6000000 | tf_op jit(solution)/shard_map/inner/pallas_call | solution.py:619
  26.5 0.0 collective-permute-done.3.refs_25_
  26.5 0.0 collective-permute-done.2.refs_24_
  26.5 5.0 %first.1 = (f32[10,416,128]{2,1,0:T(8,128)S(1)}, f32[10,416,128]{2,1,0:T(8,128)S(1)}, f32[10,416,128]{2,1,0:T(8,128)S(1)}, f32[10,416,128]{2,1,0:T(8,128)S(1)}, ...) custom-call(s32[1]{0:T(128)} %bitcast.refs_1_.refs_0_, ...), custom_call_target="tpu_custom_call", output_to_operand_aliasing={{0}: (1, {}), {1}: (2, {}), {2}: (3, {}), {3}: (4, {}), {4}... | custom-call | tf_op jit(solution)/shard_map/first/pallas_call | solution.py:626
  31.5 21.7 %all_to_all.22 = f32[128,1,128]{2,1,0:T(1,128)S(1)} all-to-all(f32[128,1,128]{2,1,0:T(1,128)S(1)} %bitcast.12), channel_id=1, replica_groups=mesh['gx_0'=4,'gx_1'=4,'gy_0'=4,'gy_1'=2] {'gx_0','gx_1','gy_0','gy_1'}, dimensions={0} | all-to-all | bytes 131072 | tf_op jit(solution)/shard_map/all_to_all | solution.py:632
  53.2 10.9 %next.1 = (f32[10,416,128]{2,1,0:T(8,128)S(1)}, f32[10,416,128]{2,1,0:T(8,128)S(1)}, f32[10,416,128]{2,1,0:T(8,128)S(1)}, f32[10,416,128]{2,1,0:T(8,128)S(1)}, f...) custom-call(f32[10,416,128]{2,1,0:T(8,128)S(1)} %get-tuple-element.8, ...), custom_call_target="tpu_custom_call", output_to_operand_aliasing={{0}: (6, {}), {1}: (7, {}), {2}: (8, {}), {3}: (9, {}), {4}... | custom-call | tf_op jit(solution)/shard_map/next/pallas_call | solution.py:635
  64.1 13.8 %all_to_all.23 = f32[128,1,128]{2,1,0:T(1,128)S(1)} all-to-all(f32[128,1,128]{2,1,0:T(1,128)S(1)} %bitcast.13), channel_id=1, replica_groups=mesh['gx_0'=4,'gx_1'=4,'gy_0'=4,'gy_1'=2] {'gx_0','gx_1','gy_0','gy_1'}, dimensions={0} | all-to-all | bytes 131072 | tf_op jit(solution)/shard_map/all_to_all | solution.py:643
  77.9 1.8 %last.1 = (f32[10,64,512]{2,1,0:T(8,128)}, f32[10,64,512]{2,1,0:T(8,128)}) custom-call(f32[10,416,128]{2,1,0:T(8,128)S(1)} %get-tuple-element.101.refs_0_, f32[10,416,128]{2,1,0:T(8,128)S(1)} %get-tuple-element.102.refs_1_, f32[10,416,128]{2,1,0:T(8,128)S(1)} %get-tuple-element.103.refs_2_, f32[10,256,128]{2,1,0:T(8,128)S(1)} %get-tuple-element.104.refs_3_, ...), custom_call_target="tpu_custom_call" | custom-call | tf_op jit(solution)/shard_map/last/pallas_call | solution.py:646
Async XLA Ops:
  3.9 4.7 %collective-permute-start = (f32[2,64,128]{2,1,0:T(8,128)S(1)}, f32[2,64,128]{2,1,0:T(8,128)S(1)}, u32[]{:S(2)}, u32[]{:S(2)}) collective-permute-start(f32[2,64,128]{2,1,0:T(8,128)S(1)} %get-tuple-element.60), channel_id=1, source_target_pairs={{0,1},{2,3},{4,5},{6,7},{1,0},{3,2},{5,4},{7,6},{8,9},{10,11},{12,... | collective-permute-start | bytes 196616 | tf_op jit(solution)/shard_map/ppermute | solution.py:579
  5.4 5.6 %collective-permute-start.1 = (f32[2,64,128]{2,1,0:T(8,128)S(1)}, f32[2,64,128]{2,1,0:T(8,128)S(1)}, u32[]{:S(2)}, u32[]{:S(2)}) collective-permute-start(f32[2,64,128]{2,1,0:T(8,128)S(1)} %get-tuple-element.61), channel_id=1, source_target_pairs={{1,2},{3,4},{5,6},{2,1},{4,3},{6,5},{9,10},{11,12},{13,14},{10,9},... | collective-permute-start | bytes 196616 | tf_op jit(solution)/shard_map/ppermute | solution.py:579
  11.5 15.0 %collective-permute-start.3 = (f32[5,192,128]{2,1,0:T(8,128)S(1)}, f32[5,192,128]{2,1,0:T(8,128)S(1)}, u32[]{:S(2)}, u32[]{:S(2)}) collective-permute-start(f32[5,192,128]{2,1,0:T(8,128)S(1)} %get-tuple-element.86), channel_id=1, source_target_pairs={{8,16},{24,32},{40,48},{56,64},{72,80},{88,96},{104,112},{16,8},{3... | collective-permute-start | bytes 1474568 | tf_op jit(solution)/shard_map/ppermute | solution.py:579
  12.2 14.3 %collective-permute-start.2 = (f32[5,192,128]{2,1,0:T(8,128)S(1)}, f32[5,192,128]{2,1,0:T(8,128)S(1)}, u32[]{:S(2)}, u32[]{:S(2)}) collective-permute-start(f32[5,192,128]{2,1,0:T(8,128)S(1)} %get-tuple-element.62.refs_9_), channel_id=1, source_target_pairs={{0,8},{16,24},{32,40},{48,56},{64,72},{80,88},{96,104},{112,120},{... | collective-permute-start | bytes 1474568 | tf_op jit(solution)/shard_map/ppermute | solution.py:579

commit v4 on v3

--- a/solution.py
+++ b/solution.py
@@ -140,10 +140,12 @@
 STRIP_ROWS = ((0, 5), (5, 5), (10, 4), (14, 4))
 
 
-def turn_kernel(layers, par_y, par_x, p_ref, k_ref, o_ref, r_ref, act_ref, rech_ref, got_a, got_b,
-                send_a, send_b, corners, act_corner, rech_corner):
-    fields = (p_ref, k_ref, o_ref, r_ref)
+GROUPS = 12
+
+
+def turn_kernel(layers, par_y, par_x, got_a, got_b, old_a, old_b, send_a, send_b, corners, act_corner, rech_corner, flat):
     odd = par_y[0] == 1
+    flat[184:192, :] = jnp.zeros((8, 128), F32)
     for side in range(2):
         def put(f, layer, value):
             if f == 4:
@@ -156,44 +158,60 @@
         unpack_strips(layers, odd, got_a, got_b, pl.ds(56 * side, 8), put)
     for send, side in ((send_a, 1 - par_x[0]), (send_b, par_x[0])):
         first5, first4 = 3 * side, 4 * side
-        start5, start4 = TOP + 59 * side, TOP + 60 * side
 
         def fill(layer, carry):
             for f, (place, depth) in enumerate(STRIP_ROWS):
-                start, first = (start5, first5) if depth == 5 else (start4, first4)
-                rows = pl.ds(layer * 18 + place, depth)
-                for t in range(4):
-                    send[t, rows, :] = fields[f][layer, at(t, start, depth), :]
-                send[4, rows, :] = corners[f, side, layer, pl.ds(first, depth), :]
+                first = first5 if depth == 5 else first4
+                flat[pl.ds(layer * 18 + place, depth), :] = corners[f, side, layer, pl.ds(first, depth), :]
             return carry
 
         lax.fori_loop(0, layers, fill, 0)
-        for t in range(4):
-            send[t, 18 * layers:18 * layers + 5, :] = act_ref[at(t, start5, 5), :]
-            send[t, 18 * layers + 5:18 * layers + 9, :] = rech_ref[at(t, start4, 4), :]
-        send[4, 18 * layers:18 * layers + 5, :] = act_corner[side, pl.ds(first5, 5), :]
-        send[4, 18 * layers + 5:18 * layers + 9, :] = rech_corner[side, pl.ds(first4, 4), :]
-
-
-def place_strips(layers, up, refs, got_a, got_b):
+        flat[18 * layers:18 * layers + 5, :] = act_corner[side, pl.ds(first5, 5), :]
+        flat[18 * layers + 5:18 * layers + 9, :] = rech_corner[side, pl.ds(first4, 4), :]
+
+        def pack(half, carry):
+            rows = jnp.zeros((8, 128), F32)
+            for g in range(GROUPS):
+                rows = rows + pltpu.roll(flat[pl.ds(pl.multiple_of(16 * g + 8 * half, 8), 8), :], 10 * g + 5, 1)
+            send[pl.ds(pl.multiple_of(768 + 8 * half, 8), 8), :] = rows
+            return carry
+
+        lax.fori_loop(0, 2, pack, 0)
+
+
+def place_strips(layers, up, refs, got_a, got_b, flat):
     p_ref, k_ref, o_ref, r_ref, rech_ref, act_ref = refs
     fields = (p_ref, k_ref, o_ref, r_ref)
     low, high = TOP, TOP + 64
+    lane = lanes()
+    beside = (lane >= 123) | (lane < 5)
     for got, above in ((got_a, jnp.logical_not(up)), (got_b, up)):
         dst5 = jnp.where(above, high, low - 5)
         dst4 = jnp.where(above, high, low - 4)
 
+        def unpack(half, carry):
+            rows = got[pl.ds(pl.multiple_of(768 + 8 * half, 8), 8), :]
+            for g in range(GROUPS):
+                flat[pl.ds(pl.multiple_of(16 * g + 8 * half, 8), 8), :] = jnp.where(
+                    beside, pltpu.roll(rows, 123 - 10 * g, 1), 0.0)
+            return carry
+
+        lax.fori_loop(0, 2, unpack, 0)
+
         def fill(layer, carry):
             for (place, depth), ref in zip(STRIP_ROWS, fields):
                 start = dst5 if depth == 5 else dst4
-                for t in range(NT):
-                    ref[layer, at(t, start, depth), :] = got[t, pl.ds(layer * 18 + place, depth), :]
+                for t in range(4):
+                    ref[layer, at(t, start, depth), :] = got[pl.ds(192 * t + layer * 18 + place, depth), :]
+                ref[layer, at(4, start, depth), :] = flat[pl.ds(layer * 18 + place, depth), :]
             return carry
 
         lax.fori_loop(0, layers, fill, 0)
         for t in range(NT):
-            act_ref[at(t, dst5, 5), :] = got[t, 18 * layers:18 * layers + 5, :]
-            rech_ref[at(t, dst4, 4), :] = got[t, 18 * layers + 5:18 * layers + 9, :]
+            rows = flat if t == 4 else got
+            first = (0 if t == 4 else 192 * t) + 18 * layers
+            act_ref[at(t, dst5, 5), :] = rows[first:first + 5, :]
+            rech_ref[at(t, dst4, 4), :] = rows[first + 5:first + 9, :]
 
 
 def sigmoid_tile(value, layer, t, start, sig_ref, mob_ref, der_ref):
@@ -214,17 +232,22 @@
 
 
 def over_layers(layers, one_layer, carry):
-    if layers % 2:
-        return lax.fori_loop(0, layers, one_layer, carry)
-    return lax.fori_loop(0, layers // 2, lambda i, c: one_layer(2 * i + 1, one_layer(2 * i, c)), carry)
-
-
-def far_faces(layers, starts, s, make_trans):
+    trip = 5 if layers % 5 == 0 else 1
+
+    def several(i, carry):
+        for layer in range(trip):
+            carry = one_layer(trip * i + layer, carry)
+        return carry
+
+    return lax.fori_loop(0, layers // trip, several, carry)
+
+
+def far_faces(layers, starts, s, make_trans, tiles=range(NT)):
     def one_layer(layer, carry):
         upper = jnp.minimum(layer + 1, layers - 1)
         inner = jnp.where(layer + 1 < layers, 1.0, 0.0).astype(F32)
         for start in starts:
-            for t in range(NT):
+            for t in tiles:
                 here = at(t, start)
                 if make_trans:
                     trans = s.ax[here, :] * (tile_of(s.k, layer, t, start) + tile_of(s.k, layer, t, start + 1))
@@ -402,7 +425,7 @@
 
 STATE = ("p", "k", "s0", "ap", "tx", "ty", "tz", "q", "w")
 COEFS = ("c", "xa", "xb", "ya", "yb", "za", "zb", "xf", "zf")
-POINT = ("sig", "m", "s", "yf")
+POINT = ("sig", "m", "s")
 TALL = ("za", "zb", "zf")
 PLANES = ("act", "rech", "ax", "ay")
 
@@ -422,20 +445,25 @@
     lax.fori_loop(0, SPAN // 8, clear, 0)
 
 
-def mask_pairs(s, starts):
+def mask_pairs_x(s, starts, tiles=range(NT)):
+    for start in starts:
+        for t in tiles:
+            s.ax[at(t, start), :] = 0.5 * s.act[at(t, start), :] * s.act[at(t, start + 1), :]
+
+
+def mask_pairs_y(s, starts):
     for start in starts:
         act = flat_tiles(s.act, start)
         north = from_north(act)
         for t in range(NT):
-            s.ax[at(t, start), :] = 0.5 * act[t] * s.act[at(t, start + 1), :]
             s.ay[at(t, start), :] = 0.5 * act[t] * north[t]
 
 
-def points(layers, s, new, old):
+def points(layers, s, new, old, tiles=range(NT)):
     def point(layer, carry):
         top = jnp.where(layer == layers - 1, 1.0, 0.0).astype(F32)
         for start in (*new, *old):
-            for t in range(NT):
+            for t in tiles:
                 sigmoid_tile(tile_of(s.p, layer, t, start), layer, t, start, s.sig, s.m, s.s)
                 if start in new:
                     act = s.act[at(t, start), :]
@@ -448,13 +476,42 @@
     lax.fori_loop(0, layers, point, 0)
 
 
-def inner_kernel(layers, par_y, p_old, k_old, o_old, r_old, act_old, rech_old, got_a, got_b, after, *refs):
-    names = STATE + COEFS + PLANES
+OWN_ROWS = range(TOP, TOP + 64, 8)
+FACE_ROWS = (*range(TOP, TOP + 56, 8), TOP + 55)
+
+
+def before_kernel(layers, par_x, p_old, k_old, o_old, r_old, act_old, rech_old, *refs):
+    names = STATE + COEFS + PLANES + POINT
     s = Refs(**dict(zip(names, refs)))
-    part_ref, s.sig, s.m, s.s, s.yf = refs[len(names):]
+    send_a, send_b = refs[len(names):]
+    fields = (s.p, s.k, s.s0, s.ap)
+    for send, side in ((send_a, 1 - par_x[0]), (send_b, par_x[0])):
+        start5, start4 = TOP + 59 * side, TOP + 60 * side
+
+        def fill(layer, carry):
+            for f, (place, depth) in enumerate(STRIP_ROWS):
+                start = start5 if depth == 5 else start4
+                for t in range(4):
+                    send[pl.ds(192 * t + layer * 18 + place, depth), :] = fields[f][layer, at(t, start, depth), :]
+            return carry
+
+        lax.fori_loop(0, layers, fill, 0)
+        for t in range(4):
+            send[pl.ds(192 * t + 18 * layers, 5), :] = s.act[at(t, start5, 5), :]
+            send[pl.ds(192 * t + 18 * layers + 5, 4), :] = s.rech[at(t, start4, 4), :]
+    clear_bottom(s)
+    points(layers, s, OWN_ROWS, (), range(4))
+    mask_pairs_x(s, FACE_ROWS, range(4))
+    far_faces(layers, FACE_ROWS, s, True, range(4))
+
+
+def inner_kernel(layers, par_y, got_a, got_b, after, *refs):
+    names = STATE + COEFS + PLANES + POINT
+    refs = refs[len(names):]
+    s = Refs(**dict(zip(names, refs)))
+    part_ref, s.yf = refs[len(names):]
     zero = jnp.zeros((8, 128), F32)
     fields = (s.p, s.k, s.s0, s.ap)
-    clear_bottom(s)
     odd = par_y[0] == 1
 
     def unpack(row, carry):
@@ -472,39 +529,41 @@
         return carry
 
     lax.fori_loop(0, 8, unpack, 0)
-    points(layers, s, range(8, 72, 8), ())
-    mask_pairs(s, (*range(8, 64, 8), 63))
-    far_faces(layers, (*range(8, 64, 8), 63), s, True)
+    points(layers, s, OWN_ROWS, (), (4,))
+    mask_pairs_x(s, FACE_ROWS, (4,))
+    mask_pairs_y(s, FACE_ROWS)
+    far_faces(layers, FACE_ROWS, s, True, (4,))
     y_faces(layers, range(12, 68, 8), s, True)
     assemble(layers, range(12, 68, 8), s)
-    first_product(layers, range(20, 60, 8), s)
-    sums = second_product(layers, range(24, 56, 8), s, (zero,) * 6, None)
+    first_product(layers, (13, 21, 29, 37, 45, 53, 59), s)
+    sums = second_product(layers, range(16, 64, 8), s, (zero,) * 6, None)
     for i in range(6):
         part_ref[i] = sums[i]
 
 
 def first_kernel(layers, par_x, *refs):
-    names = STATE + COEFS + PLANES
+    names = STATE + COEFS + PLANES + POINT
     count = len(names)
     part_ref, got_a, got_b = refs[count:count + 3]
     refs = refs[count + 3:]
     s = Refs(**dict(zip(names, refs)))
     sums_ref = refs[count]
-    s.sig, s.m, s.s, s.yf = refs[count + 1:]
-    place_strips(layers, par_x[0] == 1, (s.p, s.k, s.s0, s.ap, s.rech, s.act), got_a, got_b)
+    s.yf, flat = refs[count + 1:]
+    place_strips(layers, par_x[0] == 1, (s.p, s.k, s.s0, s.ap, s.rech, s.act), got_a, got_b, flat)
     points(layers, s, (0, 72), (8, 64))
-    mask_pairs(s, (0, 4, 64, 68))
+    mask_pairs_x(s, (0, 4, 64, 68))
+    mask_pairs_y(s, (0, 4, 64, 68))
     far_faces(layers, (0, 64, 68), s, True)
     y_faces(layers, (4, 68), s, True)
     assemble(layers, (4, 68), s)
-    first_product(layers, (4, 12, 60, 68), s)
-    sums = second_product(layers, (8, 16, 56, 64), s, tuple(part_ref[i] for i in range(6)), None)
+    first_product(layers, (5, 67), s)
+    sums = second_product(layers, (8, 64), s, tuple(part_ref[i] for i in range(6)), None)
     put_sums(sums, sums_ref)
 
 
 KEPT = ("s0", "ap", "tx", "ty", "tz", "act")
-SHARED = 4
-MOVED = ("p", "q", "w") + COEFS[:SHARED]
+SHARED = 8
+MOVED = ("p", "q", "w") + POINT + COEFS[:SHARED]
 
 
 def next_kernel(layers, *refs):
@@ -512,7 +571,7 @@
     got_ref, *refs = refs
     s = Refs(**dict(zip(KEPT, kept)), **dict(zip(MOVED, refs)))
     z_ref, sums_ref, *own = refs[len(MOVED):]
-    for name, ref in zip(COEFS[SHARED:] + POINT, own):
+    for name, ref in zip(COEFS[SHARED:] + ("yf",), own):
         setattr(s, name, ref)
     p_ref, q_ref, w_ref = s.p, s.q, s.w
     a, b = step_weights(got_ref)
@@ -529,8 +588,8 @@
         return carry
 
     lax.fori_loop(0, layers, point, 0)
-    starts = range(4, 76, 8)
-    far_faces(layers, (0, *starts), s, False)
+    far_faces(layers, range(5, 77, 8), s, False)
+    starts = range(6, 78, 8)
     y_faces(layers, starts, s, False)
     assemble(layers, starts, s)
     first_product(layers, starts, s)
@@ -593,7 +652,8 @@
     inputs = outside(pressure, conductivity, pressure_old, porosity, active, recharge)
     dma = pltpu.SemaphoreType.DMA
     strip_y = pltpu.VMEM((2, 64, 128), F32)
-    strip_x = pltpu.VMEM((NT, 192, 128), F32)
+    strip_x = pltpu.VMEM((784, 128), F32)
+    rows_x = pltpu.VMEM((192, 128), F32)
     plane = pltpu.VMEM((SPAN, 128), F32)
     part = pltpu.VMEM((8, 8, 128), F32)
     block = jax.ShapeDtypeStruct((128, 128), F32)
@@ -605,39 +665,47 @@
     )(par_y, par_x, *inputs)
     y_a = swap(send_a, GY, 0)
     y_b = swap(send_b, GY, 1)
+    state = tuple(space(layers, name) for name in STATE + COEFS) + (plane,) * 4 + tuple(space(layers, n) for n in POINT)
+    count = len(state)
+    act_at = len(STATE + COEFS)
+    flow = space(layers, "yf")
+    *fields, send_a, send_b = pl.pallas_call(
+        bound(before_kernel, layers), name="before", out_shape=state + (strip_x,) * 2,
+        in_specs=[SM] + [VM] * 6, out_specs=(VM,) * (count + 2),
+        input_output_aliases={1: 0, 2: 1, 3: 2, 4: 3, 5: act_at, 6: act_at + 1}, compiler_params=grant(GRANT),
+        cost_estimate=pl.CostEstimate(flops=20_000_000, transcendentals=0, bytes_accessed=6_000_000),
+    )(par_x, *keep(*fields))
     send_a, send_b = pl.pallas_call(
-        bound(turn_kernel, layers), name="turn", out_shape=(strip_x,) * 2, in_specs=[SM] * 2 + [VM] * 8,
-        out_specs=(VM,) * 2,
+        bound(turn_kernel, layers), name="turn", out_shape=(strip_x,) * 2, in_specs=[SM] * 2 + [VM] * 4,
+        out_specs=(VM,) * 2, input_output_aliases={4: 0, 5: 1},
         scratch_shapes=[pltpu.VMEM((4, 2, layers, 8, 128), F32), pltpu.VMEM((2, 8, 128), F32),
-                        pltpu.VMEM((2, 8, 128), F32)],
+                        pltpu.VMEM((2, 8, 128), F32), rows_x],
         compiler_params=grant(GRANT),
-    )(par_y, par_x, *keep(*fields), y_a, y_b)
+    )(par_y, par_x, y_a, y_b, *keep(send_a, send_b))
     x_a = swap(send_a, GX, 0)
     x_b = swap(send_b, GX, 1)
-    state = tuple(space(layers, name) for name in STATE + COEFS) + (plane,) * 4
-    points_scratch = [space(layers, name) for name in POINT]
     *fields, part_sums = pl.pallas_call(
         bound(inner_kernel, layers), name="inner", out_shape=state + (part,),
-        in_specs=[SM] + [VM] * 9, out_specs=(VM,) * (len(state) + 1),
-        input_output_aliases={1: 0, 2: 1, 3: 2, 4: 3, 5: len(state) - 4, 6: len(state) - 3},
-        scratch_shapes=points_scratch, compiler_params=grant(GRANT),
+        in_specs=[SM] + [VM] * (3 + count), out_specs=(VM,) * (count + 1),
+        input_output_aliases={i + 4: i for i in range(count)},
+        scratch_shapes=[flow], compiler_params=grant(GRANT),
         cost_estimate=pl.CostEstimate(flops=100_000_000, transcendentals=0, bytes_accessed=6_000_000),
-    )(par_y, *keep(*fields), y_a, y_b, send_a)
+    )(par_y, y_a, y_b, send_a, *keep(*fields))
     *fields, sums = pl.pallas_call(
         bound(first_kernel, layers), name="first", out_shape=state + (block,),
-        in_specs=[SM] + [VM] * (len(state) + 3), out_specs=(VM,) * (len(state) + 1),
-        input_output_aliases={i + 1: i for i in range(len(state))},
-        scratch_shapes=points_scratch, compiler_params=grant(GRANT),
+        in_specs=[SM] + [VM] * (count + 3), out_specs=(VM,) * (count + 1),
+        input_output_aliases={i + 1: i for i in range(count)},
+        scratch_shapes=[flow, rows_x], compiler_params=grant(GRANT),
     )(par_x, *keep(*fields, part_sums), x_a, x_b)
     sums = lax.all_to_all(sums, ALL, 0, 0, tiled=True)
-    named = dict(zip(STATE + COEFS + PLANES, fields))
+    named = dict(zip(STATE + COEFS + PLANES + POINT, fields))
     moved = tuple(space(layers, name) for name in MOVED)
     p, q, w, *rest = pl.pallas_call(
         bound(next_kernel, layers), name="next",
         out_shape=moved + (pltpu.VMEM((layers, 256, 128), F32), block),
         in_specs=[VM] * (len(KEPT) + len(MOVED) + 1), out_specs=(VM,) * (len(MOVED) + 2),
         input_output_aliases={len(KEPT) + i: i for i in range(len(MOVED))},
-        scratch_shapes=[space(layers, name) for name in COEFS[SHARED:] + POINT], compiler_params=grant(GRANT2),
+        scratch_shapes=[space(layers, name) for name in COEFS[SHARED:] + ("yf",)], compiler_params=grant(GRANT2),
     )(*keep(*(named[n] for n in KEPT + MOVED)), sums)
     z, sums = rest[-2:]
     sums = lax.all_to_all(sums, ALL, 0, 0, tiled=True)
@@ -649,8 +717,8 @@
     )(*keep(p, q, w, z), sums)
 
 
-GRANT = 12
-GRANT2 = 22
+GRANT = 6
+GRANT2 = 8
 
 
 def solution(mesh):

time: 80 us -> 75.5 us (0.944)
  Pallas kernels: 32 us -> 29.3 us
  waiting for transfers between devices: 2.35 us -> 0.01 us
    pallas_call x1, Pallas kernels: 10.5 us -> 7.77 us  [body(): pl.pallas_call(bound(inner_kernel, layers), name='inner', out_shape=state...]
    pallas_call x0 -> x1, Pallas kernels: none -> 2.49 us  [body(): pl.pallas_call(bound(before_kernel, layers), name='before', out_shape=sta...]
    ppermute x4, waiting for transfers between devices: 2.35 us -> 0.01 us  [swap(): return lax.ppermute(value, axes, pairs + [(b, a) for a, b in pairs])]
    pallas_call x1, Pallas kernels: 10.9 us -> 9.31 us  [body(): pl.pallas_call(bound(next_kernel, layers), name='next', out_shape=moved +...]
    pallas_call x1, Pallas kernels: 5.04 us -> 3.91 us  [body(): pl.pallas_call(bound(first_kernel, layers), name='first', out_shape=state...]
  transfers between devices with their start and end apart: 4 -> 4, of which waited for: 1 -> 0; matrix products, arithmetic and copies ran while one was open for 0% -> 0% of each run, Pallas kernels for 13% -> 14%
where the time goes in v4:
time: 75.5 us; the launch traced here: 75.4 us
  blocking collectives  36.2 us (48%)
  Pallas kernels  29.3 us (39%)
  starting transfers between devices  9.09 us (12%)
    all_to_all x2, blocking collectives, body(): sums = lax.all_to_all(sums, ALL, 0, 0, tiled=True)  36.2 us
    pallas_call x1, Pallas kernels, body(): pl.pallas_call(bound(next_kernel, layers), name='next', out_shape=moved +...  9.31 us
    ppermute x4, starting transfers between devices, swap(): return lax.ppermute(value, axes, pairs + [(b, a) for a, b in pairs])  9.09 us
    pallas_call x1, Pallas kernels, body(): pl.pallas_call(bound(inner_kernel, layers), name='inner', out_shape=state...  7.77 us
    pallas_call x1, Pallas kernels, body(): pl.pallas_call(bound(first_kernel, layers), name='first', out_shape=state...  3.91 us
    pallas_call x1, Pallas kernels, body(): pl.pallas_call(bound(edge_kernel, layers), name='edge', out_shape=loaded...  3.25 us
    pallas_call x1, Pallas kernels, body(): pl.pallas_call(bound(before_kernel, layers), name='before', out_shape=sta...  2.49 us
    pallas_call x1, Pallas kernels, body(): pl.pallas_call(bound(last_kernel, layers), name='last', out_shape=(out, o...  1.84 us
  transfers between devices with their start and end apart: 4, of which 0 were waited for; matrix products, arithmetic and copies ran while one was open for 0% of the time, Pallas kernels for 14%

profile of v4, /device:TPU:1, one launch (start us, length us, event | category | flops | bytes accessed | tf_op | source)
XLA Modules:
  0.0 75.4 jit_solution(559372501314544017)
XLA Ops:
  0.6 3.2 %edge.1 = (f32[10,416,128]{2,1,0:T(8,128)S(1)}, f32[10,416,128]{2,1,0:T(8,128)S(1)}, f32[10,416,128]{2,1,0:T(8,128)S(1)}, f32[10,416,128]{2,1,0:T(8,128)S(1)}, f...) custom-call(s32[1]{0:T(128)} %bitcast.1.refs_0_, ...), custom_call_target="tpu_custom_call" | custom-call | tf_op jit(solution)/shard_map/edge/pallas_call | solution.py:661
  3.9 1.5 %collective-permute-start = (f32[2,64,128]{2,1,0:T(8,128)S(1)}, f32[2,64,128]{2,1,0:T(8,128)S(1)}, u32[]{:S(2)}, u32[]{:S(2)}) collective-permute-start(f32[2,64,128]{2,1,0:T(8,128)S(1)} %get-tuple-element.91), channel_id=1, source_target_pairs={{0,1},{2,3},{4,5},{6,7},{1,0},{3,2},{5,4},{7,6},{8,9},{10,11},{12,... | collective-permute-start | bytes 196616 | tf_op jit(solution)/shard_map/ppermute | solution.py:638
  5.4 3.2 %collective-permute-start.1 = (f32[2,64,128]{2,1,0:T(8,128)S(1)}, f32[2,64,128]{2,1,0:T(8,128)S(1)}, u32[]{:S(2)}, u32[]{:S(2)}) collective-permute-start(f32[2,64,128]{2,1,0:T(8,128)S(1)} %get-tuple-element.92), channel_id=1, source_target_pairs={{1,2},{3,4},{5,6},{2,1},{4,3},{6,5},{9,10},{11,12},{13,14},{10,9},... | collective-permute-start | bytes 196616 | tf_op jit(solution)/shard_map/ppermute | solution.py:638
  8.6 2.5 %before.1 = (f32[10,416,128]{2,1,0:T(8,128)S(1)}, f32[10,416,128]{2,1,0:T(8,128)S(1)}, f32[10,416,128]{2,1,0:T(8,128)S(1)}, f32[10,416,128]{2,1,0:T(8,128)S(1)},...) custom-call(s32[1]{0:T(128)} %bitcast.refs_1_.refs_0_, ...), custom_call_target="tpu_custom_call", output_to_operand_aliasing={{0}: (1, {}), {1}: (2, {}), {2}: (3, {}), {3}: (4, {}), {18... | custom-call | flops 20000000 | bytes 6000000 | tf_op jit(solution)/shard_map/before/pallas_call | solution.py:672
  11.1 0.0 collective-permute-done.refs_2_.refs_1_
  11.1 0.0 collective-permute-done.1.refs_3_.refs_2_
  11.1 0.7 turn.1
  11.8 0.7 collective-permute-start.3
  12.5 3.7 %collective-permute-start.2 = (f32[784,128]{1,0:T(8,128)S(1)}, f32[784,128]{1,0:T(8,128)S(1)}, u32[]{:S(2)}, u32[]{:S(2)}) collective-permute-start(f32[784,128]{1,0:T(8,128)S(1)} %get-tuple-element.101.refs_3_), channel_id=1, source_target_pairs={{0,8},{16,24},{32,40},{48,56},{64,72},{80,88},{96,104},{112,120},{... | collective-permute-start | bytes 1204232 | tf_op jit(solution)/shard_map/ppermute | solution.py:638
  16.2 7.8 %inner.1 = (f32[10,416,128]{2,1,0:T(8,128)S(1)}, f32[10,416,128]{2,1,0:T(8,128)S(1)}, f32[10,416,128]{2,1,0:T(8,128)S(1)}, f32[10,416,128]{2,1,0:T(8,128)S(1)}, ...) custom-call(s32[1]{0:T(128)} %bitcast.1.refs_0_, ...), custom_call_target="tpu_custom_call", output_to_operand_aliasing={{0}: (4, {}), {1}: (5, {}), {2}: (6, {}), {3}: (7, {}), {4}... | custom-call | flops 100000000 | bytes 6000000 | tf_op jit(solution)/shard_map/inner/pallas_call | solution.py:687
  24.0 0.0 collective-permute-done.3.refs_28_
  24.0 0.0 collective-permute-done.2.refs_27_
  24.0 3.9 %first.1 = (f32[10,416,128]{2,1,0:T(8,128)S(1)}, f32[10,416,128]{2,1,0:T(8,128)S(1)}, f32[10,416,128]{2,1,0:T(8,128)S(1)}, f32[10,416,128]{2,1,0:T(8,128)S(1)}, ...) custom-call(s32[1]{0:T(128)} %bitcast.refs_1_.refs_0_, ...), custom_call_target="tpu_custom_call", output_to_operand_aliasing={{0}: (1, {}), {1}: (2, {}), {2}: (3, {}), {3}: (4, {}), {4}... | custom-call | tf_op jit(solution)/shard_map/first/pallas_call | solution.py:694
  28.0 22.4 %all_to_all.22 = f32[128,1,128]{2,1,0:T(1,128)S(1)} all-to-all(f32[128,1,128]{2,1,0:T(1,128)S(1)} %bitcast.12), channel_id=1, replica_groups=mesh['gx_0'=4,'gx_1'=4,'gy_0'=4,'gy_1'=2] {'gx_0','gx_1','gy_0','gy_1'}, dimensions={0} | all-to-all | bytes 131072 | tf_op jit(solution)/shard_map/all_to_all | solution.py:700
  50.4 9.3 %next.1 = (f32[10,416,128]{2,1,0:T(8,128)S(1)}, f32[10,416,128]{2,1,0:T(8,128)S(1)}, f32[10,416,128]{2,1,0:T(8,128)S(1)}, f32[10,416,128]{2,1,0:T(8,128)S(1)}, f...) custom-call(f32[10,416,128]{2,1,0:T(8,128)S(1)} %get-tuple-element.1, ...), custom_call_target="tpu_custom_call", output_to_operand_aliasing={{0}: (6, {}), {1}: (7, {}), {2}: (8, {}), {3}: (9, {}), {4}... | custom-call | tf_op jit(solution)/shard_map/next/pallas_call | solution.py:703
  59.7 13.8 %all_to_all.23 = f32[128,1,128]{2,1,0:T(1,128)S(1)} all-to-all(f32[128,1,128]{2,1,0:T(1,128)S(1)} %bitcast.13), channel_id=1, replica_groups=mesh['gx_0'=4,'gx_1'=4,'gy_0'=4,'gy_1'=2] {'gx_0','gx_1','gy_0','gy_1'}, dimensions={0} | all-to-all | bytes 131072 | tf_op jit(solution)/shard_map/all_to_all | solution.py:711
  73.5 1.8 %last.1 = (f32[10,64,512]{2,1,0:T(8,128)}, f32[10,64,512]{2,1,0:T(8,128)}) custom-call(f32[10,416,128]{2,1,0:T(8,128)S(1)} %get-tuple-element.175.refs_0_, f32[10,416,128]{2,1,0:T(8,128)S(1)} %get-tuple-element.176.refs_1_, f32[10,416,128]{2,1,0:T(8,128)S(1)} %get-tuple-element.177.refs_2_, f32[10,256,128]{2,1,0:T(8,128)S(1)} %get-tuple-element.178.refs_3_, ...), custom_call_target="tpu_custom_call" | custom-call | tf_op jit(solution)/shard_map/last/pallas_call | solution.py:714
Async XLA Ops:
  3.9 7.2 %collective-permute-start = (f32[2,64,128]{2,1,0:T(8,128)S(1)}, f32[2,64,128]{2,1,0:T(8,128)S(1)}, u32[]{:S(2)}, u32[]{:S(2)}) collective-permute-start(f32[2,64,128]{2,1,0:T(8,128)S(1)} %get-tuple-element.91), channel_id=1, source_target_pairs={{0,1},{2,3},{4,5},{6,7},{1,0},{3,2},{5,4},{7,6},{8,9},{10,11},{12,... | collective-permute-start | bytes 196616 | tf_op jit(solution)/shard_map/ppermute | solution.py:638
  5.4 5.7 %collective-permute-start.1 = (f32[2,64,128]{2,1,0:T(8,128)S(1)}, f32[2,64,128]{2,1,0:T(8,128)S(1)}, u32[]{:S(2)}, u32[]{:S(2)}) collective-permute-start(f32[2,64,128]{2,1,0:T(8,128)S(1)} %get-tuple-element.92), channel_id=1, source_target_pairs={{1,2},{3,4},{5,6},{2,1},{4,3},{6,5},{9,10},{11,12},{13,14},{10,9},... | collective-permute-start | bytes 196616 | tf_op jit(solution)/shard_map/ppermute | solution.py:638
  11.8 12.2 %collective-permute-start.3 = (f32[784,128]{1,0:T(8,128)S(1)}, f32[784,128]{1,0:T(8,128)S(1)}, u32[]{:S(2)}, u32[]{:S(2)}) collective-permute-start(f32[784,128]{1,0:T(8,128)S(1)} %get-tuple-element.153), channel_id=1, source_target_pairs={{8,16},{24,32},{40,48},{56,64},{72,80},{88,96},{104,112},{16,8},{3... | collective-permute-start | bytes 1204232 | tf_op jit(solution)/shard_map/ppermute | solution.py:638
  12.5 11.5 %collective-permute-start.2 = (f32[784,128]{1,0:T(8,128)S(1)}, f32[784,128]{1,0:T(8,128)S(1)}, u32[]{:S(2)}, u32[]{:S(2)}) collective-permute-start(f32[784,128]{1,0:T(8,128)S(1)} %get-tuple-element.101.refs_3_), channel_id=1, source_target_pairs={{0,8},{16,24},{32,40},{48,56},{64,72},{80,88},{96,104},{112,120},{... | collective-permute-start | bytes 1204232 | tf_op jit(solution)/shard_map/ppermute | solution.py:638

commit v5 on v4

--- a/solution.py
+++ b/solution.py
@@ -63,7 +63,7 @@
                 p_ref, k_ref, o_ref, r_ref, act_ref, rech_ref, send_a, send_b, act_int, sems):
     fields = (p_ref, k_ref, o_ref, r_ref)
     copies = []
-    for t in (0, 3, 1, 2):
+    for t in (0, 3):
         cols = pl.ds(128 * t, 128)
         own = at(t, TOP, 64)
         for f, (src, dst) in enumerate(zip((p_in, k_in, o_in, r_in), fields)):
@@ -86,7 +86,7 @@
         for t in range(NT):
             ref[at(t, 0), :] = zero
             ref[at(t, ROWS - 8), :] = zero
-    for copy in copies[:12]:
+    for copy in copies:
         copy.wait()
     first = lanes() < 5
     last = lanes() >= 123
@@ -116,9 +116,7 @@
         return carry
 
     lax.fori_loop(0, 8, pack, 0)
-    for copy in copies[12:]:
-        copy.wait()
-    for t in range(4):
+    for t in (0, 3):
         act_ref[at(t, TOP, 64), :] = act_int[t].astype(F32)
 
 
@@ -480,29 +478,49 @@
 FACE_ROWS = (*range(TOP, TOP + 56, 8), TOP + 55)
 
 
-def before_kernel(layers, par_x, p_old, k_old, o_old, r_old, act_old, rech_old, *refs):
+def before_kernel(layers, par_x, p_in, k_in, o_in, r_in, act_in, rech_in, p_old, k_old, o_old, r_old, act_old, rech_old, *refs):
     names = STATE + COEFS + PLANES + POINT
     s = Refs(**dict(zip(names, refs)))
-    send_a, send_b = refs[len(names):]
+    send_a, send_b, act_int, sems = refs[len(names):]
     fields = (s.p, s.k, s.s0, s.ap)
-    for send, side in ((send_a, 1 - par_x[0]), (send_b, par_x[0])):
-        start5, start4 = TOP + 59 * side, TOP + 60 * side
-
-        def fill(layer, carry):
-            for f, (place, depth) in enumerate(STRIP_ROWS):
-                start = start5 if depth == 5 else start4
-                for t in range(4):
-                    send[pl.ds(192 * t + layer * 18 + place, depth), :] = fields[f][layer, at(t, start, depth), :]
-            return carry
-
-        lax.fori_loop(0, layers, fill, 0)
-        for t in range(4):
-            send[pl.ds(192 * t + 18 * layers, 5), :] = s.act[at(t, start5, 5), :]
-            send[pl.ds(192 * t + 18 * layers + 5, 4), :] = s.rech[at(t, start4, 4), :]
+    copies = []
+    for t in (1, 2):
+        cols = pl.ds(128 * t, 128)
+        own = at(t, TOP, 64)
+        for f, (src, dst) in enumerate(zip((p_in, k_in, o_in, r_in), fields)):
+            copies.append(pltpu.make_async_copy(src.at[:, :, cols], dst.at[:, own, :], sems.at[t - 1, f]))
+        copies.append(pltpu.make_async_copy(act_in.at[:, cols], act_int.at[t - 1], sems.at[t - 1, 4]))
+        copies.append(pltpu.make_async_copy(rech_in.at[:, cols], s.rech.at[own, :], sems.at[t - 1, 5]))
+    for copy in copies:
+        copy.start()
     clear_bottom(s)
-    points(layers, s, OWN_ROWS, (), range(4))
-    mask_pairs_x(s, FACE_ROWS, range(4))
-    far_faces(layers, FACE_ROWS, s, True, range(4))
+
+    def pack(tiles):
+        for send, side in ((send_a, 1 - par_x[0]), (send_b, par_x[0])):
+            start5, start4 = TOP + 59 * side, TOP + 60 * side
+
+            def fill(layer, carry):
+                for f, (place, depth) in enumerate(STRIP_ROWS):
+                    start = start5 if depth == 5 else start4
+                    for t in tiles:
+                        send[pl.ds(192 * t + layer * 18 + place, depth), :] = fields[f][layer, at(t, start, depth), :]
+                return carry
+
+            lax.fori_loop(0, layers, fill, 0)
+            for t in tiles:
+                send[pl.ds(192 * t + 18 * layers, 5), :] = s.act[at(t, start5, 5), :]
+                send[pl.ds(192 * t + 18 * layers + 5, 4), :] = s.rech[at(t, start4, 4), :]
+
+    for tiles in ((0, 3), (1, 2)):
+        if tiles == (1, 2):
+            for copy in copies:
+                copy.wait()
+            for t in tiles:
+                s.act[at(t, TOP, 64), :] = act_int[t - 1].astype(F32)
+        pack(tiles)
+        points(layers, s, OWN_ROWS, (), tiles)
+        mask_pairs_x(s, FACE_ROWS, tiles)
+        far_faces(layers, FACE_ROWS, s, True, tiles)
 
 
 def inner_kernel(layers, par_y, got_a, got_b, after, *refs):
@@ -671,10 +689,11 @@
     flow = space(layers, "yf")
     *fields, send_a, send_b = pl.pallas_call(
         bound(before_kernel, layers), name="before", out_shape=state + (strip_x,) * 2,
-        in_specs=[SM] + [VM] * 6, out_specs=(VM,) * (count + 2),
-        input_output_aliases={1: 0, 2: 1, 3: 2, 4: 3, 5: act_at, 6: act_at + 1}, compiler_params=grant(GRANT),
+        in_specs=[SM] + [HB] * 6 + [VM] * 6, out_specs=(VM,) * (count + 2),
+        input_output_aliases={7: 0, 8: 1, 9: 2, 10: 3, 11: act_at, 12: act_at + 1},
+        scratch_shapes=[pltpu.VMEM((2, 64, 128), jnp.int32), dma((2, 6))], compiler_params=grant(GRANT),
         cost_estimate=pl.CostEstimate(flops=20_000_000, transcendentals=0, bytes_accessed=6_000_000),
-    )(par_x, *keep(*fields))
+    )(par_x, *inputs, *keep(*fields))
     send_a, send_b = pl.pallas_call(
         bound(turn_kernel, layers), name="turn", out_shape=(strip_x,) * 2, in_specs=[SM] * 2 + [VM] * 4,
         out_specs=(VM,) * 2, input_output_aliases={4: 0, 5: 1},

time: 75.5 us -> 76 us (level)
  no operation moved by 1% of the time
where the time goes in v5:
time: 76 us; the launch traced here: 75.8 us
  blocking collectives  36 us (47%)
  Pallas kernels  30 us (39%)
  starting transfers between devices  9.09 us (12%)
    all_to_all x2, blocking collectives, body(): sums = lax.all_to_all(sums, ALL, 0, 0, tiled=True)  36 us
    pallas_call x1, Pallas kernels, body(): pl.pallas_call(bound(next_kernel, layers), name='next', out_shape=moved +...  9.33 us
    ppermute x4, starting transfers between devices, swap(): return lax.ppermute(value, axes, pairs + [(b, a) for a, b in pairs])  9.09 us
    pallas_call x1, Pallas kernels, body(): pl.pallas_call(bound(inner_kernel, layers), name='inner', out_shape=state...  7.77 us
    pallas_call x1, Pallas kernels, body(): pl.pallas_call(bound(first_kernel, layers), name='first', out_shape=state...  3.9 us
    pallas_call x1, Pallas kernels, body(): pl.pallas_call(bound(edge_kernel, layers), name='edge', out_shape=loaded...  3.22 us
    pallas_call x1, Pallas kernels, body(): pl.pallas_call(bound(before_kernel, layers), name='before', out_shape=sta...  3.18 us
    pallas_call x1, Pallas kernels, body(): pl.pallas_call(bound(last_kernel, layers), name='last', out_shape=(out, o...  1.84 us
  transfers between devices with their start and end apart: 4, of which 0 were waited for; matrix products, arithmetic and copies ran while one was open for 0% of the time, Pallas kernels for 14%

profile of v5, /device:TPU:1, one launch (start us, length us, event | category | flops | bytes accessed | tf_op | source)
XLA Modules:
  0.0 75.8 jit_solution(166301807738513261)
XLA Ops:
  0.6 3.2 %edge.1 = (f32[10,416,128]{2,1,0:T(8,128)S(1)}, f32[10,416,128]{2,1,0:T(8,128)S(1)}, f32[10,416,128]{2,1,0:T(8,128)S(1)}, f32[10,416,128]{2,1,0:T(8,128)S(1)}, f...) custom-call(s32[1]{0:T(128)} %bitcast.1.refs_0_, ...), custom_call_target="tpu_custom_call" | custom-call | tf_op jit(solution)/shard_map/edge/pallas_call | solution.py:679
  3.9 1.5 %collective-permute-start = (f32[2,64,128]{2,1,0:T(8,128)S(1)}, f32[2,64,128]{2,1,0:T(8,128)S(1)}, u32[]{:S(2)}, u32[]{:S(2)}) collective-permute-start(f32[2,64,128]{2,1,0:T(8,128)S(1)} %get-tuple-element.91), channel_id=1, source_target_pairs={{0,1},{2,3},{4,5},{6,7},{1,0},{3,2},{5,4},{7,6},{8,9},{10,11},{12,... | collective-permute-start | bytes 196616 | tf_op jit(solution)/shard_map/ppermute | solution.py:656
  5.3 3.2 %collective-permute-start.1 = (f32[2,64,128]{2,1,0:T(8,128)S(1)}, f32[2,64,128]{2,1,0:T(8,128)S(1)}, u32[]{:S(2)}, u32[]{:S(2)}) collective-permute-start(f32[2,64,128]{2,1,0:T(8,128)S(1)} %get-tuple-element.92), channel_id=1, source_target_pairs={{1,2},{3,4},{5,6},{2,1},{4,3},{6,5},{9,10},{11,12},{13,14},{10,9},... | collective-permute-start | bytes 196616 | tf_op jit(solution)/shard_map/ppermute | solution.py:656
  8.5 3.2 %before.1 = (f32[10,416,128]{2,1,0:T(8,128)S(1)}, f32[10,416,128]{2,1,0:T(8,128)S(1)}, f32[10,416,128]{2,1,0:T(8,128)S(1)}, f32[10,416,128]{2,1,0:T(8,128)S(1)},...) custom-call(s32[1]{0:T(128)} %bitcast.refs_1_.refs_0_, ...), custom_call_target="tpu_custom_call", output_to_operand_aliasing={{0}: (7, {}), {1}: (8, {}), {2}: (9, {}), {3}: (10, {}), {1... | custom-call | flops 20000000 | bytes 6000000 | tf_op jit(solution)/shard_map/before/pallas_call | solution.py:690
  11.7 0.0 collective-permute-done.refs_2_.refs_1_
  11.7 0.0 collective-permute-done.1.refs_3_.refs_2_
  11.8 0.7 turn.1
  12.5 0.7 collective-permute-start.3
  13.2 3.7 %collective-permute-start.2 = (f32[784,128]{1,0:T(8,128)S(1)}, f32[784,128]{1,0:T(8,128)S(1)}, u32[]{:S(2)}, u32[]{:S(2)}) collective-permute-start(f32[784,128]{1,0:T(8,128)S(1)} %get-tuple-element.101.refs_3_), channel_id=1, source_target_pairs={{0,8},{16,24},{32,40},{48,56},{64,72},{80,88},{96,104},{112,120},{... | collective-permute-start | bytes 1204232 | tf_op jit(solution)/shard_map/ppermute | solution.py:656
  16.9 7.8 %inner.1 = (f32[10,416,128]{2,1,0:T(8,128)S(1)}, f32[10,416,128]{2,1,0:T(8,128)S(1)}, f32[10,416,128]{2,1,0:T(8,128)S(1)}, f32[10,416,128]{2,1,0:T(8,128)S(1)}, ...) custom-call(s32[1]{0:T(128)} %bitcast.1.refs_0_, ...), custom_call_target="tpu_custom_call", output_to_operand_aliasing={{0}: (4, {}), {1}: (5, {}), {2}: (6, {}), {3}: (7, {}), {4}... | custom-call | flops 100000000 | bytes 6000000 | tf_op jit(solution)/shard_map/inner/pallas_call | solution.py:706
  24.7 0.0 collective-permute-done.3.refs_28_
  24.7 0.0 collective-permute-done.2.refs_27_
  24.7 3.9 %first.1 = (f32[10,416,128]{2,1,0:T(8,128)S(1)}, f32[10,416,128]{2,1,0:T(8,128)S(1)}, f32[10,416,128]{2,1,0:T(8,128)S(1)}, f32[10,416,128]{2,1,0:T(8,128)S(1)}, ...) custom-call(s32[1]{0:T(128)} %bitcast.refs_1_.refs_0_, ...), custom_call_target="tpu_custom_call", output_to_operand_aliasing={{0}: (1, {}), {1}: (2, {}), {2}: (3, {}), {3}: (4, {}), {4}... | custom-call | tf_op jit(solution)/shard_map/first/pallas_call | solution.py:713
  28.6 22.2 %all_to_all.22 = f32[128,1,128]{2,1,0:T(1,128)S(1)} all-to-all(f32[128,1,128]{2,1,0:T(1,128)S(1)} %bitcast.12), channel_id=1, replica_groups=mesh['gx_0'=4,'gx_1'=4,'gy_0'=4,'gy_1'=2] {'gx_0','gx_1','gy_0','gy_1'}, dimensions={0} | all-to-all | bytes 131072 | tf_op jit(solution)/shard_map/all_to_all | solution.py:719
  50.8 9.3 %next.1 = (f32[10,416,128]{2,1,0:T(8,128)S(1)}, f32[10,416,128]{2,1,0:T(8,128)S(1)}, f32[10,416,128]{2,1,0:T(8,128)S(1)}, f32[10,416,128]{2,1,0:T(8,128)S(1)}, f...) custom-call(f32[10,416,128]{2,1,0:T(8,128)S(1)} %get-tuple-element.1, ...), custom_call_target="tpu_custom_call", output_to_operand_aliasing={{0}: (6, {}), {1}: (7, {}), {2}: (8, {}), {3}: (9, {}), {4}... | custom-call | tf_op jit(solution)/shard_map/next/pallas_call | solution.py:722
  60.1 13.8 %all_to_all.23 = f32[128,1,128]{2,1,0:T(1,128)S(1)} all-to-all(f32[128,1,128]{2,1,0:T(1,128)S(1)} %bitcast.13), channel_id=1, replica_groups=mesh['gx_0'=4,'gx_1'=4,'gy_0'=4,'gy_1'=2] {'gx_0','gx_1','gy_0','gy_1'}, dimensions={0} | all-to-all | bytes 131072 | tf_op jit(solution)/shard_map/all_to_all | solution.py:730
  73.9 1.8 %last.1 = (f32[10,64,512]{2,1,0:T(8,128)}, f32[10,64,512]{2,1,0:T(8,128)}) custom-call(f32[10,416,128]{2,1,0:T(8,128)S(1)} %get-tuple-element.175.refs_0_, f32[10,416,128]{2,1,0:T(8,128)S(1)} %get-tuple-element.176.refs_1_, f32[10,416,128]{2,1,0:T(8,128)S(1)} %get-tuple-element.177.refs_2_, f32[10,256,128]{2,1,0:T(8,128)S(1)} %get-tuple-element.178.refs_3_, ...), custom_call_target="tpu_custom_call" | custom-call | tf_op jit(solution)/shard_map/last/pallas_call | solution.py:733
Async XLA Ops:
  3.9 7.9 %collective-permute-start = (f32[2,64,128]{2,1,0:T(8,128)S(1)}, f32[2,64,128]{2,1,0:T(8,128)S(1)}, u32[]{:S(2)}, u32[]{:S(2)}) collective-permute-start(f32[2,64,128]{2,1,0:T(8,128)S(1)} %get-tuple-element.91), channel_id=1, source_target_pairs={{0,1},{2,3},{4,5},{6,7},{1,0},{3,2},{5,4},{7,6},{8,9},{10,11},{12,... | collective-permute-start | bytes 196616 | tf_op jit(solution)/shard_map/ppermute | solution.py:656
  5.3 6.4 %collective-permute-start.1 = (f32[2,64,128]{2,1,0:T(8,128)S(1)}, f32[2,64,128]{2,1,0:T(8,128)S(1)}, u32[]{:S(2)}, u32[]{:S(2)}) collective-permute-start(f32[2,64,128]{2,1,0:T(8,128)S(1)} %get-tuple-element.92), channel_id=1, source_target_pairs={{1,2},{3,4},{5,6},{2,1},{4,3},{6,5},{9,10},{11,12},{13,14},{10,9},... | collective-permute-start | bytes 196616 | tf_op jit(solution)/shard_map/ppermute | solution.py:656
  12.5 12.2 %collective-permute-start.3 = (f32[784,128]{1,0:T(8,128)S(1)}, f32[784,128]{1,0:T(8,128)S(1)}, u32[]{:S(2)}, u32[]{:S(2)}) collective-permute-start(f32[784,128]{1,0:T(8,128)S(1)} %get-tuple-element.153), channel_id=1, source_target_pairs={{8,16},{24,32},{40,48},{56,64},{72,80},{88,96},{104,112},{16,8},{3... | collective-permute-start | bytes 1204232 | tf_op jit(solution)/shard_map/ppermute | solution.py:656
  13.2 11.5 %collective-permute-start.2 = (f32[784,128]{1,0:T(8,128)S(1)}, f32[784,128]{1,0:T(8,128)S(1)}, u32[]{:S(2)}, u32[]{:S(2)}) collective-permute-start(f32[784,128]{1,0:T(8,128)S(1)} %get-tuple-element.101.refs_3_), channel_id=1, source_target_pairs={{0,8},{16,24},{32,40},{48,56},{64,72},{80,88},{96,104},{112,120},{... | collective-permute-start | bytes 1204232 | tf_op jit(solution)/shard_map/ppermute | solution.py:656
